TPU v7x, 512 devices: a whole 4x8x8 slice. The times are simulated.
512 devices in a mesh: list: 32 (over y_hi, x, core), shard: 16 (over z, y_lo).
Axes of the slice: x: 4, y: 8 (y_hi: 4, y_lo: 2; y = y_hi * 2 + y_lo), z: 8, core: 2. Of those that a mesh axis runs over, the one named last changes fastest.
Arguments:
- features: bfloat16 [4096, 4096], P(('list', 'shard')), may hold values from -6 to 6
- norm_gain: float32 [4096], replicated, may hold values from 0.5 to 1.5
- gate_weight: bfloat16 [4096, 11008], P('shard', 'list'), may hold values from -0.09375 to 0.09375
- up_weight: bfloat16 [4096, 11008], P('shard', 'list'), may hold values from -0.09375 to 0.09375
- down_weight: bfloat16 [11008, 4096], P('list', 'shard'), may hold values from -0.0546875 to 0.0546875
- centroids: float32 [64, 4096], P('list'), may hold values from -6 to 6
- list_ids: int32 [4096], P(('list', 'shard')), may hold values from 0 to 63
- live: int32 [4096], P(('list', 'shard')), may hold values 0 or 1
Outputs:
- residuals: bfloat16 [4096, 4096], P(('list', 'shard'))
- refreshed: float32 [64, 4096], P('list')
All inputs are finite; a program needn't handle non-finite values. No bound on the sum of `live` on one device may be relied on, other than what follows from the above.
Results may differ from a plain program's by a relative error of at most 0.015.
Values may be sent and summed in bfloat16 or wider, within the bound.
No kernel may reach another device: no remote copies, remote signals or barrier semaphores. Data moves between devices by JAX's collectives and lax.ppermute only.
A program may use at most 64 MiB of HBM per device.

v0:
```python
import jax
import jax.numpy as jnp
from jax import lax
from jax.experimental import pallas as pl
from jax.experimental.pallas import tpu as pltpu
from jax.sharding import Mesh, PartitionSpec as P

F32 = jnp.float32
BF16 = jnp.bfloat16
SWAP = [(0, 1), (1, 0)]
ROWS = ("x", "yh")
LIST = ("yh", "x", "c")
SHARD = ("z", "yl")


def swapped(value, axis):
    return lax.ppermute(value, axis, SWAP)


def to_everyone(value, axis):
    copies = jnp.broadcast_to(value, (lax.axis_size(axis), *value.shape))
    return lax.all_to_all(copies, axis, split_axis=0, concat_axis=0, tiled=True)


def by_class(value, mine):
    blocks = value.reshape(*value.shape[:-1], 8, 2, 256)
    even = blocks[..., 0, :].reshape(*value.shape[:-1], 2048)
    odd = blocks[..., 1, :].reshape(*value.shape[:-1], 2048)
    return jnp.where(mine == 0, even, odd), jnp.where(mine == 0, odd, even)


def interleaved(own, other, mine):
    even, odd = jnp.where(mine == 0, own, other), jnp.where(mine == 0, other, own)
    shape = own.shape[:-1]
    both = jnp.stack([even.reshape(*shape, 8, 256), odd.reshape(*shape, 8, 256)], axis=-2)
    return both.reshape(*shape, 4096)


def around(value, axis, index):
    turned = jnp.flip(value, axis)
    return lax.dynamic_slice_in_dim(jnp.concatenate([turned, turned], axis), 7 - index, 8, axis)


def ring(block):
    ahead = [(i, (i + 1) % 8) for i in range(8)]
    back = [(i, (i + 7) % 8) for i in range(8)]
    blocks = [block] + [None] * 7
    up = low = block
    for step in range(1, 4):
        up = lax.ppermute(up, "z", ahead)
        low = lax.ppermute(low, "z", back)
        blocks[step], blocks[8 - step] = up, low
    upper = lax.ppermute(up[:512], "z", ahead)
    lower = lax.ppermute(low[512:], "z", back)
    return [*blocks[:4], upper, lower, *blocks[5:]]


def gate_up_kernel(rows, *refs):
    *blocks, upper, lower, out = refs
    for start in range(0, 256, 128):
        total, left, right = 0.0, None, None
        for j in range(8):
            x = rows[start : start + 128, 256 * j : 256 * j + 256]
            if j == 4:
                left, right = times(x, upper[...]), times(x, lower[:176])
            else:
                total += times(x, blocks[j - (j > 4)][:688])
        out[start : start + 128, :512] = (total[:, :512] + left).astype(out.dtype)
        out[start : start + 128, 512:] = (total[:, 512:] + right).astype(out.dtype)


def times(a, b):
    return lax.dot_general(a, b, (((1,), (1,)), ((), ())), preferred_element_type=F32)


VMEM = pl.BlockSpec(memory_space=pltpu.VMEM)


def gate_up(rows, ring_blocks, dtype):
    upper, lower = ring_blocks[4:6]
    blocks = [*ring_blocks[:4], *ring_blocks[6:]]
    return pl.pallas_call(
        gate_up_kernel,
        out_shape=jax.ShapeDtypeStruct((256, 688), dtype),
        in_specs=[VMEM] * 10,
        out_specs=VMEM,
        cost_estimate=pl.CostEstimate(flops=2 * 256 * 2048 * 688, bytes_accessed=4 << 20, transcendentals=0),
        compiler_params=pltpu.CompilerParams(vmem_limit_bytes=16 << 20),
        name="gate_up",
    )(rows, *blocks, upper, lower)


def down_kernel(hidden, *refs):
    *blocks, lower, out = refs
    for j in range(8):
        weights = lower[176:] if j == 4 else blocks[j - (j > 4)][688:]
        out[j] = jnp.dot(hidden[...], weights, preferred_element_type=F32).astype(BF16)


def down_added_kernel(hidden, added, *refs):
    *blocks, lower, out = refs
    for j in range(8):
        weights = lower[176:] if j == 4 else blocks[j - (j > 4)][688:]
        terms = jnp.dot(hidden[...], weights, preferred_element_type=F32)
        terms = (terms + added[j].astype(F32)).astype(BF16)
        for x in range(4):
            out[x, j] = terms[64 * x : 64 * x + 64]


def down(hidden, ring_blocks, added=None):
    blocks = [*ring_blocks[:4], *ring_blocks[6:]]
    shape = (8, 256, 256) if added is None else (4, 8, 64, 256)
    extra = () if added is None else (added,)
    return pl.pallas_call(
        down_kernel if added is None else down_added_kernel,
        out_shape=jax.ShapeDtypeStruct(shape, BF16),
        in_specs=[VMEM] * (9 + len(extra)),
        out_specs=VMEM,
        cost_estimate=pl.CostEstimate(flops=2 * 256 * 2048 * 344, bytes_accessed=3 << 20, transcendentals=0),
        compiler_params=pltpu.CompilerParams(vmem_limit_bytes=16 << 20),
        name="down" if added is None else "down_added",
    )(hidden, *extra, *blocks, ring_blocks[5])


def one_hot(codes):
    return (codes[:, None] == jnp.arange(64, dtype=F32)[None, :].astype(BF16)).astype(BF16)


def program(features, norm_gain, gate_weight, up_weight, down_weight, centroids, list_ids, live):
    yl = lax.axis_index("yl")
    weights = jnp.concatenate([gate_weight.T, up_weight.T, down_weight], axis=0)
    z = lax.axis_index("z")
    weights = ring(weights)

    code = jnp.where(live > 0, list_ids, -1).astype(BF16)
    code_block = jnp.broadcast_to(code[:, None], (8, 128))
    own_x, away_x = (around(v.reshape(8, 8, 256), 1, z).reshape(8, 2048) for v in by_class(features, yl))
    received = swapped(jnp.concatenate([away_x, code_block], axis=1), "yl")
    x = jnp.concatenate([own_x, received[:, :2048]], axis=0)
    other_code = received[:, 2048]
    table, _ = by_class(centroids.astype(BF16), yl)
    sent = jnp.concatenate([x, table.reshape(16, 256)], axis=1)
    mine = to_everyone(sent, ROWS)
    theirs = swapped(mine, "c")
    both = jnp.stack([mine, theirs])
    rows = both[..., :2048].reshape(2, 16, 2, 8, 2048)
    kept = rows[:, :, 0].reshape(256, 2048)
    away = rows[:, :, 1].reshape(256, 2048)
    core = lax.axis_index("c")
    lists = both[..., 2048:].reshape(2, 4, 4, 2, 2048)
    lists = jnp.where(core == 0, lists, lists[::-1])
    lists = lists.transpose(2, 1, 0, 3, 4).reshape(64, 2048)
    picked = jnp.dot(one_hot(code), lists, preferred_element_type=F32).astype(BF16)
    other_picked = jnp.dot(one_hot(other_code), lists, preferred_element_type=F32).astype(BF16)
    coarse = interleaved(picked, swapped(other_picked, "yl"), yl)

    away_part = swapped(gate_up(away, weights, BF16), "yl")
    both = gate_up(kept, weights, F32) + away_part.astype(F32)
    hidden = (jax.nn.silu(both[:, :344]) * both[:, 344:]).astype(BF16)
    other_hidden = swapped(hidden, "yl")
    hidden = jnp.stack([hidden.reshape(2, 4, 32, 344), other_hidden.reshape(2, 4, 32, 344)], axis=2)
    hidden = hidden.reshape(2, 256, 344)
    from_core = swapped(down(hidden[1], weights), "c")
    terms = down(hidden[0], weights, from_core)
    terms = lax.all_to_all(terms, "x", 0, 0, tiled=True)
    terms = jnp.sum(terms.astype(F32), axis=0).astype(BF16)
    terms = terms.reshape(8, 2, 4, 8, 256).transpose(2, 1, 0, 3, 4)
    terms = jnp.where(yl == 0, terms, terms[:, ::-1]).reshape(8, 8, 8, 256)
    terms = lax.all_to_all(terms, ("yh", "yl"), 0, 0, tiled=True)
    terms = jnp.sum(terms.reshape(4, 2, 8, 8, 256).astype(F32), axis=0)
    mixed = around(terms, 1, z).transpose(2, 1, 0, 3).reshape(8, 4096)

    stream = features.astype(F32) + mixed
    scale = lax.rsqrt(jnp.mean(stream * stream, axis=1, keepdims=True) + 1e-05)
    embedding = (stream * scale * norm_gain).astype(BF16)
    alive = (live > 0).astype(F32)[:, None]
    residuals = (alive * (embedding.astype(F32) - coarse.astype(F32))).astype(BF16)

    blocks = embedding.reshape(8, 16, 256).transpose(1, 0, 2)
    blocks = jnp.concatenate([blocks, jnp.broadcast_to(code_block, (16, 8, 128))], axis=2)
    blocks = lax.all_to_all(blocks, SHARD, 0, 0, tiled=True).reshape(128, 384)
    member = one_hot(blocks[:, 256])
    sums = jnp.dot(member.T, blocks[:, :256], preferred_element_type=F32).astype(BF16)
    counts = jnp.sum(member.astype(F32), axis=0).astype(BF16)
    sums = jnp.concatenate([sums, jnp.broadcast_to(counts[:, None], (64, 128))], axis=1)
    sums = lax.all_to_all(sums.reshape(32, 2, 384), LIST, 0, 0, tiled=True)
    sums = jnp.sum(sums.astype(F32), axis=0)
    total = to_everyone(sums[:, :256], SHARD).transpose(1, 0, 2).reshape(2, 4096)
    refreshed = (centroids + total) / (1.0 + sums[:, 256:257])
    return residuals, refreshed


def solution(mesh):
    fine = Mesh(mesh.devices.reshape(4, 4, 2, 8, 2), ("yh", "x", "c", "z", "yl"))
    in_specs = (
        P((*LIST, *SHARD), None),
        P(),
        P(SHARD, LIST),
        P(SHARD, LIST),
        P(LIST, SHARD),
        P(LIST, None),
        P((*LIST, *SHARD)),
        P((*LIST, *SHARD)),
    )
    out_specs = (P((*LIST, *SHARD), None), P(LIST, None))
    return jax.shard_map(program, mesh=fine, in_specs=in_specs, out_specs=out_specs, check_vma=False)
```

profile of v0, /device:TPU:1, one launch (start us, length us, event | category | flops | bytes accessed | tf_op | source)
XLA Modules:
  0.0 218.6 jit_solution(2329925445642038716)
XLA Ops:
  2.3 4.0 %collective-permute-start = (bf16[8,2176]{1,0:T(8,128)(2,1)S(1)}, bf16[8,2176]{1,0:T(8,128)(2,1)S(1)}, u32[]{:S(2)}, u32[]{:S(2)}) collective-permute-start(bf16[8,2176]{1,0:T(8,128)(2,1)S(1)} %pad_maximum_fusion.6), channel_id=1, source_target_pairs={{0,1},{1,0},{2,3},{3,2},{4,5},{5,4},{6,7},{7,6},{8,9},{9,8},{10,11... | collective-permute-start | bytes 104456 | tf_op jit(solution)/shard_map/ppermute | solution.py:17
  8.7 9.7 %all-to-all-start = ((bf16[16,16,2304]{2,1,0:T(8,128)(2,1)}), bf16[16,16,2304]{2,1,0:T(8,128)(2,1)}, u32[]{:S(2)}, u32[]{:S(2)}) async-start(bf16[16,16,2304]{2,1,0:T(8,128)(2,1)} %broadcast_in_dim.14), calls=%async_computation | async-start | bytes 2359296 | tf_op jit(solution)/shard_map/all_to_all | solution.py:22
  18.5 4.0 %collective-permute-start.2 = (bf16[1032,256]{1,0:T(8,128)(2,1)S(1)}, bf16[1032,256]{1,0:T(8,128)(2,1)S(1)}, u32[]{:S(2)}, u32[]{:S(2)}) collective-permute-start(bf16[1032,256]{1,0:T(8,128)(2,1)S(1)} %pad_maximum_fusion.refs_0_), channel_id=1, source_target_pairs={{0,2},{2,4},{4,6},{6,8},{8,10},{10,12},{12,14},{14,0},{1,3},{3,5},... | collective-permute-start | bytes 1585160 | tf_op jit(solution)/shard_map/ppermute | solution.py:50
  22.5 8.6 %collective-permute-start.5 = (bf16[1032,256]{1,0:T(8,128)(2,1)S(1)}, bf16[1032,256]{1,0:T(8,128)(2,1)S(1)}, u32[]{:S(2)}, u32[]{:S(2)}) collective-permute-start(bf16[1032,256]{1,0:T(8,128)(2,1)S(1)} %pad_maximum_fusion.refs_0_), channel_id=1, source_target_pairs={{0,14},{2,0},{4,2},{6,4},{8,6},{10,8},{12,10},{14,12},{1,15},{3,1}... | collective-permute-start | bytes 1585160 | tf_op jit(solution)/shard_map/ppermute | solution.py:51
  31.1 16.5 %all-to-all-done = bf16[16,16,2304]{2,1,0:T(8,128)(2,1)} async-done(((bf16[16,16,2304]{2,1,0:T(8,128)(2,1)}), bf16[16,16,2304]{2,1,0:T(8,128)(2,1)}, u32[]{:S(2)}, u32[]{:S(2)}) %all-to-all-start) | async-done | bytes 1179680 | tf_op jit(solution)/shard_map/all_to_all | solution.py:22
  47.6 6.2 %collective-permute-start.1 = (bf16[16,16,2304]{2,1,0:T(8,128)(2,1)}, bf16[16,16,2304]{2,1,0:T(8,128)(2,1)S(1)}, u32[]{:S(2)}, u32[]{:S(2)}) collective-permute-start(bf16[16,16,2304]{2,1,0:T(8,128)(2,1)} %all-to-all-done), channel_id=1, source_target_pairs={{0,16},{16,0},{1,17},{17,1},{2,18},{18,2},{3,19},{19,3},{4,20},{20... | collective-permute-start | bytes 3538952 | tf_op jit(solution)/shard_map/ppermute | solution.py:17
  53.8 4.0 %collective-permute-start.3 = (bf16[1032,256]{1,0:T(8,128)(2,1)S(1)}, bf16[1032,256]{1,0:T(8,128)(2,1)S(1)}, u32[]{:S(2)}, u32[]{:S(2)}) collective-permute-start(bf16[1032,256]{1,0:T(8,128)(2,1)S(1)} %collective-permute-done.2.refs_1_), channel_id=1, source_target_pairs={{0,2},{2,4},{4,6},{6,8},{8,10},{10,12},{12,14},{14,0},{1,3},{3,5},... | collective-permute-start | bytes 1585160 | tf_op jit(solution)/shard_map/ppermute | solution.py:50
  57.8 8.6 %collective-permute-start.6 = (bf16[1032,256]{1,0:T(8,128)(2,1)S(1)}, bf16[1032,256]{1,0:T(8,128)(2,1)S(1)}, u32[]{:S(2)}, u32[]{:S(2)}) collective-permute-start(bf16[1032,256]{1,0:T(8,128)(2,1)S(1)} %collective-permute-done.5.refs_6_), channel_id=1, source_target_pairs={{0,14},{2,0},{4,2},{6,4},{8,6},{10,8},{12,10},{14,12},{1,15},{3,1}... | collective-permute-start | bytes 1585160 | tf_op jit(solution)/shard_map/ppermute | solution.py:51
  66.4 10.4 %collective-permute-done.3.refs_2_ = bf16[1032,256]{1,0:T(8,128)(2,1)S(1)} collective-permute-done((bf16[1032,256]{1,0:T(8,128)(2,1)S(1)}, bf16[1032,256]{1,0:T(8,128)(2,1)S(1)}, u32[]{:S(2)}, u32[]{:S(2)}) %collective-permute-start.3) | collective-permute-done | bytes 528416 | tf_op jit(solution)/shard_map/ppermute | solution.py:50
  76.9 1.9 collective-permute-start.4
  78.8 4.6 %collective-permute-start.7 = (bf16[1032,256]{1,0:T(8,128)(2,1)S(1)}, bf16[1032,256]{1,0:T(8,128)(2,1)S(1)}, u32[]{:S(2)}, u32[]{:S(2)}) collective-permute-start(bf16[1032,256]{1,0:T(8,128)(2,1)S(1)} %collective-permute-done.6.refs_5_), channel_id=1, source_target_pairs={{0,14},{2,0},{4,2},{6,4},{8,6},{10,8},{12,10},{14,12},{1,15},{3,1}... | collective-permute-start | bytes 1585160 | tf_op jit(solution)/shard_map/ppermute | solution.py:51
  83.4 9.6 %collective-permute-done.4.refs_3_ = bf16[1032,256]{1,0:T(8,128)(2,1)S(1)} collective-permute-done((bf16[1032,256]{1,0:T(8,128)(2,1)S(1)}, bf16[1032,256]{1,0:T(8,128)(2,1)S(1)}, u32[]{:S(2)}, u32[]{:S(2)}) %collective-permute-start.4) | collective-permute-done | bytes 528416 | tf_op jit(solution)/shard_map/ppermute | solution.py:50
  92.9 1.9 collective-permute-start.8
  94.9 4.6 %collective-permute-start.9 = (bf16[520,256]{1,0:T(8,128)(2,1)S(1)}, bf16[520,256]{1,0:T(8,128)(2,1)S(1)}, u32[]{:S(2)}, u32[]{:S(2)}) collective-permute-start(bf16[520,256]{1,0:T(8,128)(2,1)S(1)} %slice.91), channel_id=1, source_target_pairs={{0,14},{2,0},{4,2},{6,4},{8,6},{10,8},{12,10},{14,12},{1,15},{3,1}... | collective-permute-start | bytes 798728 | tf_op jit(solution)/shard_map/ppermute | solution.py:54
  103.5 1.9 gate_up.3
  105.4 1.9 collective-permute-start.10
  107.3 1.9 gate_up.2
  109.2 6.2 %collective-permute-done.10 = bf16[256,688]{1,0:T(8,128)(2,1)S(1)} collective-permute-done((bf16[256,688]{1,0:T(8,128)(2,1)S(1)}, bf16[256,688]{1,0:T(8,128)(2,1)S(1)}, u32[]{:S(2)}, u32[]{:S(2)}) %collective-permute-start.10) | collective-permute-done | bytes 352288 | tf_op jit(solution)/shard_map/ppermute | solution.py:17
  115.6 2.2 %collective-permute-start.11 = (bf16[256,344]{1,0:T(8,128)(2,1)S(1)}, bf16[256,344]{1,0:T(8,128)(2,1)S(1)}, u32[]{:S(2)}, u32[]{:S(2)}) collective-permute-start(bf16[256,344]{1,0:T(8,128)(2,1)S(1)} %fusion.2), channel_id=1, source_target_pairs={{0,1},{1,0},{2,3},{3,2},{4,5},{5,4},{6,7},{7,6},{8,9},{9,8},{10,11... | collective-permute-start | bytes 528392 | tf_op jit(solution)/shard_map/ppermute | solution.py:17
  117.8 4.2 %collective-permute-done.11 = bf16[256,344]{1,0:T(8,128)(2,1)S(1)} collective-permute-done((bf16[256,344]{1,0:T(8,128)(2,1)S(1)}, bf16[256,344]{1,0:T(8,128)(2,1)S(1)}, u32[]{:S(2)}, u32[]{:S(2)}) %collective-permute-start.11) | collective-permute-done | bytes 176160 | tf_op jit(solution)/shard_map/ppermute | solution.py:17
  124.5 6.5 %collective-permute-start.12 = (bf16[8,256,256]{2,1,0:T(8,128)(2,1)}, bf16[8,256,256]{2,1,0:T(8,128)(2,1)}, u32[]{:S(2)}, u32[]{:S(2)}) collective-permute-start(bf16[8,256,256]{2,1,0:T(8,128)(2,1)} %down.1), channel_id=1, source_target_pairs={{0,16},{16,0},{1,17},{17,1},{2,18},{18,2},{3,19},{19,3},{4,20},{20... | collective-permute-start | bytes 3145736 | tf_op jit(solution)/shard_map/ppermute | solution.py:17
  134.5 1.9 copy.64
  138.4 2.0 down_added.1
  141.4 3.6 %all-to-all-start.1 = ((bf16[4,8,64,256]{3,2,1,0:T(8,128)(2,1)}), bf16[4,8,64,256]{3,2,1,0:T(8,128)(2,1)S(1)}, u32[]{:S(2)}, u32[]{:S(2)}) async-start(bf16[4,8,64,256]{3,2,1,0:T(8,128)(2,1)} %copy-done.2), calls=%async_computation.1 | async-start | bytes 2097152 | tf_op jit(solution)/shard_map/all_to_all | solution.py:165
  145.6 1.9 collective-permute-start.13
  147.8 12.4 %all-to-all-done.1 = bf16[4,8,64,256]{3,2,1,0:T(8,128)(2,1)S(1)} async-done(((bf16[4,8,64,256]{3,2,1,0:T(8,128)(2,1)}), bf16[4,8,64,256]{3,2,1,0:T(8,128)(2,1)S(1)}, u32[]{:S(2)}, u32[]{:S(2)}) %all-to-all-start.1) | async-done | bytes 1048608 | tf_op jit(solution)/shard_map/all_to_all | solution.py:165
  161.2 3.5 %all-to-all-start.2 = ((bf16[8,8,8,256]{3,2,1,0:T(8,128)(2,1)}), bf16[8,8,8,256]{3,2,1,0:T(8,128)(2,1)S(1)}, u32[]{:S(2)}, u32[]{:S(2)}) async-start(bf16[8,8,8,256]{3,2,1,0:T(8,128)(2,1)} %bitcast.21), calls=%async_computation.2 | async-start | bytes 524288 | tf_op jit(solution)/shard_map/all_to_all | solution.py:169
  164.8 10.5 %all-to-all-done.2 = bf16[8,8,8,256]{3,2,1,0:T(8,128)(2,1)S(1)} async-done(((bf16[8,8,8,256]{3,2,1,0:T(8,128)(2,1)}), bf16[8,8,8,256]{3,2,1,0:T(8,128)(2,1)S(1)}, u32[]{:S(2)}, u32[]{:S(2)}) %all-to-all-start.2) | async-done | bytes 262176 | tf_op jit(solution)/shard_map/all_to_all | solution.py:169
  176.6 12.5 %all_to_all.30 = bf16[16,8,384]{2,1,0:T(8,128)(2,1)S(1)} all-to-all(bf16[16,8,384]{2,1,0:T(8,128)(2,1)S(1)} %pad_maximum_fusion.3), channel_id=1, replica_groups=mesh['yh'=4,'x'=4,'c'=2,'z'=8,'yl'=2] {'z','yl'}, dimensions={0} | all-to-all | bytes 196608 | tf_op jit(solution)/shard_map/all_to_all | solution.py:181
  189.8 16.5 %all_to_all.31 = bf16[32,2,384]{2,1,0:T(2,128)(2,1)S(1)} all-to-all(bf16[32,2,384]{2,1,0:T(2,128)(2,1)S(1)} %reshape.101), channel_id=1, replica_groups=mesh['yh'=4,'x'=4,'c'=2,'z'=8,'yl'=2] {'yh','x','c'}, dimensions={0} | all-to-all | bytes 98304 | tf_op jit(solution)/shard_map/all_to_all | solution.py:186
  206.9 3.5 %all-to-all-start.5 = ((f32[16,2,256]{2,1,0:T(2,128)}), f32[16,2,256]{2,1,0:T(2,128)S(1)}, u32[]{:S(2)}, u32[]{:S(2)}) async-start(f32[16,2,256]{2,1,0:T(2,128)} %broadcast_in_dim.16), calls=%async_computation.5 | async-start | bytes 65536 | tf_op jit(solution)/shard_map/all_to_all | solution.py:22
  210.6 7.4 %all-to-all-done.5 = f32[16,2,256]{2,1,0:T(2,128)S(1)} async-done(((f32[16,2,256]{2,1,0:T(2,128)}), f32[16,2,256]{2,1,0:T(2,128)S(1)}, u32[]{:S(2)}, u32[]{:S(2)}) %all-to-all-start.5) | async-done | bytes 32800 | tf_op jit(solution)/shard_map/all_to_all | solution.py:22
  (96 shorter events, 22.4 us)
Async XLA Ops:
  2.3 5.3 %collective-permute-start = (bf16[8,2176]{1,0:T(8,128)(2,1)S(1)}, bf16[8,2176]{1,0:T(8,128)(2,1)S(1)}, u32[]{:S(2)}, u32[]{:S(2)}) collective-permute-start(bf16[8,2176]{1,0:T(8,128)(2,1)S(1)} %pad_maximum_fusion.6), channel_id=1, source_target_pairs={{0,1},{1,0},{2,3},{3,2},{4,5},{5,4},{6,7},{7,6},{8,9},{9,8},{10,11... | collective-permute-start | bytes 104456 | tf_op jit(solution)/shard_map/ppermute | solution.py:17
  8.7 9.7 %copy-start.7 = (bf16[344,256]{1,0:T(8,128)(2,1)S(1)}, bf16[344,256]{1,0:T(8,128)(2,1)}, u32[]{:S(2)}) copy-start(bf16[344,256]{1,0:T(8,128)(2,1)} %param.12) | copy-start | bytes 528388
  8.7 9.7 %copy-start.8 = (bf16[256,344]{0,1:T(8,128)(2,1)S(1)}, bf16[256,344]{0,1:T(8,128)(2,1)}, u32[]{:S(2)}) copy-start(bf16[256,344]{0,1:T(8,128)(2,1)} %param.11) | copy-start | bytes 528388
  8.7 9.8 %copy-start.9 = (bf16[256,344]{0,1:T(8,128)(2,1)S(1)}, bf16[256,344]{0,1:T(8,128)(2,1)}, u32[]{:S(2)}) copy-start(bf16[256,344]{0,1:T(8,128)(2,1)} %param.10) | copy-start | bytes 528388
  8.7 38.9 %all-to-all-start = ((bf16[16,16,2304]{2,1,0:T(8,128)(2,1)}), bf16[16,16,2304]{2,1,0:T(8,128)(2,1)}, u32[]{:S(2)}, u32[]{:S(2)}) async-start(bf16[16,16,2304]{2,1,0:T(8,128)(2,1)} %broadcast_in_dim.14), calls=%async_computation | async-start | bytes 2359296 | tf_op jit(solution)/shard_map/all_to_all | solution.py:22
  18.5 35.3 %collective-permute-start.2 = (bf16[1032,256]{1,0:T(8,128)(2,1)S(1)}, bf16[1032,256]{1,0:T(8,128)(2,1)S(1)}, u32[]{:S(2)}, u32[]{:S(2)}) collective-permute-start(bf16[1032,256]{1,0:T(8,128)(2,1)S(1)} %pad_maximum_fusion.refs_0_), channel_id=1, source_target_pairs={{0,2},{2,4},{4,6},{6,8},{8,10},{10,12},{12,14},{14,0},{1,3},{3,5},... | collective-permute-start | bytes 1585160 | tf_op jit(solution)/shard_map/ppermute | solution.py:50
  22.5 35.3 %collective-permute-start.5 = (bf16[1032,256]{1,0:T(8,128)(2,1)S(1)}, bf16[1032,256]{1,0:T(8,128)(2,1)S(1)}, u32[]{:S(2)}, u32[]{:S(2)}) collective-permute-start(bf16[1032,256]{1,0:T(8,128)(2,1)S(1)} %pad_maximum_fusion.refs_0_), channel_id=1, source_target_pairs={{0,14},{2,0},{4,2},{6,4},{8,6},{10,8},{12,10},{14,12},{1,15},{3,1}... | collective-permute-start | bytes 1585160 | tf_op jit(solution)/shard_map/ppermute | solution.py:51
  47.6 51.9 %collective-permute-start.1 = (bf16[16,16,2304]{2,1,0:T(8,128)(2,1)}, bf16[16,16,2304]{2,1,0:T(8,128)(2,1)S(1)}, u32[]{:S(2)}, u32[]{:S(2)}) collective-permute-start(bf16[16,16,2304]{2,1,0:T(8,128)(2,1)} %all-to-all-done), channel_id=1, source_target_pairs={{0,16},{16,0},{1,17},{17,1},{2,18},{18,2},{3,19},{19,3},{4,20},{20... | collective-permute-start | bytes 3538952 | tf_op jit(solution)/shard_map/ppermute | solution.py:17
  53.8 23.0 %collective-permute-start.3 = (bf16[1032,256]{1,0:T(8,128)(2,1)S(1)}, bf16[1032,256]{1,0:T(8,128)(2,1)S(1)}, u32[]{:S(2)}, u32[]{:S(2)}) collective-permute-start(bf16[1032,256]{1,0:T(8,128)(2,1)S(1)} %collective-permute-done.2.refs_1_), channel_id=1, source_target_pairs={{0,2},{2,4},{4,6},{6,8},{8,10},{10,12},{12,14},{14,0},{1,3},{3,5},... | collective-permute-start | bytes 1585160 | tf_op jit(solution)/shard_map/ppermute | solution.py:50
  57.8 20.9 %collective-permute-start.6 = (bf16[1032,256]{1,0:T(8,128)(2,1)S(1)}, bf16[1032,256]{1,0:T(8,128)(2,1)S(1)}, u32[]{:S(2)}, u32[]{:S(2)}) collective-permute-start(bf16[1032,256]{1,0:T(8,128)(2,1)S(1)} %collective-permute-done.5.refs_6_), channel_id=1, source_target_pairs={{0,14},{2,0},{4,2},{6,4},{8,6},{10,8},{12,10},{14,12},{1,15},{3,1}... | collective-permute-start | bytes 1585160 | tf_op jit(solution)/shard_map/ppermute | solution.py:51
  76.9 16.1 %collective-permute-start.4 = (bf16[1032,256]{1,0:T(8,128)(2,1)S(1)}, bf16[1032,256]{1,0:T(8,128)(2,1)S(1)}, u32[]{:S(2)}, u32[]{:S(2)}) collective-permute-start(bf16[1032,256]{1,0:T(8,128)(2,1)S(1)} %collective-permute-done.3.refs_2_), channel_id=1, source_target_pairs={{0,2},{2,4},{4,6},{6,8},{8,10},{10,12},{12,14},{14,0},{1,3},{3,5},... | collective-permute-start | bytes 1585160 | tf_op jit(solution)/shard_map/ppermute | solution.py:50
  78.8 44.0 %copy-start = (bf16[1032,256]{1,0:T(8,128)(2,1)}, bf16[1032,256]{1,0:T(8,128)(2,1)S(1)}, u32[]{:S(2)}) copy-start(bf16[1032,256]{1,0:T(8,128)(2,1)S(1)} %collective-permute-done.6.refs_5_) | copy-start | bytes 1585156
  78.8 16.1 %collective-permute-start.7 = (bf16[1032,256]{1,0:T(8,128)(2,1)S(1)}, bf16[1032,256]{1,0:T(8,128)(2,1)S(1)}, u32[]{:S(2)}, u32[]{:S(2)}) collective-permute-start(bf16[1032,256]{1,0:T(8,128)(2,1)S(1)} %collective-permute-done.6.refs_5_), channel_id=1, source_target_pairs={{0,14},{2,0},{4,2},{6,4},{8,6},{10,8},{12,10},{14,12},{1,15},{3,1}... | collective-permute-start | bytes 1585160 | tf_op jit(solution)/shard_map/ppermute | solution.py:51
  92.9 9.5 %collective-permute-start.8 = (bf16[512,256]{1,0:T(8,128)(2,1)S(1)}, bf16[512,256]{1,0:T(8,128)(2,1)S(1)}, u32[]{:S(2)}, u32[]{:S(2)}) collective-permute-start(bf16[512,256]{1,0:T(8,128)(2,1)S(1)} %slice.90), channel_id=1, source_target_pairs={{0,2},{2,4},{4,6},{6,8},{8,10},{10,12},{12,14},{14,0},{1,3},{3,5},... | collective-permute-start | bytes 786440 | tf_op jit(solution)/shard_map/ppermute | solution.py:53
  94.9 8.6 %collective-permute-start.9 = (bf16[520,256]{1,0:T(8,128)(2,1)S(1)}, bf16[520,256]{1,0:T(8,128)(2,1)S(1)}, u32[]{:S(2)}, u32[]{:S(2)}) collective-permute-start(bf16[520,256]{1,0:T(8,128)(2,1)S(1)} %slice.91), channel_id=1, source_target_pairs={{0,14},{2,0},{4,2},{6,4},{8,6},{10,8},{12,10},{14,12},{1,15},{3,1}... | collective-permute-start | bytes 798728 | tf_op jit(solution)/shard_map/ppermute | solution.py:54
  99.5 1.9 copy-start.4
  105.4 10.0 %collective-permute-start.10 = (bf16[256,688]{1,0:T(8,128)(2,1)S(1)}, bf16[256,688]{1,0:T(8,128)(2,1)S(1)}, u32[]{:S(2)}, u32[]{:S(2)}) collective-permute-start(bf16[256,688]{1,0:T(8,128)(2,1)S(1)} %gate_up.3), channel_id=1, source_target_pairs={{0,1},{1,0},{2,3},{3,2},{4,5},{5,4},{6,7},{7,6},{8,9},{9,8},{10,11... | collective-permute-start | bytes 1056776 | tf_op jit(solution)/shard_map/ppermute | solution.py:17
  115.6 6.4 %collective-permute-start.11 = (bf16[256,344]{1,0:T(8,128)(2,1)S(1)}, bf16[256,344]{1,0:T(8,128)(2,1)S(1)}, u32[]{:S(2)}, u32[]{:S(2)}) collective-permute-start(bf16[256,344]{1,0:T(8,128)(2,1)S(1)} %fusion.2), channel_id=1, source_target_pairs={{0,1},{1,0},{2,3},{3,2},{4,5},{5,4},{6,7},{7,6},{8,9},{9,8},{10,11... | collective-permute-start | bytes 528392 | tf_op jit(solution)/shard_map/ppermute | solution.py:17
  122.8 8.2 %copy-start.12 = (s32[8]{0:T(128)S(1)}, s32[8]{0:T(128)}, u32[]{:S(2)}) copy-start(s32[8]{0:T(128)} %param.15) | copy-start | bytes 100
  124.5 12.0 %collective-permute-start.12 = (bf16[8,256,256]{2,1,0:T(8,128)(2,1)}, bf16[8,256,256]{2,1,0:T(8,128)(2,1)}, u32[]{:S(2)}, u32[]{:S(2)}) collective-permute-start(bf16[8,256,256]{2,1,0:T(8,128)(2,1)} %down.1), channel_id=1, source_target_pairs={{0,16},{16,0},{1,17},{17,1},{2,18},{18,2},{3,19},{19,3},{4,20},{20... | collective-permute-start | bytes 3145736 | tf_op jit(solution)/shard_map/ppermute | solution.py:17
  136.5 1.0 copy-start.1
  137.5 0.9 copy-start.3
  140.4 1.0 copy-start.2
  141.4 3.7 %copy-start.5 = (bf16[2,4,4,2,2048]{4,3,0,1,2:T(2,128)(2,1)S(1)}, bf16[2,4,4,2,2048]{4,3,0,1,2:T(2,128)(2,1)}, u32[]{:S(2)}) copy-start(bf16[2,4,4,2,2048]{4,3,0,1,2:T(2,128)(2,1)} %copy.64) | copy-start | bytes 786436
  141.4 18.8 %all-to-all-start.1 = ((bf16[4,8,64,256]{3,2,1,0:T(8,128)(2,1)}), bf16[4,8,64,256]{3,2,1,0:T(8,128)(2,1)S(1)}, u32[]{:S(2)}, u32[]{:S(2)}) async-start(bf16[4,8,64,256]{3,2,1,0:T(8,128)(2,1)} %copy-done.2), calls=%async_computation.1 | async-start | bytes 2097152 | tf_op jit(solution)/shard_map/all_to_all | solution.py:165
  145.6 19.1 %collective-permute-start.13 = (bf16[8,2048]{1,0:T(8,128)(2,1)S(1)}, bf16[8,2048]{1,0:T(8,128)(2,1)S(1)}, u32[]{:S(2)}, u32[]{:S(2)}) collective-permute-start(bf16[8,2048]{1,0:T(8,128)(2,1)S(1)} %convolution_convert_fusion), channel_id=1, source_target_pairs={{0,1},{1,0},{2,3},{3,2},{4,5},{5,4},{6,7},{7,6},{8,9},{9,8},{10,11... | collective-permute-start | bytes 98312 | tf_op jit(solution)/shard_map/ppermute | solution.py:17
  161.2 14.5 %copy-start.6 = (bf16[8,4096]{1,0:T(8,128)(2,1)S(1)}, bf16[8,4096]{1,0:T(8,128)(2,1)}, u32[]{:S(2)}) copy-start(bf16[8,4096]{1,0:T(8,128)(2,1)} %param.8) | copy-start | bytes 196612
  161.2 14.1 %all-to-all-start.2 = ((bf16[8,8,8,256]{3,2,1,0:T(8,128)(2,1)}), bf16[8,8,8,256]{3,2,1,0:T(8,128)(2,1)S(1)}, u32[]{:S(2)}, u32[]{:S(2)}) async-start(bf16[8,8,8,256]{3,2,1,0:T(8,128)(2,1)} %bitcast.21), calls=%async_computation.2 | async-start | bytes 524288 | tf_op jit(solution)/shard_map/all_to_all | solution.py:169
  164.7 11.1 %copy-start.11 = (f32[4096]{0:T(1024)S(1)}, f32[4096]{0:T(1024)}, u32[]{:S(2)}) copy-start(f32[4096]{0:T(1024)} %param.9) | copy-start | bytes 49156
  175.4 42.5 %copy-start.10 = (f32[2,4096]{1,0:T(2,128)S(1)}, f32[2,4096]{1,0:T(2,128)}, u32[]{:S(2)}) copy-start(f32[2,4096]{1,0:T(2,128)} %param.13) | copy-start | bytes 98308
  206.9 11.0 %all-to-all-start.5 = ((f32[16,2,256]{2,1,0:T(2,128)}), f32[16,2,256]{2,1,0:T(2,128)S(1)}, u32[]{:S(2)}, u32[]{:S(2)}) async-start(f32[16,2,256]{2,1,0:T(2,128)} %broadcast_in_dim.16), calls=%async_computation.5 | async-start | bytes 65536 | tf_op jit(solution)/shard_map/all_to_all | solution.py:22
where the time goes:
time: 220 us; the launch traced here: 219 us
  starting transfers between devices  81.3 us (37%)
  waiting for transfers between devices  79.4 us (36%)
  blocking collectives  29 us (13%)
  local copies, waits for them, and re-layouts  10.1 us (5%)
  other arithmetic  9.59 us (4%)
  Pallas kernels  7.42 us (3%)
    all_to_all x2, waiting for transfers between devices, to_everyone(): return lax.all_to_all(copies, axis, split_axis=0, concat_axis=0, tiled=True)  23.9 us
    ppermute x6, starting transfers between devices, swapped(): return lax.ppermute(value, axis, SWAP)  22.7 us
    ppermute x3, starting transfers between devices, ring(): low = lax.ppermute(low, 'z', back)  21.7 us
    ppermute x3, waiting for transfers between devices, ring(): up = lax.ppermute(up, 'z', ahead)  20 us
    all_to_all x1, blocking collectives, program(): sums = lax.all_to_all(sums.reshape(32, 2, 384), LIST, 0, 0, tiled=True)  16.5 us
    all_to_all x2, starting transfers between devices, to_everyone(): return lax.all_to_all(copies, axis, split_axis=0, concat_axis=0, tiled=True)  13.2 us
    all_to_all x1, blocking collectives, program(): blocks = lax.all_to_all(blocks, SHARD, 0, 0, tiled=True).reshape(128, 384)  12.5 us
    all_to_all x1, waiting for transfers between devices, program(): terms = lax.all_to_all(terms, 'x', 0, 0, tiled=True)  12.4 us
  transfers between devices with their start and end apart: 18, of which 11 were waited for; matrix products, arithmetic and copies ran while one was open for 5% of the time, Pallas kernels for 1%

commit v1 on v0

--- a/solution.py
+++ b/solution.py
@@ -41,32 +41,37 @@
     return lax.dynamic_slice_in_dim(jnp.concatenate([turned, turned], axis), 7 - index, 8, axis)
 
 
-def ring(block):
-    ahead = [(i, (i + 1) % 8) for i in range(8)]
-    back = [(i, (i + 7) % 8) for i in range(8)]
-    blocks = [block] + [None] * 7
-    up = low = block
+AHEAD = [(i, (i + 1) % 8) for i in range(8)]
+BACK = [(i, (i + 7) % 8) for i in range(8)]
+
+
+def hop(value, pairs):
+    return lax.ppermute(value, "z", pairs)
+
+
+def rings(first, second):
+    firsts, seconds = [first] + [None] * 7, [second] + [None] * 7
     for step in range(1, 4):
-        up = lax.ppermute(up, "z", ahead)
-        low = lax.ppermute(low, "z", back)
-        blocks[step], blocks[8 - step] = up, low
-    upper = lax.ppermute(up[:512], "z", ahead)
-    lower = lax.ppermute(low[512:], "z", back)
-    return [*blocks[:4], upper, lower, *blocks[5:]]
+        firsts[step] = hop(firsts[step - 1], AHEAD)
+        firsts[8 - step] = hop(firsts[(9 - step) % 8], BACK)
+        seconds[step] = hop(seconds[step - 1], AHEAD)
+        seconds[8 - step] = hop(seconds[(9 - step) % 8], BACK)
+    upper = hop(firsts[3][:384], AHEAD)
+    lower = hop(firsts[5][384:], BACK)
+    seconds[4] = hop(seconds[3], AHEAD)
+    return [*firsts[:4], *firsts[5:], upper, lower], seconds
 
 
 def gate_up_kernel(rows, *refs):
     *blocks, upper, lower, out = refs
     for start in range(0, 256, 128):
-        total, left, right = 0.0, None, None
-        for j in range(8):
+        total = 0.0
+        for j in (0, 1, 2, 3, 5, 6, 7):
             x = rows[start : start + 128, 256 * j : 256 * j + 256]
-            if j == 4:
-                left, right = times(x, upper[...]), times(x, lower[:176])
-            else:
-                total += times(x, blocks[j - (j > 4)][:688])
-        out[start : start + 128, :512] = (total[:, :512] + left).astype(out.dtype)
-        out[start : start + 128, 512:] = (total[:, 512:] + right).astype(out.dtype)
+            total += times(x, blocks[j - (j > 4)][...])
+        x = rows[start : start + 128, 1024:1280]
+        out[start : start + 128, :384] = (total[:, :384] + times(x, upper[...])).astype(out.dtype)
+        out[start : start + 128, 384:] = (total[:, 384:] + times(x, lower[...])).astype(out.dtype)
 
 
 def times(a, b):
@@ -76,9 +81,11 @@
 VMEM = pl.BlockSpec(memory_space=pltpu.VMEM)
 
 
-def gate_up(rows, ring_blocks, dtype):
-    upper, lower = ring_blocks[4:6]
-    blocks = [*ring_blocks[:4], *ring_blocks[6:]]
+def whole(shape):
+    return pl.BlockSpec(shape, lambda: (0,) * len(shape))
+
+
+def gate_up(rows, blocks, dtype):
     return pl.pallas_call(
         gate_up_kernel,
         out_shape=jax.ShapeDtypeStruct((256, 688), dtype),
@@ -87,39 +94,44 @@
         cost_estimate=pl.CostEstimate(flops=2 * 256 * 2048 * 688, bytes_accessed=4 << 20, transcendentals=0),
         compiler_params=pltpu.CompilerParams(vmem_limit_bytes=16 << 20),
         name="gate_up",
-    )(rows, *blocks, upper, lower)
-
-
-def down_kernel(hidden, *refs):
-    *blocks, lower, out = refs
+    )(rows, *blocks)
+
+
+def rows_of(core, own, other):
+    pieces = []
+    for at in range(128 * core, 128 * core + 128, 32):
+        pieces += [own[at : at + 32], other[at : at + 32]]
+    return jnp.concatenate(pieces, axis=0)
+
+
+def down_kernel(own, other, *refs):
+    *blocks, out = refs
+    hidden = rows_of(1, own, other)
     for j in range(8):
-        weights = lower[176:] if j == 4 else blocks[j - (j > 4)][688:]
-        out[j] = jnp.dot(hidden[...], weights, preferred_element_type=F32).astype(BF16)
-
-
-def down_added_kernel(hidden, added, *refs):
-    *blocks, lower, out = refs
+        out[j] = jnp.dot(hidden, blocks[j][...], preferred_element_type=F32).astype(BF16)
+
+
+def down_added_kernel(own, other, added, *refs):
+    *blocks, out = refs
+    hidden = rows_of(0, own, other)
     for j in range(8):
-        weights = lower[176:] if j == 4 else blocks[j - (j > 4)][688:]
-        terms = jnp.dot(hidden[...], weights, preferred_element_type=F32)
+        terms = jnp.dot(hidden, blocks[j][...], preferred_element_type=F32)
         terms = (terms + added[j].astype(F32)).astype(BF16)
         for x in range(4):
             out[x, j] = terms[64 * x : 64 * x + 64]
 
 
-def down(hidden, ring_blocks, added=None):
-    blocks = [*ring_blocks[:4], *ring_blocks[6:]]
-    shape = (8, 256, 256) if added is None else (4, 8, 64, 256)
-    extra = () if added is None else (added,)
+def down(own, other, blocks, *added):
+    shape = (4, 8, 64, 256) if added else (8, 256, 256)
     return pl.pallas_call(
-        down_kernel if added is None else down_added_kernel,
+        down_added_kernel if added else down_kernel,
         out_shape=jax.ShapeDtypeStruct(shape, BF16),
-        in_specs=[VMEM] * (9 + len(extra)),
-        out_specs=VMEM,
+        in_specs=[VMEM] * (10 + len(added)),
+        out_specs=whole(shape) if added else VMEM,
         cost_estimate=pl.CostEstimate(flops=2 * 256 * 2048 * 344, bytes_accessed=3 << 20, transcendentals=0),
         compiler_params=pltpu.CompilerParams(vmem_limit_bytes=16 << 20),
-        name="down" if added is None else "down_added",
-    )(hidden, *extra, *blocks, ring_blocks[5])
+        name="down_added" if added else "down",
+    )(own, other, *added, *blocks)
 
 
 def one_hot(codes):
@@ -128,9 +140,8 @@
 
 def program(features, norm_gain, gate_weight, up_weight, down_weight, centroids, list_ids, live):
     yl = lax.axis_index("yl")
-    weights = jnp.concatenate([gate_weight.T, up_weight.T, down_weight], axis=0)
     z = lax.axis_index("z")
-    weights = ring(weights)
+    first, second = rings(jnp.concatenate([gate_weight.T, up_weight.T], axis=0), down_weight)
 
     code = jnp.where(live > 0, list_ids, -1).astype(BF16)
     code_block = jnp.broadcast_to(code[:, None], (8, 128))
@@ -146,22 +157,22 @@
     rows = both[..., :2048].reshape(2, 16, 2, 8, 2048)
     kept = rows[:, :, 0].reshape(256, 2048)
     away = rows[:, :, 1].reshape(256, 2048)
+    away_part = swapped(gate_up(away, first, BF16), "yl")
+    both = gate_up(kept, first, F32) + away_part.astype(F32)
+    hidden = (jax.nn.silu(both[:, :344]) * both[:, 344:]).astype(BF16)
+    other_hidden = swapped(hidden, "yl")
+    from_core = swapped(down(hidden, other_hidden, second), "c")
+    terms = down(hidden, other_hidden, second, from_core)
+
+    mine, theirs, terms = lax.optimization_barrier((mine, theirs, terms))
     core = lax.axis_index("c")
-    lists = both[..., 2048:].reshape(2, 4, 4, 2, 2048)
+    lists = jnp.stack([mine[..., 2048:], theirs[..., 2048:]]).reshape(2, 4, 4, 2, 2048)
     lists = jnp.where(core == 0, lists, lists[::-1])
     lists = lists.transpose(2, 1, 0, 3, 4).reshape(64, 2048)
     picked = jnp.dot(one_hot(code), lists, preferred_element_type=F32).astype(BF16)
     other_picked = jnp.dot(one_hot(other_code), lists, preferred_element_type=F32).astype(BF16)
     coarse = interleaved(picked, swapped(other_picked, "yl"), yl)
 
-    away_part = swapped(gate_up(away, weights, BF16), "yl")
-    both = gate_up(kept, weights, F32) + away_part.astype(F32)
-    hidden = (jax.nn.silu(both[:, :344]) * both[:, 344:]).astype(BF16)
-    other_hidden = swapped(hidden, "yl")
-    hidden = jnp.stack([hidden.reshape(2, 4, 32, 344), other_hidden.reshape(2, 4, 32, 344)], axis=2)
-    hidden = hidden.reshape(2, 256, 344)
-    from_core = swapped(down(hidden[1], weights), "c")
-    terms = down(hidden[0], weights, from_core)
     terms = lax.all_to_all(terms, "x", 0, 0, tiled=True)
     terms = jnp.sum(terms.astype(F32), axis=0).astype(BF16)
     terms = terms.reshape(8, 2, 4, 8, 256).transpose(2, 1, 0, 3, 4)

time: 220 us -> 234 us (1.064)
  blocking collectives: 29 us -> 69.1 us
  waiting for transfers between devices: 79.4 us -> 49.1 us
  starting transfers between devices: 81.3 us -> 89.7 us
  other arithmetic: 9.59 us -> 7.1 us
    all_to_all x0 -> x1, blocking collectives: none -> 40.4 us  [to_everyone(): return lax.all_to_all(copies, axis, split_axis=0, concat_axis=0, tiled=True)]
    all_to_all x2 -> x1, waiting for transfers between devices: 23.9 us -> 7.36 us  [to_everyone(): return lax.all_to_all(copies, axis, split_axis=0, concat_axis=0, tiled=True)]
    ppermute x8 -> x15, starting transfers between devices: 38.2 us -> 53.3 us  [hop(): return lax.ppermute(value, 'z', pairs)]
    all_to_all x2 -> x1, starting transfers between devices: 13.2 us -> 3.5 us  [to_everyone(): return lax.all_to_all(copies, axis, split_axis=0, concat_axis=0, tiled=True)]
    ppermute x6, waiting for transfers between devices: 10.7 us -> 3.29 us  [swapped(): return lax.ppermute(value, axis, SWAP)]
    ppermute x8 -> x15, waiting for transfers between devices: 21.9 us -> 17.7 us  [hop(): return lax.ppermute(value, 'z', pairs)]
    reshape x2 -> x0, local copies, waits for them, and re-layouts: 3.63 us -> none  [program(): lists = both[..., 2048:].reshape(2, 4, 4, 2, 2048)]
    ppermute x6, starting transfers between devices: 22.7 us -> 25.3 us  [swapped(): return lax.ppermute(value, axis, SWAP)]
  transfers between devices with their start and end apart: 18 -> 24, of which waited for: 11 -> 12; matrix products, arithmetic and copies ran while one was open for 5% -> 3% of each run, Pallas kernels for 1% -> 1%
where the time goes in v1:
time: 234 us; the launch traced here: 232 us
  starting transfers between devices  89.7 us (38%)
  blocking collectives  69.1 us (30%)
  waiting for transfers between devices  49.1 us (21%)
  local copies, waits for them, and re-layouts  9.65 us (4%)
  other arithmetic  7.1 us (3%)
  Pallas kernels  5.86 us (3%)
    ppermute x15, starting transfers between devices, hop(): return lax.ppermute(value, 'z', pairs)  53.3 us
    all_to_all x1, blocking collectives, to_everyone(): return lax.all_to_all(copies, axis, split_axis=0, concat_axis=0, tiled=True)  40.4 us
    ppermute x6, starting transfers between devices, swapped(): return lax.ppermute(value, axis, SWAP)  25.3 us
    ppermute x15, waiting for transfers between devices, hop(): return lax.ppermute(value, 'z', pairs)  17.7 us
    all_to_all x1, blocking collectives, program(): sums = lax.all_to_all(sums.reshape(32, 2, 384), LIST, 0, 0, tiled=True)  16.8 us
    all_to_all x1, blocking collectives, program(): blocks = lax.all_to_all(blocks, SHARD, 0, 0, tiled=True).reshape(128, 384)  11.9 us
    all_to_all x1, waiting for transfers between devices, program(): terms = lax.all_to_all(terms, 'x', 0, 0, tiled=True)  10.6 us
    all_to_all x1, waiting for transfers between devices, program(): terms = lax.all_to_all(terms, ('yh', 'yl'), 0, 0, tiled=True)  10.2 us
  transfers between devices with their start and end apart: 24, of which 12 were waited for; matrix products, arithmetic and copies ran while one was open for 3% of the time, Pallas kernels for 1%

profile of v1, /device:TPU:1, one launch (start us, length us, event | category | flops | bytes accessed | tf_op | source)
XLA Modules:
  0.0 232.4 jit_solution(3833462617051796420)
XLA Ops:
  2.3 4.1 %collective-permute-start = (bf16[8,2176]{1,0:T(8,128)(2,1)S(1)}, bf16[8,2176]{1,0:T(8,128)(2,1)S(1)}, u32[]{:S(2)}, u32[]{:S(2)}) collective-permute-start(bf16[8,2176]{1,0:T(8,128)(2,1)S(1)} %pad_maximum_fusion.6), channel_id=1, source_target_pairs={{0,1},{1,0},{2,3},{3,2},{4,5},{5,4},{6,7},{7,6},{8,9},{9,8},{10,11... | collective-permute-start | bytes 104456 | tf_op jit(solution)/shard_map/ppermute | solution.py:17
  8.4 40.4 %all_to_all.30 = bf16[16,16,2304]{2,1,0:T(8,128)(2,1)S(1)} all-to-all(bf16[16,16,2304]{2,1,0:T(8,128)(2,1)S(1)} %broadcast_in_dim.14), channel_id=1, replica_groups=mesh['yh'=4,'x'=4,'c'=2,'z'=8,'yl'=2] {'x','yh'}, dimensions={0} | all-to-all | bytes 2359296 | tf_op jit(solution)/shard_map/all_to_all | solution.py:22
  48.9 4.5 %collective-permute-start.1 = (bf16[16,16,2304]{2,1,0:T(8,128)(2,1)S(1)}, bf16[16,16,2304]{2,1,0:T(8,128)(2,1)S(1)}, u32[]{:S(2)}, u32[]{:S(2)}) collective-permute-start(bf16[16,16,2304]{2,1,0:T(8,128)(2,1)S(1)} %all_to_all.30), channel_id=1, source_target_pairs={{0,16},{16,0},{1,17},{17,1},{2,18},{18,2},{3,19},{19,3},{4,20},{20... | collective-permute-start | bytes 3538952 | tf_op jit(solution)/shard_map/ppermute | solution.py:17
  53.4 4.0 %collective-permute-start.2 = (bf16[688,256]{1,0:T(8,128)(2,1)S(1)}, bf16[688,256]{1,0:T(8,128)(2,1)S(1)}, u32[]{:S(2)}, u32[]{:S(2)}) collective-permute-start(bf16[688,256]{1,0:T(8,128)(2,1)S(1)} %pad_maximum_fusion.1.refs_0_), channel_id=1, source_target_pairs={{0,2},{2,4},{4,6},{6,8},{8,10},{10,12},{12,14},{14,0},{1,3},{3,5},... | collective-permute-start | bytes 1056776 | tf_op jit(solution)/shard_map/ppermute | solution.py:49
  57.4 8.6 %collective-permute-start.5 = (bf16[688,256]{1,0:T(8,128)(2,1)S(1)}, bf16[688,256]{1,0:T(8,128)(2,1)S(1)}, u32[]{:S(2)}, u32[]{:S(2)}) collective-permute-start(bf16[688,256]{1,0:T(8,128)(2,1)S(1)} %pad_maximum_fusion.1.refs_0_), channel_id=1, source_target_pairs={{0,14},{2,0},{4,2},{6,4},{8,6},{10,8},{12,10},{14,12},{1,15},{3,1}... | collective-permute-start | bytes 1056776 | tf_op jit(solution)/shard_map/ppermute | solution.py:49
  66.0 6.7 %collective-permute-done.2.refs_1_ = bf16[688,256]{1,0:T(8,128)(2,1)S(1)} collective-permute-done((bf16[688,256]{1,0:T(8,128)(2,1)S(1)}, bf16[688,256]{1,0:T(8,128)(2,1)S(1)}, u32[]{:S(2)}, u32[]{:S(2)}) %collective-permute-start.2) | collective-permute-done | bytes 352288 | tf_op jit(solution)/shard_map/ppermute | solution.py:49
  72.7 1.9 collective-permute-start.3
  74.6 4.6 %collective-permute-start.6 = (bf16[688,256]{1,0:T(8,128)(2,1)S(1)}, bf16[688,256]{1,0:T(8,128)(2,1)S(1)}, u32[]{:S(2)}, u32[]{:S(2)}) collective-permute-start(bf16[688,256]{1,0:T(8,128)(2,1)S(1)} %collective-permute-done.5.refs_6_), channel_id=1, source_target_pairs={{0,14},{2,0},{4,2},{6,4},{8,6},{10,8},{12,10},{14,12},{1,15},{3,1}... | collective-permute-start | bytes 1056776 | tf_op jit(solution)/shard_map/ppermute | solution.py:49
  79.2 5.8 %collective-permute-done.3.refs_2_ = bf16[688,256]{1,0:T(8,128)(2,1)S(1)} collective-permute-done((bf16[688,256]{1,0:T(8,128)(2,1)S(1)}, bf16[688,256]{1,0:T(8,128)(2,1)S(1)}, u32[]{:S(2)}, u32[]{:S(2)}) %collective-permute-start.3) | collective-permute-done | bytes 352288 | tf_op jit(solution)/shard_map/ppermute | solution.py:49
  86.9 4.6 %collective-permute-start.7 = (bf16[688,256]{1,0:T(8,128)(2,1)S(1)}, bf16[688,256]{1,0:T(8,128)(2,1)S(1)}, u32[]{:S(2)}, u32[]{:S(2)}) collective-permute-start(bf16[688,256]{1,0:T(8,128)(2,1)S(1)} %collective-permute-done.6.refs_5_), channel_id=1, source_target_pairs={{0,14},{2,0},{4,2},{6,4},{8,6},{10,8},{12,10},{14,12},{1,15},{3,1}... | collective-permute-start | bytes 1056776 | tf_op jit(solution)/shard_map/ppermute | solution.py:49
  91.5 1.9 collective-permute-start.12
  93.4 4.6 %collective-permute-start.16 = (bf16[344,256]{1,0:T(8,128)(2,1)S(1)}, bf16[344,256]{1,0:T(8,128)(2,1)S(1)}, u32[]{:S(2)}, u32[]{:S(2)}) collective-permute-start(bf16[344,256]{1,0:T(8,128)(2,1)S(1)} %copy-done), channel_id=1, source_target_pairs={{0,14},{2,0},{4,2},{6,4},{8,6},{10,8},{12,10},{14,12},{1,15},{3,1}... | collective-permute-start | bytes 528392 | tf_op jit(solution)/shard_map/ppermute | solution.py:49
  98.0 2.6 %collective-permute-done.12.refs_1_ = bf16[344,256]{1,0:T(8,128)(2,1)S(1)} collective-permute-done((bf16[344,256]{1,0:T(8,128)(2,1)S(1)}, bf16[344,256]{1,0:T(8,128)(2,1)S(1)}, u32[]{:S(2)}, u32[]{:S(2)}) %collective-permute-start.12) | collective-permute-done | bytes 176160 | tf_op jit(solution)/shard_map/ppermute | solution.py:49
  102.6 1.9 collective-permute-start.8
  104.5 4.6 %collective-permute-start.9 = (bf16[304,256]{1,0:T(8,128)(2,1)S(1)}, bf16[304,256]{1,0:T(8,128)(2,1)S(1)}, u32[]{:S(2)}, u32[]{:S(2)}) collective-permute-start(bf16[304,256]{1,0:T(8,128)(2,1)S(1)} %slice.83), channel_id=1, source_target_pairs={{0,14},{2,0},{4,2},{6,4},{8,6},{10,8},{12,10},{14,12},{1,15},{3,1}... | collective-permute-start | bytes 466952 | tf_op jit(solution)/shard_map/ppermute | solution.py:49
  114.0 1.9 collective-permute-start.10
  115.9 4.0 %collective-permute-start.17 = (bf16[344,256]{1,0:T(8,128)(2,1)S(1)}, bf16[344,256]{1,0:T(8,128)(2,1)S(1)}, u32[]{:S(2)}, u32[]{:S(2)}) collective-permute-start(bf16[344,256]{1,0:T(8,128)(2,1)S(1)} %collective-permute-done.16.refs_7_), channel_id=1, source_target_pairs={{0,14},{2,0},{4,2},{6,4},{8,6},{10,8},{12,10},{14,12},{1,15},{3,1}... | collective-permute-start | bytes 528392 | tf_op jit(solution)/shard_map/ppermute | solution.py:49
  120.0 1.9 collective-permute-start.14
  122.4 5.0 %collective-permute-start.18 = (bf16[344,256]{1,0:T(8,128)(2,1)S(1)}, bf16[344,256]{1,0:T(8,128)(2,1)S(1)}, u32[]{:S(2)}, u32[]{:S(2)}) collective-permute-start(bf16[344,256]{1,0:T(8,128)(2,1)S(1)} %collective-permute-done.17.refs_6_), channel_id=1, source_target_pairs={{0,14},{2,0},{4,2},{6,4},{8,6},{10,8},{12,10},{14,12},{1,15},{3,1}... | collective-permute-start | bytes 528392 | tf_op jit(solution)/shard_map/ppermute | solution.py:49
  127.4 1.9 collective-permute-start.15
  131.3 3.4 %collective-permute-start.11 = (bf16[256,344]{1,0:T(8,128)(2,1)S(1)}, bf16[256,344]{1,0:T(8,128)(2,1)S(1)}, u32[]{:S(2)}, u32[]{:S(2)}) collective-permute-start(bf16[256,344]{1,0:T(8,128)(2,1)S(1)} %fusion.1.own), channel_id=1, source_target_pairs={{0,1},{1,0},{2,3},{3,2},{4,5},{5,4},{6,7},{7,6},{8,9},{9,8},{10,11... | collective-permute-start | bytes 528392 | tf_op jit(solution)/shard_map/ppermute | solution.py:17
  134.8 2.9 %collective-permute-done.11.other = bf16[256,344]{1,0:T(8,128)(2,1)S(1)} collective-permute-done((bf16[256,344]{1,0:T(8,128)(2,1)S(1)}, bf16[256,344]{1,0:T(8,128)(2,1)S(1)}, u32[]{:S(2)}, u32[]{:S(2)}) %collective-permute-start.11) | collective-permute-done | bytes 176160 | tf_op jit(solution)/shard_map/ppermute | solution.py:17
  139.1 7.8 %collective-permute-start.19 = (bf16[8,256,256]{2,1,0:T(8,128)(2,1)S(1)}, bf16[8,256,256]{2,1,0:T(8,128)(2,1)S(1)}, u32[]{:S(2)}, u32[]{:S(2)}) collective-permute-start(bf16[8,256,256]{2,1,0:T(8,128)(2,1)S(1)} %down.1), channel_id=1, source_target_pairs={{0,16},{16,0},{1,17},{17,1},{2,18},{18,2},{3,19},{19,3},{4,20},{20... | collective-permute-start | bytes 3145736 | tf_op jit(solution)/shard_map/ppermute | solution.py:17
  155.5 3.5 %all-to-all-start.1 = ((bf16[4,8,64,256]{3,2,1,0:T(8,128)(2,1)}), bf16[4,8,64,256]{3,2,1,0:T(8,128)(2,1)S(1)}, u32[]{:S(2)}, u32[]{:S(2)}) async-start(bf16[4,8,64,256]{3,2,1,0:T(8,128)(2,1)} %down_added.1), calls=%async_computation.1 | async-start | bytes 2097152 | tf_op jit(solution)/shard_map/all_to_all | solution.py:176
  159.6 3.6 %collective-permute-start.20 = (bf16[8,2048]{1,0:T(8,128)(2,1)S(1)}, bf16[8,2048]{1,0:T(8,128)(2,1)S(1)}, u32[]{:S(2)}, u32[]{:S(2)}) collective-permute-start(bf16[8,2048]{1,0:T(8,128)(2,1)S(1)} %convolution_convert_fusion), channel_id=1, source_target_pairs={{0,1},{1,0},{2,3},{3,2},{4,5},{5,4},{6,7},{7,6},{8,9},{9,8},{10,11... | collective-permute-start | bytes 98312 | tf_op jit(solution)/shard_map/ppermute | solution.py:17
  163.5 10.6 %all-to-all-done.1 = bf16[4,8,64,256]{3,2,1,0:T(8,128)(2,1)S(1)} async-done(((bf16[4,8,64,256]{3,2,1,0:T(8,128)(2,1)}), bf16[4,8,64,256]{3,2,1,0:T(8,128)(2,1)S(1)}, u32[]{:S(2)}, u32[]{:S(2)}) %all-to-all-start.1) | async-done | bytes 1048608 | tf_op jit(solution)/shard_map/all_to_all | solution.py:176
  175.0 4.1 %all-to-all-start.2 = ((bf16[8,8,8,256]{3,2,1,0:T(8,128)(2,1)}), bf16[8,8,8,256]{3,2,1,0:T(8,128)(2,1)S(1)}, u32[]{:S(2)}, u32[]{:S(2)}) async-start(bf16[8,8,8,256]{3,2,1,0:T(8,128)(2,1)} %bitcast.15), calls=%async_computation.2 | async-start | bytes 524288 | tf_op jit(solution)/shard_map/all_to_all | solution.py:180
  179.2 10.2 %all-to-all-done.2 = bf16[8,8,8,256]{3,2,1,0:T(8,128)(2,1)S(1)} async-done(((bf16[8,8,8,256]{3,2,1,0:T(8,128)(2,1)}), bf16[8,8,8,256]{3,2,1,0:T(8,128)(2,1)S(1)}, u32[]{:S(2)}, u32[]{:S(2)}) %all-to-all-start.2) | async-done | bytes 262176 | tf_op jit(solution)/shard_map/all_to_all | solution.py:180
  190.7 11.9 %all_to_all.31 = bf16[16,8,384]{2,1,0:T(8,128)(2,1)S(1)} all-to-all(bf16[16,8,384]{2,1,0:T(8,128)(2,1)S(1)} %pad_maximum_fusion.3), channel_id=1, replica_groups=mesh['yh'=4,'x'=4,'c'=2,'z'=8,'yl'=2] {'z','yl'}, dimensions={0} | all-to-all | bytes 196608 | tf_op jit(solution)/shard_map/all_to_all | solution.py:192
  203.2 16.8 %all_to_all.32 = bf16[32,2,384]{2,1,0:T(2,128)(2,1)S(1)} all-to-all(bf16[32,2,384]{2,1,0:T(2,128)(2,1)S(1)} %reshape.97), channel_id=1, replica_groups=mesh['yh'=4,'x'=4,'c'=2,'z'=8,'yl'=2] {'yh','x','c'}, dimensions={0} | all-to-all | bytes 98304 | tf_op jit(solution)/shard_map/all_to_all | solution.py:197
  220.7 3.5 %all-to-all-start.5 = ((f32[16,2,256]{2,1,0:T(2,128)}), f32[16,2,256]{2,1,0:T(2,128)S(1)}, u32[]{:S(2)}, u32[]{:S(2)}) async-start(f32[16,2,256]{2,1,0:T(2,128)} %broadcast_in_dim.16), calls=%async_computation.5 | async-start | bytes 65536 | tf_op jit(solution)/shard_map/all_to_all | solution.py:22
  224.3 7.4 %all-to-all-done.5 = f32[16,2,256]{2,1,0:T(2,128)S(1)} async-done(((f32[16,2,256]{2,1,0:T(2,128)}), f32[16,2,256]{2,1,0:T(2,128)S(1)}, u32[]{:S(2)}, u32[]{:S(2)}) %all-to-all-start.5) | async-done | bytes 32800 | tf_op jit(solution)/shard_map/all_to_all | solution.py:22
  (115 shorter events, 30.0 us)
Async XLA Ops:
  2.2 51.1 %copy-start.8 = (bf16[256,344]{0,1:T(8,128)(2,1)S(1)}, bf16[256,344]{0,1:T(8,128)(2,1)}, u32[]{:S(2)}) copy-start(bf16[256,344]{0,1:T(8,128)(2,1)} %param.11) | copy-start | bytes 528388
  2.2 51.2 %copy-start.9 = (bf16[256,344]{0,1:T(8,128)(2,1)S(1)}, bf16[256,344]{0,1:T(8,128)(2,1)}, u32[]{:S(2)}) copy-start(bf16[256,344]{0,1:T(8,128)(2,1)} %param.10) | copy-start | bytes 528388
  2.3 5.5 %collective-permute-start = (bf16[8,2176]{1,0:T(8,128)(2,1)S(1)}, bf16[8,2176]{1,0:T(8,128)(2,1)S(1)}, u32[]{:S(2)}, u32[]{:S(2)}) collective-permute-start(bf16[8,2176]{1,0:T(8,128)(2,1)S(1)} %pad_maximum_fusion.6), channel_id=1, source_target_pairs={{0,1},{1,0},{2,3},{3,2},{4,5},{5,4},{6,7},{7,6},{8,9},{9,8},{10,11... | collective-permute-start | bytes 104456 | tf_op jit(solution)/shard_map/ppermute | solution.py:17
  8.4 83.1 %copy-start = (bf16[344,256]{1,0:T(8,128)(2,1)S(1)}, bf16[344,256]{1,0:T(8,128)(2,1)}, u32[]{:S(2)}) copy-start(bf16[344,256]{1,0:T(8,128)(2,1)} %refs_0_.3) | copy-start | bytes 528388
  48.9 60.3 %copy-start.5 = (bf16[16,16,2304]{2,1,0:T(8,128)(2,1)}, bf16[16,16,2304]{2,1,0:T(8,128)(2,1)S(1)}, u32[]{:S(2)}) copy-start(bf16[16,16,2304]{2,1,0:T(8,128)(2,1)S(1)} %all_to_all.30) | copy-start | bytes 3538948
  48.9 60.3 %collective-permute-start.1 = (bf16[16,16,2304]{2,1,0:T(8,128)(2,1)S(1)}, bf16[16,16,2304]{2,1,0:T(8,128)(2,1)S(1)}, u32[]{:S(2)}, u32[]{:S(2)}) collective-permute-start(bf16[16,16,2304]{2,1,0:T(8,128)(2,1)S(1)} %all_to_all.30), channel_id=1, source_target_pairs={{0,16},{16,0},{1,17},{17,1},{2,18},{18,2},{3,19},{19,3},{4,20},{20... | collective-permute-start | bytes 3538952 | tf_op jit(solution)/shard_map/ppermute | solution.py:17
  53.4 19.3 %collective-permute-start.2 = (bf16[688,256]{1,0:T(8,128)(2,1)S(1)}, bf16[688,256]{1,0:T(8,128)(2,1)S(1)}, u32[]{:S(2)}, u32[]{:S(2)}) collective-permute-start(bf16[688,256]{1,0:T(8,128)(2,1)S(1)} %pad_maximum_fusion.1.refs_0_), channel_id=1, source_target_pairs={{0,2},{2,4},{4,6},{6,8},{8,10},{10,12},{12,14},{14,0},{1,3},{3,5},... | collective-permute-start | bytes 1056776 | tf_op jit(solution)/shard_map/ppermute | solution.py:49
  57.4 17.2 %collective-permute-start.5 = (bf16[688,256]{1,0:T(8,128)(2,1)S(1)}, bf16[688,256]{1,0:T(8,128)(2,1)S(1)}, u32[]{:S(2)}, u32[]{:S(2)}) collective-permute-start(bf16[688,256]{1,0:T(8,128)(2,1)S(1)} %pad_maximum_fusion.1.refs_0_), channel_id=1, source_target_pairs={{0,14},{2,0},{4,2},{6,4},{8,6},{10,8},{12,10},{14,12},{1,15},{3,1}... | collective-permute-start | bytes 1056776 | tf_op jit(solution)/shard_map/ppermute | solution.py:49
  72.7 12.3 %collective-permute-start.3 = (bf16[688,256]{1,0:T(8,128)(2,1)S(1)}, bf16[688,256]{1,0:T(8,128)(2,1)S(1)}, u32[]{:S(2)}, u32[]{:S(2)}) collective-permute-start(bf16[688,256]{1,0:T(8,128)(2,1)S(1)} %collective-permute-done.2.refs_1_), channel_id=1, source_target_pairs={{0,2},{2,4},{4,6},{6,8},{8,10},{10,12},{12,14},{14,0},{1,3},{3,5},... | collective-permute-start | bytes 1056776 | tf_op jit(solution)/shard_map/ppermute | solution.py:49
  74.6 12.3 %collective-permute-start.6 = (bf16[688,256]{1,0:T(8,128)(2,1)S(1)}, bf16[688,256]{1,0:T(8,128)(2,1)S(1)}, u32[]{:S(2)}, u32[]{:S(2)}) collective-permute-start(bf16[688,256]{1,0:T(8,128)(2,1)S(1)} %collective-permute-done.5.refs_6_), channel_id=1, source_target_pairs={{0,14},{2,0},{4,2},{6,4},{8,6},{10,8},{12,10},{14,12},{1,15},{3,1}... | collective-permute-start | bytes 1056776 | tf_op jit(solution)/shard_map/ppermute | solution.py:49
  84.9 17.6 %collective-permute-start.4 = (bf16[688,256]{1,0:T(8,128)(2,1)S(1)}, bf16[688,256]{1,0:T(8,128)(2,1)S(1)}, u32[]{:S(2)}, u32[]{:S(2)}) collective-permute-start(bf16[688,256]{1,0:T(8,128)(2,1)S(1)} %collective-permute-done.3.refs_2_), channel_id=1, source_target_pairs={{0,2},{2,4},{4,6},{6,8},{8,10},{10,12},{12,14},{14,0},{1,3},{3,5},... | collective-permute-start | bytes 1056776 | tf_op jit(solution)/shard_map/ppermute | solution.py:49
  86.9 17.6 %collective-permute-start.7 = (bf16[688,256]{1,0:T(8,128)(2,1)S(1)}, bf16[688,256]{1,0:T(8,128)(2,1)S(1)}, u32[]{:S(2)}, u32[]{:S(2)}) collective-permute-start(bf16[688,256]{1,0:T(8,128)(2,1)S(1)} %collective-permute-done.6.refs_5_), channel_id=1, source_target_pairs={{0,14},{2,0},{4,2},{6,4},{8,6},{10,8},{12,10},{14,12},{1,15},{3,1}... | collective-permute-start | bytes 1056776 | tf_op jit(solution)/shard_map/ppermute | solution.py:49
  91.5 9.2 %collective-permute-start.12 = (bf16[344,256]{1,0:T(8,128)(2,1)S(1)}, bf16[344,256]{1,0:T(8,128)(2,1)S(1)}, u32[]{:S(2)}, u32[]{:S(2)}) collective-permute-start(bf16[344,256]{1,0:T(8,128)(2,1)S(1)} %copy-done), channel_id=1, source_target_pairs={{0,2},{2,4},{4,6},{6,8},{8,10},{10,12},{12,14},{14,0},{1,3},{3,5},... | collective-permute-start | bytes 528392 | tf_op jit(solution)/shard_map/ppermute | solution.py:49
  93.4 22.5 %collective-permute-start.16 = (bf16[344,256]{1,0:T(8,128)(2,1)S(1)}, bf16[344,256]{1,0:T(8,128)(2,1)S(1)}, u32[]{:S(2)}, u32[]{:S(2)}) collective-permute-start(bf16[344,256]{1,0:T(8,128)(2,1)S(1)} %copy-done), channel_id=1, source_target_pairs={{0,14},{2,0},{4,2},{6,4},{8,6},{10,8},{12,10},{14,12},{1,15},{3,1}... | collective-permute-start | bytes 528392 | tf_op jit(solution)/shard_map/ppermute | solution.py:49
  100.6 19.3 %collective-permute-start.13 = (bf16[344,256]{1,0:T(8,128)(2,1)S(1)}, bf16[344,256]{1,0:T(8,128)(2,1)S(1)}, u32[]{:S(2)}, u32[]{:S(2)}) collective-permute-start(bf16[344,256]{1,0:T(8,128)(2,1)S(1)} %collective-permute-done.12.refs_1_), channel_id=1, source_target_pairs={{0,2},{2,4},{4,6},{6,8},{8,10},{10,12},{12,14},{14,0},{1,3},{3,5},... | collective-permute-start | bytes 528392 | tf_op jit(solution)/shard_map/ppermute | solution.py:49
  102.6 9.7 %collective-permute-start.8 = (bf16[384,256]{1,0:T(8,128)(2,1)S(1)}, bf16[384,256]{1,0:T(8,128)(2,1)S(1)}, u32[]{:S(2)}, u32[]{:S(2)}) collective-permute-start(bf16[384,256]{1,0:T(8,128)(2,1)S(1)} %slice.82), channel_id=1, source_target_pairs={{0,2},{2,4},{4,6},{6,8},{8,10},{10,12},{12,14},{14,0},{1,3},{3,5},... | collective-permute-start | bytes 589832 | tf_op jit(solution)/shard_map/ppermute | solution.py:49
  104.5 6.7 %collective-permute-start.9 = (bf16[304,256]{1,0:T(8,128)(2,1)S(1)}, bf16[304,256]{1,0:T(8,128)(2,1)S(1)}, u32[]{:S(2)}, u32[]{:S(2)}) collective-permute-start(bf16[304,256]{1,0:T(8,128)(2,1)S(1)} %slice.83), channel_id=1, source_target_pairs={{0,14},{2,0},{4,2},{6,4},{8,6},{10,8},{12,10},{14,12},{1,15},{3,1}... | collective-permute-start | bytes 466952 | tf_op jit(solution)/shard_map/ppermute | solution.py:49
  114.0 17.0 %collective-permute-start.10 = (bf16[256,688]{1,0:T(8,128)(2,1)S(1)}, bf16[256,688]{1,0:T(8,128)(2,1)S(1)}, u32[]{:S(2)}, u32[]{:S(2)}) collective-permute-start(bf16[256,688]{1,0:T(8,128)(2,1)S(1)} %gate_up.3), channel_id=1, source_target_pairs={{0,1},{1,0},{2,3},{3,2},{4,5},{5,4},{6,7},{7,6},{8,9},{9,8},{10,11... | collective-permute-start | bytes 1056776 | tf_op jit(solution)/shard_map/ppermute | solution.py:17
  115.9 6.5 %collective-permute-start.17 = (bf16[344,256]{1,0:T(8,128)(2,1)S(1)}, bf16[344,256]{1,0:T(8,128)(2,1)S(1)}, u32[]{:S(2)}, u32[]{:S(2)}) collective-permute-start(bf16[344,256]{1,0:T(8,128)(2,1)S(1)} %collective-permute-done.16.refs_7_), channel_id=1, source_target_pairs={{0,14},{2,0},{4,2},{6,4},{8,6},{10,8},{12,10},{14,12},{1,15},{3,1}... | collective-permute-start | bytes 528392 | tf_op jit(solution)/shard_map/ppermute | solution.py:49
  120.0 7.4 %collective-permute-start.14 = (bf16[344,256]{1,0:T(8,128)(2,1)S(1)}, bf16[344,256]{1,0:T(8,128)(2,1)S(1)}, u32[]{:S(2)}, u32[]{:S(2)}) collective-permute-start(bf16[344,256]{1,0:T(8,128)(2,1)S(1)} %collective-permute-done.13.refs_2_), channel_id=1, source_target_pairs={{0,2},{2,4},{4,6},{6,8},{8,10},{10,12},{12,14},{14,0},{1,3},{3,5},... | collective-permute-start | bytes 528392 | tf_op jit(solution)/shard_map/ppermute | solution.py:49
  122.4 12.3 %collective-permute-start.18 = (bf16[344,256]{1,0:T(8,128)(2,1)S(1)}, bf16[344,256]{1,0:T(8,128)(2,1)S(1)}, u32[]{:S(2)}, u32[]{:S(2)}) collective-permute-start(bf16[344,256]{1,0:T(8,128)(2,1)S(1)} %collective-permute-done.17.refs_6_), channel_id=1, source_target_pairs={{0,14},{2,0},{4,2},{6,4},{8,6},{10,8},{12,10},{14,12},{1,15},{3,1}... | collective-permute-start | bytes 528392 | tf_op jit(solution)/shard_map/ppermute | solution.py:49
  127.4 7.4 %collective-permute-start.15 = (bf16[344,256]{1,0:T(8,128)(2,1)S(1)}, bf16[344,256]{1,0:T(8,128)(2,1)S(1)}, u32[]{:S(2)}, u32[]{:S(2)}) collective-permute-start(bf16[344,256]{1,0:T(8,128)(2,1)S(1)} %collective-permute-done.14.refs_3_), channel_id=1, source_target_pairs={{0,2},{2,4},{4,6},{6,8},{8,10},{10,12},{12,14},{14,0},{1,3},{3,5},... | collective-permute-start | bytes 528392 | tf_op jit(solution)/shard_map/ppermute | solution.py:49
  131.3 6.4 %collective-permute-start.11 = (bf16[256,344]{1,0:T(8,128)(2,1)S(1)}, bf16[256,344]{1,0:T(8,128)(2,1)S(1)}, u32[]{:S(2)}, u32[]{:S(2)}) collective-permute-start(bf16[256,344]{1,0:T(8,128)(2,1)S(1)} %fusion.1.own), channel_id=1, source_target_pairs={{0,1},{1,0},{2,3},{3,2},{4,5},{5,4},{6,7},{7,6},{8,9},{9,8},{10,11... | collective-permute-start | bytes 528392 | tf_op jit(solution)/shard_map/ppermute | solution.py:17
  139.1 10.3 %collective-permute-start.19 = (bf16[8,256,256]{2,1,0:T(8,128)(2,1)S(1)}, bf16[8,256,256]{2,1,0:T(8,128)(2,1)S(1)}, u32[]{:S(2)}, u32[]{:S(2)}) collective-permute-start(bf16[8,256,256]{2,1,0:T(8,128)(2,1)S(1)} %down.1), channel_id=1, source_target_pairs={{0,16},{16,0},{1,17},{17,1},{2,18},{18,2},{3,19},{19,3},{4,20},{20... | collective-permute-start | bytes 3145736 | tf_op jit(solution)/shard_map/ppermute | solution.py:17
  155.5 18.6 %all-to-all-start.1 = ((bf16[4,8,64,256]{3,2,1,0:T(8,128)(2,1)}), bf16[4,8,64,256]{3,2,1,0:T(8,128)(2,1)S(1)}, u32[]{:S(2)}, u32[]{:S(2)}) async-start(bf16[4,8,64,256]{3,2,1,0:T(8,128)(2,1)} %down_added.1), calls=%async_computation.1 | async-start | bytes 2097152 | tf_op jit(solution)/shard_map/all_to_all | solution.py:176
  159.6 19.6 %collective-permute-start.20 = (bf16[8,2048]{1,0:T(8,128)(2,1)S(1)}, bf16[8,2048]{1,0:T(8,128)(2,1)S(1)}, u32[]{:S(2)}, u32[]{:S(2)}) collective-permute-start(bf16[8,2048]{1,0:T(8,128)(2,1)S(1)} %convolution_convert_fusion), channel_id=1, source_target_pairs={{0,1},{1,0},{2,3},{3,2},{4,5},{5,4},{6,7},{7,6},{8,9},{9,8},{10,11... | collective-permute-start | bytes 98312 | tf_op jit(solution)/shard_map/ppermute | solution.py:17
  174.2 15.5 %copy-start.7 = (bf16[8,4096]{1,0:T(8,128)(2,1)S(1)}, bf16[8,4096]{1,0:T(8,128)(2,1)}, u32[]{:S(2)}) copy-start(bf16[8,4096]{1,0:T(8,128)(2,1)} %param.8) | copy-start | bytes 196612
  174.2 15.7 %copy-start.12 = (f32[4096]{0:T(1024)S(1)}, f32[4096]{0:T(1024)}, u32[]{:S(2)}) copy-start(f32[4096]{0:T(1024)} %param.9) | copy-start | bytes 49156
  174.3 15.6 %copy-start.14 = (f32[8]{0:T(128)S(1)}, f32[8]{0:T(128)}, u32[]{:S(2)}) copy-start(f32[8]{0:T(128)} %compare_convert_fusion.1) | copy-start | bytes 100
  175.0 56.7 %copy-start.10 = (f32[2,4096]{1,0:T(2,128)S(1)}, f32[2,4096]{1,0:T(2,128)}, u32[]{:S(2)}) copy-start(f32[2,4096]{1,0:T(2,128)} %param.13) | copy-start | bytes 98308
  175.0 14.4 %all-to-all-start.2 = ((bf16[8,8,8,256]{3,2,1,0:T(8,128)(2,1)}), bf16[8,8,8,256]{3,2,1,0:T(8,128)(2,1)S(1)}, u32[]{:S(2)}, u32[]{:S(2)}) async-start(bf16[8,8,8,256]{3,2,1,0:T(8,128)(2,1)} %bitcast.15), calls=%async_computation.2 | async-start | bytes 524288 | tf_op jit(solution)/shard_map/all_to_all | solution.py:180
  220.7 11.0 %all-to-all-start.5 = ((f32[16,2,256]{2,1,0:T(2,128)}), f32[16,2,256]{2,1,0:T(2,128)S(1)}, u32[]{:S(2)}, u32[]{:S(2)}) async-start(f32[16,2,256]{2,1,0:T(2,128)} %broadcast_in_dim.16), calls=%async_computation.5 | async-start | bytes 65536 | tf_op jit(solution)/shard_map/all_to_all | solution.py:22
  (7 other events, 12.4 us)

commit v2 on v1

--- a/solution.py
+++ b/solution.py
@@ -49,29 +49,30 @@
     return lax.ppermute(value, "z", pairs)
 
 
-def rings(first, second):
-    firsts, seconds = [first] + [None] * 7, [second] + [None] * 7
+def ring(block):
+    blocks = [block] + [None] * 7
     for step in range(1, 4):
-        firsts[step] = hop(firsts[step - 1], AHEAD)
-        firsts[8 - step] = hop(firsts[(9 - step) % 8], BACK)
-        seconds[step] = hop(seconds[step - 1], AHEAD)
-        seconds[8 - step] = hop(seconds[(9 - step) % 8], BACK)
-    upper = hop(firsts[3][:384], AHEAD)
-    lower = hop(firsts[5][384:], BACK)
-    seconds[4] = hop(seconds[3], AHEAD)
-    return [*firsts[:4], *firsts[5:], upper, lower], seconds
-
-
-def gate_up_kernel(rows, *refs):
-    *blocks, upper, lower, out = refs
+        blocks[step] = hop(blocks[step - 1], AHEAD)
+        blocks[8 - step] = hop(blocks[(9 - step) % 8], BACK)
+    blocks[4] = hop(blocks[3], AHEAD)
+    return blocks
+
+
+EARLY = (0, 1, 7, 2, 6, 3, 5)
+
+
+def early_kernel(rows, *refs):
+    *blocks, out = refs
     for start in range(0, 256, 128):
         total = 0.0
-        for j in (0, 1, 2, 3, 5, 6, 7):
+        for j, block in zip(EARLY, blocks):
             x = rows[start : start + 128, 256 * j : 256 * j + 256]
-            total += times(x, blocks[j - (j > 4)][...])
-        x = rows[start : start + 128, 1024:1280]
-        out[start : start + 128, :384] = (total[:, :384] + times(x, upper[...])).astype(out.dtype)
-        out[start : start + 128, 384:] = (total[:, 384:] + times(x, lower[...])).astype(out.dtype)
+            total += times(x, block[:688])
+        out[start : start + 128] = total
+
+
+def last_kernel(rows, early, block, out):
+    out[...] = (early[...] + times(rows[:, 1024:1280], block[:688])).astype(out.dtype)
 
 
 def times(a, b):
@@ -85,16 +86,23 @@
     return pl.BlockSpec(shape, lambda: (0,) * len(shape))
 
 
-def gate_up(rows, blocks, dtype):
+def product(kernel, dtype, depth, *operands):
     return pl.pallas_call(
-        gate_up_kernel,
+        kernel,
         out_shape=jax.ShapeDtypeStruct((256, 688), dtype),
-        in_specs=[VMEM] * 10,
+        in_specs=[VMEM] * len(operands),
         out_specs=VMEM,
-        cost_estimate=pl.CostEstimate(flops=2 * 256 * 2048 * 688, bytes_accessed=4 << 20, transcendentals=0),
+        cost_estimate=pl.CostEstimate(flops=2 * 256 * depth * 688, bytes_accessed=2048 * depth, transcendentals=0),
         compiler_params=pltpu.CompilerParams(vmem_limit_bytes=16 << 20),
-        name="gate_up",
-    )(rows, *blocks)
+    )(*operands)
+
+
+def early_product(rows, blocks):
+    return product(early_kernel, F32, 1792, rows, *[blocks[j] for j in EARLY])
+
+
+def last_product(rows, early, blocks, dtype):
+    return product(last_kernel, dtype, 256, rows, early, blocks[4])
 
 
 def rows_of(core, own, other):
@@ -108,14 +116,14 @@
     *blocks, out = refs
     hidden = rows_of(1, own, other)
     for j in range(8):
-        out[j] = jnp.dot(hidden, blocks[j][...], preferred_element_type=F32).astype(BF16)
+        out[j] = jnp.dot(hidden, blocks[j][688:], preferred_element_type=F32).astype(BF16)
 
 
 def down_added_kernel(own, other, added, *refs):
     *blocks, out = refs
     hidden = rows_of(0, own, other)
     for j in range(8):
-        terms = jnp.dot(hidden, blocks[j][...], preferred_element_type=F32)
+        terms = jnp.dot(hidden, blocks[j][688:], preferred_element_type=F32)
         terms = (terms + added[j].astype(F32)).astype(BF16)
         for x in range(4):
             out[x, j] = terms[64 * x : 64 * x + 64]
@@ -141,7 +149,7 @@
 def program(features, norm_gain, gate_weight, up_weight, down_weight, centroids, list_ids, live):
     yl = lax.axis_index("yl")
     z = lax.axis_index("z")
-    first, second = rings(jnp.concatenate([gate_weight.T, up_weight.T], axis=0), down_weight)
+    weights = ring(jnp.concatenate([gate_weight.T, up_weight.T, down_weight], axis=0))
 
     code = jnp.where(live > 0, list_ids, -1).astype(BF16)
     code_block = jnp.broadcast_to(code[:, None], (8, 128))
@@ -157,12 +165,13 @@
     rows = both[..., :2048].reshape(2, 16, 2, 8, 2048)
     kept = rows[:, :, 0].reshape(256, 2048)
     away = rows[:, :, 1].reshape(256, 2048)
-    away_part = swapped(gate_up(away, first, BF16), "yl")
-    both = gate_up(kept, first, F32) + away_part.astype(F32)
+    away_early, kept_early = early_product(away, weights), early_product(kept, weights)
+    away_part = swapped(last_product(away, away_early, weights, BF16), "yl")
+    both = last_product(kept, kept_early, weights, F32) + away_part.astype(F32)
     hidden = (jax.nn.silu(both[:, :344]) * both[:, 344:]).astype(BF16)
     other_hidden = swapped(hidden, "yl")
-    from_core = swapped(down(hidden, other_hidden, second), "c")
-    terms = down(hidden, other_hidden, second, from_core)
+    from_core = swapped(down(hidden, other_hidden, weights), "c")
+    terms = down(hidden, other_hidden, weights, from_core)
 
     mine, theirs, terms = lax.optimization_barrier((mine, theirs, terms))
     core = lax.axis_index("c")

time: 234 us -> 223 us (0.953)
  waiting for transfers between devices: 49.1 us -> 94.3 us
  blocking collectives: 69.1 us -> 26.6 us
  starting transfers between devices: 89.7 us -> 74.3 us
  Pallas kernels: 5.86 us -> 8.56 us
    all_to_all x1 -> x0, blocking collectives: 40.4 us -> none  [to_everyone(): return lax.all_to_all(copies, axis, split_axis=0, concat_axis=0, tiled=True)]
    all_to_all x1 -> x2, waiting for transfers between devices: 7.36 us -> 32.5 us  [to_everyone(): return lax.all_to_all(copies, axis, split_axis=0, concat_axis=0, tiled=True)]
    ppermute x15 -> x7, starting transfers between devices: 53.3 us -> 31 us  [hop(): return lax.ppermute(value, 'z', pairs)]
    all_to_all x1 -> x2, starting transfers between devices: 3.5 us -> 13.2 us  [to_everyone(): return lax.all_to_all(copies, axis, split_axis=0, concat_axis=0, tiled=True)]
    ppermute x6, waiting for transfers between devices: 3.29 us -> 12.8 us  [swapped(): return lax.ppermute(value, axis, SWAP)]
    ppermute x15 -> x7, waiting for transfers between devices: 17.7 us -> 26.9 us  [hop(): return lax.ppermute(value, 'z', pairs)]
  transfers between devices with their start and end apart: 24 -> 17, of which waited for: 12 -> 12; matrix products, arithmetic and copies ran while one was open for 3% -> 2% of each run, Pallas kernels for 1% -> 2%
where the time goes in v2:
time: 223 us; the launch traced here: 222 us
  waiting for transfers between devices  94.3 us (42%)
  starting transfers between devices  74.3 us (33%)
  blocking collectives  26.6 us (12%)
  local copies, waits for them, and re-layouts  8.66 us (4%)
  Pallas kernels  8.56 us (4%)
  other arithmetic  7.55 us (3%)
    all_to_all x2, waiting for transfers between devices, to_everyone(): return lax.all_to_all(copies, axis, split_axis=0, concat_axis=0, tiled=True)  32.5 us
    ppermute x7, starting transfers between devices, hop(): return lax.ppermute(value, 'z', pairs)  31 us
    ppermute x7, waiting for transfers between devices, hop(): return lax.ppermute(value, 'z', pairs)  26.9 us
    ppermute x6, starting transfers between devices, swapped(): return lax.ppermute(value, axis, SWAP)  23 us
    all_to_all x1, blocking collectives, program(): sums = lax.all_to_all(sums.reshape(32, 2, 384), LIST, 0, 0, tiled=True)  16 us
    all_to_all x2, starting transfers between devices, to_everyone(): return lax.all_to_all(copies, axis, split_axis=0, concat_axis=0, tiled=True)  13.2 us
    ppermute x6, waiting for transfers between devices, swapped(): return lax.ppermute(value, axis, SWAP)  12.8 us
    all_to_all x1, waiting for transfers between devices, program(): terms = lax.all_to_all(terms, 'x', 0, 0, tiled=True)  12.1 us
  transfers between devices with their start and end apart: 17, of which 12 were waited for; matrix products, arithmetic and copies ran while one was open for 2% of the time, Pallas kernels for 2%

profile of v2, /device:TPU:1, one launch (start us, length us, event | category | flops | bytes accessed | tf_op | source)
XLA Modules:
  0.0 221.8 jit_solution(17800188388763003126)
XLA Ops:
  2.3 4.0 %collective-permute-start = (bf16[8,2176]{1,0:T(8,128)(2,1)S(1)}, bf16[8,2176]{1,0:T(8,128)(2,1)S(1)}, u32[]{:S(2)}, u32[]{:S(2)}) collective-permute-start(bf16[8,2176]{1,0:T(8,128)(2,1)S(1)} %pad_maximum_fusion.6), channel_id=1, source_target_pairs={{0,1},{1,0},{2,3},{3,2},{4,5},{5,4},{6,7},{7,6},{8,9},{9,8},{10,11... | collective-permute-start | bytes 104456 | tf_op jit(solution)/shard_map/ppermute | solution.py:17
  8.7 9.7 %all-to-all-start = ((bf16[16,16,2304]{2,1,0:T(8,128)(2,1)}), bf16[16,16,2304]{2,1,0:T(8,128)(2,1)}, u32[]{:S(2)}, u32[]{:S(2)}) async-start(bf16[16,16,2304]{2,1,0:T(8,128)(2,1)} %broadcast_in_dim.14), calls=%async_computation | async-start | bytes 2359296 | tf_op jit(solution)/shard_map/all_to_all | solution.py:22
  18.5 4.0 %collective-permute-start.2 = (bf16[1032,256]{1,0:T(8,128)(2,1)S(1)}, bf16[1032,256]{1,0:T(8,128)(2,1)S(1)}, u32[]{:S(2)}, u32[]{:S(2)}) collective-permute-start(bf16[1032,256]{1,0:T(8,128)(2,1)S(1)} %pad_maximum_fusion.1.refs_0_), channel_id=1, source_target_pairs={{0,2},{2,4},{4,6},{6,8},{8,10},{10,12},{12,14},{14,0},{1,3},{3,5},... | collective-permute-start | bytes 1585160 | tf_op jit(solution)/shard_map/ppermute | solution.py:49
  22.5 25.1 %all-to-all-done = bf16[16,16,2304]{2,1,0:T(8,128)(2,1)} async-done(((bf16[16,16,2304]{2,1,0:T(8,128)(2,1)}), bf16[16,16,2304]{2,1,0:T(8,128)(2,1)}, u32[]{:S(2)}, u32[]{:S(2)}) %all-to-all-start) | async-done | bytes 1179680 | tf_op jit(solution)/shard_map/all_to_all | solution.py:22
  47.6 6.2 %collective-permute-start.1 = (bf16[16,16,2304]{2,1,0:T(8,128)(2,1)}, bf16[16,16,2304]{2,1,0:T(8,128)(2,1)S(1)}, u32[]{:S(2)}, u32[]{:S(2)}) collective-permute-start(bf16[16,16,2304]{2,1,0:T(8,128)(2,1)} %all-to-all-done), channel_id=1, source_target_pairs={{0,16},{16,0},{1,17},{17,1},{2,18},{18,2},{3,19},{19,3},{4,20},{20... | collective-permute-start | bytes 3538952 | tf_op jit(solution)/shard_map/ppermute | solution.py:17
  53.8 10.7 %collective-permute-start.3 = (bf16[1032,256]{1,0:T(8,128)(2,1)S(1)}, bf16[1032,256]{1,0:T(8,128)(2,1)S(1)}, u32[]{:S(2)}, u32[]{:S(2)}) collective-permute-start(bf16[1032,256]{1,0:T(8,128)(2,1)S(1)} %pad_maximum_fusion.1.refs_0_), channel_id=1, source_target_pairs={{0,14},{2,0},{4,2},{6,4},{8,6},{10,8},{12,10},{14,12},{1,15},{3,1}... | collective-permute-start | bytes 1585160 | tf_op jit(solution)/shard_map/ppermute | solution.py:49
  64.5 1.9 collective-permute-start.4
  66.4 9.4 %collective-permute-done.3.refs_2_.refs_7_ = bf16[1032,256]{1,0:T(8,128)(2,1)S(1)} collective-permute-done((bf16[1032,256]{1,0:T(8,128)(2,1)S(1)}, bf16[1032,256]{1,0:T(8,128)(2,1)S(1)}, u32[]{:S(2)}, u32[]{:S(2)}) %collective-permute-start.3) | collective-permute-done | bytes 528416 | tf_op jit(solution)/shard_map/ppermute | solution.py:49
  75.8 5.3 %collective-permute-start.5 = (bf16[1032,256]{1,0:T(8,128)(2,1)S(1)}, bf16[1032,256]{1,0:T(8,128)(2,1)S(1)}, u32[]{:S(2)}, u32[]{:S(2)}) collective-permute-start(bf16[1032,256]{1,0:T(8,128)(2,1)S(1)} %collective-permute-done.3.refs_2_.refs_7_), channel_id=1, source_target_pairs={{0,14},{2,0},{4,2},{6,4},{8,6},{10,8},{12,10},{14,12},{1,15},{3,1}... | collective-permute-start | bytes 1585160 | tf_op jit(solution)/shard_map/ppermute | solution.py:49
  81.2 1.9 collective-permute-start.6
  83.1 8.5 %collective-permute-done.5.refs_4_.refs_6_ = bf16[1032,256]{1,0:T(8,128)(2,1)S(1)} collective-permute-done((bf16[1032,256]{1,0:T(8,128)(2,1)S(1)}, bf16[1032,256]{1,0:T(8,128)(2,1)S(1)}, u32[]{:S(2)}, u32[]{:S(2)}) %collective-permute-start.5) | collective-permute-done | bytes 528416 | tf_op jit(solution)/shard_map/ppermute | solution.py:49
  91.6 5.3 %collective-permute-start.7 = (bf16[1032,256]{1,0:T(8,128)(2,1)S(1)}, bf16[1032,256]{1,0:T(8,128)(2,1)S(1)}, u32[]{:S(2)}, u32[]{:S(2)}) collective-permute-start(bf16[1032,256]{1,0:T(8,128)(2,1)S(1)} %collective-permute-done.5.refs_4_.refs_6_), channel_id=1, source_target_pairs={{0,14},{2,0},{4,2},{6,4},{8,6},{10,8},{12,10},{14,12},{1,15},{3,1}... | collective-permute-start | bytes 1585160 | tf_op jit(solution)/shard_map/ppermute | solution.py:49
  96.9 1.9 collective-permute-start.8
  98.9 1.9 fusion
  101.0 5.6 %collective-permute-done.7.refs_6_.refs_5_ = bf16[1032,256]{1,0:T(8,128)(2,1)S(1)} collective-permute-done((bf16[1032,256]{1,0:T(8,128)(2,1)S(1)}, bf16[1032,256]{1,0:T(8,128)(2,1)S(1)}, u32[]{:S(2)}, u32[]{:S(2)}) %collective-permute-start.7) | collective-permute-done | bytes 528416 | tf_op jit(solution)/shard_map/ppermute | solution.py:49
  108.2 3.4 %collective-permute-done.8.block.refs_4_ = bf16[1032,256]{1,0:T(8,128)(2,1)S(1)} collective-permute-done((bf16[1032,256]{1,0:T(8,128)(2,1)S(1)}, bf16[1032,256]{1,0:T(8,128)(2,1)S(1)}, u32[]{:S(2)}, u32[]{:S(2)}) %collective-permute-start.8) | collective-permute-done | bytes 528416 | tf_op jit(solution)/shard_map/ppermute | solution.py:49
  111.9 1.9 collective-permute-start.9
  115.8 5.8 %collective-permute-done.9 = bf16[256,688]{1,0:T(8,128)(2,1)S(1)} collective-permute-done((bf16[256,688]{1,0:T(8,128)(2,1)S(1)}, bf16[256,688]{1,0:T(8,128)(2,1)S(1)}, u32[]{:S(2)}, u32[]{:S(2)}) %collective-permute-start.9) | collective-permute-done | bytes 352288 | tf_op jit(solution)/shard_map/ppermute | solution.py:17
  121.9 2.2 collective-permute-start.10
  124.1 4.2 %collective-permute-done.10.other = bf16[256,344]{1,0:T(8,128)(2,1)S(1)} collective-permute-done((bf16[256,344]{1,0:T(8,128)(2,1)S(1)}, bf16[256,344]{1,0:T(8,128)(2,1)S(1)}, u32[]{:S(2)}, u32[]{:S(2)}) %collective-permute-start.10) | collective-permute-done | bytes 176160 | tf_op jit(solution)/shard_map/ppermute | solution.py:17
  130.0 6.8 %collective-permute-start.11 = (bf16[8,256,256]{2,1,0:T(8,128)(2,1)}, bf16[8,256,256]{2,1,0:T(8,128)(2,1)}, u32[]{:S(2)}, u32[]{:S(2)}) collective-permute-start(bf16[8,256,256]{2,1,0:T(8,128)(2,1)} %down.1), channel_id=1, source_target_pairs={{0,16},{16,0},{1,17},{17,1},{2,18},{18,2},{3,19},{19,3},{4,20},{20... | collective-permute-start | bytes 3145736 | tf_op jit(solution)/shard_map/ppermute | solution.py:17
  136.9 2.5 %collective-permute-done.11.added = bf16[8,256,256]{2,1,0:T(8,128)(2,1)} collective-permute-done((bf16[8,256,256]{2,1,0:T(8,128)(2,1)}, bf16[8,256,256]{2,1,0:T(8,128)(2,1)}, u32[]{:S(2)}, u32[]{:S(2)}) %collective-permute-start.11) | collective-permute-done | bytes 1048608 | tf_op jit(solution)/shard_map/ppermute | solution.py:17
  142.4 2.9 %down_added.1 = bf16[4,8,64,256]{3,2,1,0:T(8,128)(2,1)} custom-call(bf16[256,344]{1,0:T(8,128)(2,1)S(1)} %fusion.1.own, bf16[256,344]{1,0:T(8,128)(2,1)S(1)} %copy-done.5, bf16[8,256,256]{2,1,0:T(8,128)(2,1)} %collective-permute-done.11.added, bf16[1032,256]{1,0:T(8,128)(2,1)S(1)} %pad_maximum_fusion.1.refs_0_, ...), custom_call_target="tpu_custom_call" | custom-call | flops 360710144 | bytes 3145728 | tf_op jit(solution)/shard_map/down_added/pallas_call | solution.py:134
  147.9 3.5 %all-to-all-start.1 = ((bf16[4,8,64,256]{3,2,1,0:T(8,128)(2,1)}), bf16[4,8,64,256]{3,2,1,0:T(8,128)(2,1)S(1)}, u32[]{:S(2)}, u32[]{:S(2)}) async-start(bf16[4,8,64,256]{3,2,1,0:T(8,128)(2,1)} %down_added.1), calls=%async_computation.1 | async-start | bytes 2097152 | tf_op jit(solution)/shard_map/all_to_all | solution.py:185
  152.0 1.9 collective-permute-start.12
  154.1 12.1 %all-to-all-done.1 = bf16[4,8,64,256]{3,2,1,0:T(8,128)(2,1)S(1)} async-done(((bf16[4,8,64,256]{3,2,1,0:T(8,128)(2,1)}), bf16[4,8,64,256]{3,2,1,0:T(8,128)(2,1)S(1)}, u32[]{:S(2)}, u32[]{:S(2)}) %all-to-all-start.1) | async-done | bytes 1048608 | tf_op jit(solution)/shard_map/all_to_all | solution.py:185
  167.2 3.5 %all-to-all-start.2 = ((bf16[8,8,8,256]{3,2,1,0:T(8,128)(2,1)}), bf16[8,8,8,256]{3,2,1,0:T(8,128)(2,1)S(1)}, u32[]{:S(2)}, u32[]{:S(2)}) async-start(bf16[8,8,8,256]{3,2,1,0:T(8,128)(2,1)} %bitcast.15), calls=%async_computation.2 | async-start | bytes 524288 | tf_op jit(solution)/shard_map/all_to_all | solution.py:189
  170.8 10.1 %all-to-all-done.2 = bf16[8,8,8,256]{3,2,1,0:T(8,128)(2,1)S(1)} async-done(((bf16[8,8,8,256]{3,2,1,0:T(8,128)(2,1)}), bf16[8,8,8,256]{3,2,1,0:T(8,128)(2,1)S(1)}, u32[]{:S(2)}, u32[]{:S(2)}) %all-to-all-start.2) | async-done | bytes 262176 | tf_op jit(solution)/shard_map/all_to_all | solution.py:189
  182.2 10.6 %all_to_all.30 = bf16[16,8,384]{2,1,0:T(8,128)(2,1)S(1)} all-to-all(bf16[16,8,384]{2,1,0:T(8,128)(2,1)S(1)} %pad_maximum_fusion.3), channel_id=1, replica_groups=mesh['yh'=4,'x'=4,'c'=2,'z'=8,'yl'=2] {'z','yl'}, dimensions={0} | all-to-all | bytes 196608 | tf_op jit(solution)/shard_map/all_to_all | solution.py:201
  193.4 16.0 %all_to_all.31 = bf16[32,2,384]{2,1,0:T(2,128)(2,1)S(1)} all-to-all(bf16[32,2,384]{2,1,0:T(2,128)(2,1)S(1)} %reshape.97), channel_id=1, replica_groups=mesh['yh'=4,'x'=4,'c'=2,'z'=8,'yl'=2] {'yh','x','c'}, dimensions={0} | all-to-all | bytes 98304 | tf_op jit(solution)/shard_map/all_to_all | solution.py:206
  210.1 3.5 %all-to-all-start.5 = ((f32[16,2,256]{2,1,0:T(2,128)}), f32[16,2,256]{2,1,0:T(2,128)S(1)}, u32[]{:S(2)}, u32[]{:S(2)}) async-start(f32[16,2,256]{2,1,0:T(2,128)} %broadcast_in_dim.16), calls=%async_computation.5 | async-start | bytes 65536 | tf_op jit(solution)/shard_map/all_to_all | solution.py:22
  213.7 7.4 %all-to-all-done.5 = f32[16,2,256]{2,1,0:T(2,128)S(1)} async-done(((f32[16,2,256]{2,1,0:T(2,128)}), f32[16,2,256]{2,1,0:T(2,128)S(1)}, u32[]{:S(2)}, u32[]{:S(2)}) %all-to-all-start.5) | async-done | bytes 32800 | tf_op jit(solution)/shard_map/all_to_all | solution.py:22
  (98 shorter events, 20.9 us)
Async XLA Ops:
  2.3 5.3 %collective-permute-start = (bf16[8,2176]{1,0:T(8,128)(2,1)S(1)}, bf16[8,2176]{1,0:T(8,128)(2,1)S(1)}, u32[]{:S(2)}, u32[]{:S(2)}) collective-permute-start(bf16[8,2176]{1,0:T(8,128)(2,1)S(1)} %pad_maximum_fusion.6), channel_id=1, source_target_pairs={{0,1},{1,0},{2,3},{3,2},{4,5},{5,4},{6,7},{7,6},{8,9},{9,8},{10,11... | collective-permute-start | bytes 104456 | tf_op jit(solution)/shard_map/ppermute | solution.py:17
  8.7 9.7 %copy-start.8 = (bf16[344,256]{1,0:T(8,128)(2,1)S(1)}, bf16[344,256]{1,0:T(8,128)(2,1)}, u32[]{:S(2)}) copy-start(bf16[344,256]{1,0:T(8,128)(2,1)} %param.12) | copy-start | bytes 528388
  8.7 9.7 %copy-start.9 = (bf16[256,344]{0,1:T(8,128)(2,1)S(1)}, bf16[256,344]{0,1:T(8,128)(2,1)}, u32[]{:S(2)}) copy-start(bf16[256,344]{0,1:T(8,128)(2,1)} %param.11) | copy-start | bytes 528388
  8.7 9.8 %copy-start.10 = (bf16[256,344]{0,1:T(8,128)(2,1)S(1)}, bf16[256,344]{0,1:T(8,128)(2,1)}, u32[]{:S(2)}) copy-start(bf16[256,344]{0,1:T(8,128)(2,1)} %param.10) | copy-start | bytes 528388
  8.7 38.9 %all-to-all-start = ((bf16[16,16,2304]{2,1,0:T(8,128)(2,1)}), bf16[16,16,2304]{2,1,0:T(8,128)(2,1)}, u32[]{:S(2)}, u32[]{:S(2)}) async-start(bf16[16,16,2304]{2,1,0:T(8,128)(2,1)} %broadcast_in_dim.14), calls=%async_computation | async-start | bytes 2359296 | tf_op jit(solution)/shard_map/all_to_all | solution.py:22
  18.5 46.0 %collective-permute-start.2 = (bf16[1032,256]{1,0:T(8,128)(2,1)S(1)}, bf16[1032,256]{1,0:T(8,128)(2,1)S(1)}, u32[]{:S(2)}, u32[]{:S(2)}) collective-permute-start(bf16[1032,256]{1,0:T(8,128)(2,1)S(1)} %pad_maximum_fusion.1.refs_0_), channel_id=1, source_target_pairs={{0,2},{2,4},{4,6},{6,8},{8,10},{10,12},{12,14},{14,0},{1,3},{3,5},... | collective-permute-start | bytes 1585160 | tf_op jit(solution)/shard_map/ppermute | solution.py:49
  47.6 51.2 %collective-permute-start.1 = (bf16[16,16,2304]{2,1,0:T(8,128)(2,1)}, bf16[16,16,2304]{2,1,0:T(8,128)(2,1)S(1)}, u32[]{:S(2)}, u32[]{:S(2)}) collective-permute-start(bf16[16,16,2304]{2,1,0:T(8,128)(2,1)} %all-to-all-done), channel_id=1, source_target_pairs={{0,16},{16,0},{1,17},{17,1},{2,18},{18,2},{3,19},{19,3},{4,20},{20... | collective-permute-start | bytes 3538952 | tf_op jit(solution)/shard_map/ppermute | solution.py:17
  53.8 22.0 %collective-permute-start.3 = (bf16[1032,256]{1,0:T(8,128)(2,1)S(1)}, bf16[1032,256]{1,0:T(8,128)(2,1)S(1)}, u32[]{:S(2)}, u32[]{:S(2)}) collective-permute-start(bf16[1032,256]{1,0:T(8,128)(2,1)S(1)} %pad_maximum_fusion.1.refs_0_), channel_id=1, source_target_pairs={{0,14},{2,0},{4,2},{6,4},{8,6},{10,8},{12,10},{14,12},{1,15},{3,1}... | collective-permute-start | bytes 1585160 | tf_op jit(solution)/shard_map/ppermute | solution.py:49
  64.5 16.6 %collective-permute-start.4 = (bf16[1032,256]{1,0:T(8,128)(2,1)S(1)}, bf16[1032,256]{1,0:T(8,128)(2,1)S(1)}, u32[]{:S(2)}, u32[]{:S(2)}) collective-permute-start(bf16[1032,256]{1,0:T(8,128)(2,1)S(1)} %collective-permute-done.2.refs_1_), channel_id=1, source_target_pairs={{0,2},{2,4},{4,6},{6,8},{8,10},{10,12},{12,14},{14,0},{1,3},{3,5},... | collective-permute-start | bytes 1585160 | tf_op jit(solution)/shard_map/ppermute | solution.py:49
  75.8 15.8 %collective-permute-start.5 = (bf16[1032,256]{1,0:T(8,128)(2,1)S(1)}, bf16[1032,256]{1,0:T(8,128)(2,1)S(1)}, u32[]{:S(2)}, u32[]{:S(2)}) collective-permute-start(bf16[1032,256]{1,0:T(8,128)(2,1)S(1)} %collective-permute-done.3.refs_2_.refs_7_), channel_id=1, source_target_pairs={{0,14},{2,0},{4,2},{6,4},{8,6},{10,8},{12,10},{14,12},{1,15},{3,1}... | collective-permute-start | bytes 1585160 | tf_op jit(solution)/shard_map/ppermute | solution.py:49
  81.2 15.8 %collective-permute-start.6 = (bf16[1032,256]{1,0:T(8,128)(2,1)S(1)}, bf16[1032,256]{1,0:T(8,128)(2,1)S(1)}, u32[]{:S(2)}, u32[]{:S(2)}) collective-permute-start(bf16[1032,256]{1,0:T(8,128)(2,1)S(1)} %collective-permute-done.4.refs_3_.refs_2_), channel_id=1, source_target_pairs={{0,2},{2,4},{4,6},{6,8},{8,10},{10,12},{12,14},{14,0},{1,3},{3,5},... | collective-permute-start | bytes 1585160 | tf_op jit(solution)/shard_map/ppermute | solution.py:49
  91.6 14.9 %collective-permute-start.7 = (bf16[1032,256]{1,0:T(8,128)(2,1)S(1)}, bf16[1032,256]{1,0:T(8,128)(2,1)S(1)}, u32[]{:S(2)}, u32[]{:S(2)}) collective-permute-start(bf16[1032,256]{1,0:T(8,128)(2,1)S(1)} %collective-permute-done.5.refs_4_.refs_6_), channel_id=1, source_target_pairs={{0,14},{2,0},{4,2},{6,4},{8,6},{10,8},{12,10},{14,12},{1,15},{3,1}... | collective-permute-start | bytes 1585160 | tf_op jit(solution)/shard_map/ppermute | solution.py:49
  96.9 14.7 %collective-permute-start.8 = (bf16[1032,256]{1,0:T(8,128)(2,1)S(1)}, bf16[1032,256]{1,0:T(8,128)(2,1)S(1)}, u32[]{:S(2)}, u32[]{:S(2)}) collective-permute-start(bf16[1032,256]{1,0:T(8,128)(2,1)S(1)} %collective-permute-done.6.refs_5_.refs_3_), channel_id=1, source_target_pairs={{0,2},{2,4},{4,6},{6,8},{8,10},{10,12},{12,14},{14,0},{1,3},{3,5},... | collective-permute-start | bytes 1585160 | tf_op jit(solution)/shard_map/ppermute | solution.py:49
  98.9 2.1 copy-start.6
  106.6 21.7 %copy-start = (bf16[1032,256]{1,0:T(8,128)(2,1)}, bf16[1032,256]{1,0:T(8,128)(2,1)S(1)}, u32[]{:S(2)}) copy-start(bf16[1032,256]{1,0:T(8,128)(2,1)S(1)} %collective-permute-done.7.refs_6_.refs_5_) | copy-start | bytes 1585156
  111.6 16.7 %copy-start.2 = (bf16[1032,256]{1,0:T(8,128)(2,1)}, bf16[1032,256]{1,0:T(8,128)(2,1)S(1)}, u32[]{:S(2)}) copy-start(bf16[1032,256]{1,0:T(8,128)(2,1)S(1)} %collective-permute-done.8.block.refs_4_) | copy-start | bytes 1585156
  111.9 9.7 %collective-permute-start.9 = (bf16[256,688]{1,0:T(8,128)(2,1)S(1)}, bf16[256,688]{1,0:T(8,128)(2,1)S(1)}, u32[]{:S(2)}, u32[]{:S(2)}) collective-permute-start(bf16[256,688]{1,0:T(8,128)(2,1)S(1)} %shard_map.98), channel_id=1, source_target_pairs={{0,1},{1,0},{2,3},{3,2},{4,5},{5,4},{6,7},{7,6},{8,9},{9,8},{10,11... | collective-permute-start | bytes 1056776 | tf_op jit(solution)/shard_map/ppermute | solution.py:17
  121.9 14.9 %copy-start.13 = (s32[8]{0:T(128)S(1)}, s32[8]{0:T(128)}, u32[]{:S(2)}) copy-start(s32[8]{0:T(128)} %param.15) | copy-start | bytes 100
  121.9 6.4 %collective-permute-start.10 = (bf16[256,344]{1,0:T(8,128)(2,1)S(1)}, bf16[256,344]{1,0:T(8,128)(2,1)S(1)}, u32[]{:S(2)}, u32[]{:S(2)}) collective-permute-start(bf16[256,344]{1,0:T(8,128)(2,1)S(1)} %fusion.1.own), channel_id=1, source_target_pairs={{0,1},{1,0},{2,3},{3,2},{4,5},{5,4},{6,7},{7,6},{8,9},{9,8},{10,11... | collective-permute-start | bytes 528392 | tf_op jit(solution)/shard_map/ppermute | solution.py:17
  128.3 1.7 copy-start.4
  130.0 9.4 %collective-permute-start.11 = (bf16[8,256,256]{2,1,0:T(8,128)(2,1)}, bf16[8,256,256]{2,1,0:T(8,128)(2,1)}, u32[]{:S(2)}, u32[]{:S(2)}) collective-permute-start(bf16[8,256,256]{2,1,0:T(8,128)(2,1)} %down.1), channel_id=1, source_target_pairs={{0,16},{16,0},{1,17},{17,1},{2,18},{18,2},{3,19},{19,3},{4,20},{20... | collective-permute-start | bytes 3145736 | tf_op jit(solution)/shard_map/ppermute | solution.py:17
  139.4 1.0 copy-start.1
  140.4 1.0 copy-start.3
  141.5 0.9 copy-start.5
  147.9 18.3 %all-to-all-start.1 = ((bf16[4,8,64,256]{3,2,1,0:T(8,128)(2,1)}), bf16[4,8,64,256]{3,2,1,0:T(8,128)(2,1)S(1)}, u32[]{:S(2)}, u32[]{:S(2)}) async-start(bf16[4,8,64,256]{3,2,1,0:T(8,128)(2,1)} %down_added.1), calls=%async_computation.1 | async-start | bytes 2097152 | tf_op jit(solution)/shard_map/all_to_all | solution.py:185
  152.0 18.7 %collective-permute-start.12 = (bf16[8,2048]{1,0:T(8,128)(2,1)S(1)}, bf16[8,2048]{1,0:T(8,128)(2,1)S(1)}, u32[]{:S(2)}, u32[]{:S(2)}) collective-permute-start(bf16[8,2048]{1,0:T(8,128)(2,1)S(1)} %convolution_convert_fusion), channel_id=1, source_target_pairs={{0,1},{1,0},{2,3},{3,2},{4,5},{5,4},{6,7},{7,6},{8,9},{9,8},{10,11... | collective-permute-start | bytes 98312 | tf_op jit(solution)/shard_map/ppermute | solution.py:17
  167.2 14.1 %copy-start.7 = (bf16[8,4096]{1,0:T(8,128)(2,1)S(1)}, bf16[8,4096]{1,0:T(8,128)(2,1)}, u32[]{:S(2)}) copy-start(bf16[8,4096]{1,0:T(8,128)(2,1)} %param.8) | copy-start | bytes 196612
  167.2 13.7 %all-to-all-start.2 = ((bf16[8,8,8,256]{3,2,1,0:T(8,128)(2,1)}), bf16[8,8,8,256]{3,2,1,0:T(8,128)(2,1)S(1)}, u32[]{:S(2)}, u32[]{:S(2)}) async-start(bf16[8,8,8,256]{3,2,1,0:T(8,128)(2,1)} %bitcast.15), calls=%async_computation.2 | async-start | bytes 524288 | tf_op jit(solution)/shard_map/all_to_all | solution.py:189
  170.7 10.7 %copy-start.12 = (f32[4096]{0:T(1024)S(1)}, f32[4096]{0:T(1024)}, u32[]{:S(2)}) copy-start(f32[4096]{0:T(1024)} %param.9) | copy-start | bytes 49156
  181.0 40.1 %copy-start.11 = (f32[2,4096]{1,0:T(2,128)S(1)}, f32[2,4096]{1,0:T(2,128)}, u32[]{:S(2)}) copy-start(f32[2,4096]{1,0:T(2,128)} %param.13) | copy-start | bytes 98308
  210.1 11.0 %all-to-all-start.5 = ((f32[16,2,256]{2,1,0:T(2,128)}), f32[16,2,256]{2,1,0:T(2,128)S(1)}, u32[]{:S(2)}, u32[]{:S(2)}) async-start(f32[16,2,256]{2,1,0:T(2,128)} %broadcast_in_dim.16), calls=%async_computation.5 | async-start | bytes 65536 | tf_op jit(solution)/shard_map/all_to_all | solution.py:22

commit v3 on v2

--- a/solution.py
+++ b/solution.py
@@ -1,3 +1,5 @@
+import functools
+
 import jax
 import jax.numpy as jnp
 from jax import lax
@@ -54,11 +56,11 @@
     for step in range(1, 4):
         blocks[step] = hop(blocks[step - 1], AHEAD)
         blocks[8 - step] = hop(blocks[(9 - step) % 8], BACK)
-    blocks[4] = hop(blocks[3], AHEAD)
-    return blocks
-
-
-EARLY = (0, 1, 7, 2, 6, 3, 5)
+    fourth = hop(blocks[3][:688], AHEAD), hop(blocks[5][688:], BACK)
+    return [*blocks[:4], *blocks[5:]], *fourth
+
+
+EARLY = (0, 1, 2, 3, 5, 6, 7)
 
 
 def early_kernel(rows, *refs):
@@ -72,7 +74,7 @@
 
 
 def last_kernel(rows, early, block, out):
-    out[...] = (early[...] + times(rows[:, 1024:1280], block[:688])).astype(out.dtype)
+    out[...] = (early[...] + times(rows[:, 1024:1280], block[...])).astype(out.dtype)
 
 
 def times(a, b):
@@ -80,10 +82,6 @@
 
 
 VMEM = pl.BlockSpec(memory_space=pltpu.VMEM)
-
-
-def whole(shape):
-    return pl.BlockSpec(shape, lambda: (0,) * len(shape))
 
 
 def product(kernel, dtype, depth, *operands):
@@ -98,11 +96,11 @@
 
 
 def early_product(rows, blocks):
-    return product(early_kernel, F32, 1792, rows, *[blocks[j] for j in EARLY])
-
-
-def last_product(rows, early, blocks, dtype):
-    return product(last_kernel, dtype, 256, rows, early, blocks[4])
+    return product(early_kernel, F32, 1792, rows, *blocks)
+
+
+def last_product(rows, early, block, dtype):
+    return product(last_kernel, dtype, 256, rows, early, block)
 
 
 def rows_of(core, own, other):
@@ -112,34 +110,25 @@
     return jnp.concatenate(pieces, axis=0)
 
 
-def down_kernel(own, other, *refs):
+def down_kernel(core, own, other, fourth, *refs):
     *blocks, out = refs
-    hidden = rows_of(1, own, other)
+    hidden = rows_of(core, own, other)
     for j in range(8):
-        out[j] = jnp.dot(hidden, blocks[j][688:], preferred_element_type=F32).astype(BF16)
-
-
-def down_added_kernel(own, other, added, *refs):
-    *blocks, out = refs
-    hidden = rows_of(0, own, other)
-    for j in range(8):
-        terms = jnp.dot(hidden, blocks[j][688:], preferred_element_type=F32)
-        terms = (terms + added[j].astype(F32)).astype(BF16)
+        weights = fourth[...] if j == 4 else blocks[j - (j > 4)][688:]
+        terms = jnp.dot(hidden, weights, preferred_element_type=F32).astype(out.dtype)
         for x in range(4):
             out[x, j] = terms[64 * x : 64 * x + 64]
 
 
-def down(own, other, blocks, *added):
-    shape = (4, 8, 64, 256) if added else (8, 256, 256)
+def down(core, dtype, own, other, fourth, blocks):
     return pl.pallas_call(
-        down_added_kernel if added else down_kernel,
-        out_shape=jax.ShapeDtypeStruct(shape, BF16),
-        in_specs=[VMEM] * (10 + len(added)),
-        out_specs=whole(shape) if added else VMEM,
+        functools.partial(down_kernel, core),
+        out_shape=jax.ShapeDtypeStruct((4, 8, 64, 256), dtype),
+        in_specs=[VMEM] * 10,
+        out_specs=VMEM,
         cost_estimate=pl.CostEstimate(flops=2 * 256 * 2048 * 344, bytes_accessed=3 << 20, transcendentals=0),
         compiler_params=pltpu.CompilerParams(vmem_limit_bytes=16 << 20),
-        name="down_added" if added else "down",
-    )(own, other, *added, *blocks)
+    )(own, other, fourth, *blocks)
 
 
 def one_hot(codes):
@@ -149,7 +138,7 @@
 def program(features, norm_gain, gate_weight, up_weight, down_weight, centroids, list_ids, live):
     yl = lax.axis_index("yl")
     z = lax.axis_index("z")
-    weights = ring(jnp.concatenate([gate_weight.T, up_weight.T, down_weight], axis=0))
+    weights, last_first, last_second = ring(jnp.concatenate([gate_weight.T, up_weight.T, down_weight], axis=0))
 
     code = jnp.where(live > 0, list_ids, -1).astype(BF16)
     code_block = jnp.broadcast_to(code[:, None], (8, 128))
@@ -165,13 +154,17 @@
     rows = both[..., :2048].reshape(2, 16, 2, 8, 2048)
     kept = rows[:, :, 0].reshape(256, 2048)
     away = rows[:, :, 1].reshape(256, 2048)
-    away_early, kept_early = early_product(away, weights), early_product(kept, weights)
-    away_part = swapped(last_product(away, away_early, weights, BF16), "yl")
-    both = last_product(kept, kept_early, weights, F32) + away_part.astype(F32)
+    away_early = early_product(away, weights)
+    away_part = last_product(away, away_early, last_first, BF16)
+    away_part = swapped(away_part, "yl")
+    kept_part = last_product(kept, early_product(kept, weights), last_first, F32)
+    both = kept_part + away_part.astype(F32)
     hidden = (jax.nn.silu(both[:, :344]) * both[:, 344:]).astype(BF16)
     other_hidden = swapped(hidden, "yl")
-    from_core = swapped(down(hidden, other_hidden, weights), "c")
-    terms = down(hidden, other_hidden, weights, from_core)
+    to_core = down(1, BF16, hidden, other_hidden, last_second, weights)
+    from_core = swapped(to_core, "c")
+    terms = down(0, F32, hidden, other_hidden, last_second, weights)
+    terms = (terms + from_core.astype(F32)).astype(BF16)
 
     mine, theirs, terms = lax.optimization_barrier((mine, theirs, terms))
     core = lax.axis_index("c")

time: 223 us -> 221 us (level)
  waiting for transfers between devices: 94.3 us -> 82.7 us
  starting transfers between devices: 74.3 us -> 80.2 us
  other arithmetic: 7.55 us -> 10.2 us
  blocking collectives: 26.6 us -> 29 us
    ppermute x6, waiting for transfers between devices: 12.8 us -> 4.85 us  [swapped(): return lax.ppermute(value, axis, SWAP)]
    ppermute x7 -> x8, starting transfers between devices: 31 us -> 36.4 us  [hop(): return lax.ppermute(value, 'z', pairs)]
    ppermute x7 -> x8, waiting for transfers between devices: 26.9 us -> 22.9 us  [hop(): return lax.ppermute(value, 'z', pairs)]
    convert_element_type x0 -> x1, other arithmetic: none -> 2.6 us  [program(): terms = (terms + from_core.astype(F32)).astype(BF16)]
  transfers between devices with their start and end apart: 17 -> 18, of which waited for: 12 -> 10; matrix products, arithmetic and copies ran while one was open for 2% -> 3% of each run, Pallas kernels for 2% -> 2%
where the time goes in v3:
time: 221 us; the launch traced here: 220 us
  waiting for transfers between devices  82.7 us (37%)
  starting transfers between devices  80.2 us (36%)
  blocking collectives  29 us (13%)
  other arithmetic  10.2 us (5%)
  local copies, waits for them, and re-layouts  9.35 us (4%)
  Pallas kernels  6.35 us (3%)
    ppermute x8, starting transfers between devices, hop(): return lax.ppermute(value, 'z', pairs)  36.4 us
    all_to_all x2, waiting for transfers between devices, to_everyone(): return lax.all_to_all(copies, axis, split_axis=0, concat_axis=0, tiled=True)  32.5 us
    ppermute x6, starting transfers between devices, swapped(): return lax.ppermute(value, axis, SWAP)  23.7 us
    ppermute x8, waiting for transfers between devices, hop(): return lax.ppermute(value, 'z', pairs)  22.9 us
    all_to_all x1, blocking collectives, program(): sums = lax.all_to_all(sums.reshape(32, 2, 384), LIST, 0, 0, tiled=True)  16.5 us
    all_to_all x2, starting transfers between devices, to_everyone(): return lax.all_to_all(copies, axis, split_axis=0, concat_axis=0, tiled=True)  13.1 us
    all_to_all x1, blocking collectives, program(): blocks = lax.all_to_all(blocks, SHARD, 0, 0, tiled=True).reshape(128, 384)  12.5 us
    all_to_all x1, waiting for transfers between devices, program(): terms = lax.all_to_all(terms, 'x', 0, 0, tiled=True)  12 us
  transfers between devices with their start and end apart: 18, of which 10 were waited for; matrix products, arithmetic and copies ran while one was open for 3% of the time, Pallas kernels for 2%

profile of v3, /device:TPU:1, one launch (start us, length us, event | category | flops | bytes accessed | tf_op | source)
XLA Modules:
  0.0 219.7 jit_solution(4587794100308001138)
XLA Ops:
  2.3 4.1 %collective-permute-start = (bf16[8,2176]{1,0:T(8,128)(2,1)S(1)}, bf16[8,2176]{1,0:T(8,128)(2,1)S(1)}, u32[]{:S(2)}, u32[]{:S(2)}) collective-permute-start(bf16[8,2176]{1,0:T(8,128)(2,1)S(1)} %pad_maximum_fusion.6), channel_id=1, source_target_pairs={{0,1},{1,0},{2,3},{3,2},{4,5},{5,4},{6,7},{7,6},{8,9},{9,8},{10,11... | collective-permute-start | bytes 104456 | tf_op jit(solution)/shard_map/ppermute | solution.py:19
  8.9 9.6 %all-to-all-start = ((bf16[16,16,2304]{2,1,0:T(8,128)(2,1)}), bf16[16,16,2304]{2,1,0:T(8,128)(2,1)}, u32[]{:S(2)}, u32[]{:S(2)}) async-start(bf16[16,16,2304]{2,1,0:T(8,128)(2,1)} %broadcast_in_dim.14), calls=%async_computation | async-start | bytes 2359296 | tf_op jit(solution)/shard_map/all_to_all | solution.py:24
  18.5 4.0 %collective-permute-start.2 = (bf16[1032,256]{1,0:T(8,128)(2,1)S(1)}, bf16[1032,256]{1,0:T(8,128)(2,1)S(1)}, u32[]{:S(2)}, u32[]{:S(2)}) collective-permute-start(bf16[1032,256]{1,0:T(8,128)(2,1)S(1)} %pad_maximum_fusion.1.refs_0_), channel_id=1, source_target_pairs={{0,2},{2,4},{4,6},{6,8},{8,10},{10,12},{12,14},{14,0},{1,3},{3,5},... | collective-permute-start | bytes 1585160 | tf_op jit(solution)/shard_map/ppermute | solution.py:51
  22.5 25.1 %all-to-all-done = bf16[16,16,2304]{2,1,0:T(8,128)(2,1)} async-done(((bf16[16,16,2304]{2,1,0:T(8,128)(2,1)}), bf16[16,16,2304]{2,1,0:T(8,128)(2,1)}, u32[]{:S(2)}, u32[]{:S(2)}) %all-to-all-start) | async-done | bytes 1179680 | tf_op jit(solution)/shard_map/all_to_all | solution.py:24
  47.7 6.2 %collective-permute-start.1 = (bf16[16,16,2304]{2,1,0:T(8,128)(2,1)}, bf16[16,16,2304]{2,1,0:T(8,128)(2,1)S(1)}, u32[]{:S(2)}, u32[]{:S(2)}) collective-permute-start(bf16[16,16,2304]{2,1,0:T(8,128)(2,1)} %all-to-all-done), channel_id=1, source_target_pairs={{0,16},{16,0},{1,17},{17,1},{2,18},{18,2},{3,19},{19,3},{4,20},{20... | collective-permute-start | bytes 3538952 | tf_op jit(solution)/shard_map/ppermute | solution.py:19
  53.8 10.7 %collective-permute-start.5 = (bf16[1032,256]{1,0:T(8,128)(2,1)S(1)}, bf16[1032,256]{1,0:T(8,128)(2,1)S(1)}, u32[]{:S(2)}, u32[]{:S(2)}) collective-permute-start(bf16[1032,256]{1,0:T(8,128)(2,1)S(1)} %pad_maximum_fusion.1.refs_0_), channel_id=1, source_target_pairs={{0,14},{2,0},{4,2},{6,4},{8,6},{10,8},{12,10},{14,12},{1,15},{3,1}... | collective-permute-start | bytes 1585160 | tf_op jit(solution)/shard_map/ppermute | solution.py:51
  64.5 1.9 collective-permute-start.3
  66.4 9.4 %collective-permute-done.5.refs_6_ = bf16[1032,256]{1,0:T(8,128)(2,1)S(1)} collective-permute-done((bf16[1032,256]{1,0:T(8,128)(2,1)S(1)}, bf16[1032,256]{1,0:T(8,128)(2,1)S(1)}, u32[]{:S(2)}, u32[]{:S(2)}) %collective-permute-start.5) | collective-permute-done | bytes 528416 | tf_op jit(solution)/shard_map/ppermute | solution.py:51
  75.8 5.3 %collective-permute-start.6 = (bf16[1032,256]{1,0:T(8,128)(2,1)S(1)}, bf16[1032,256]{1,0:T(8,128)(2,1)S(1)}, u32[]{:S(2)}, u32[]{:S(2)}) collective-permute-start(bf16[1032,256]{1,0:T(8,128)(2,1)S(1)} %collective-permute-done.5.refs_6_), channel_id=1, source_target_pairs={{0,14},{2,0},{4,2},{6,4},{8,6},{10,8},{12,10},{14,12},{1,15},{3,1}... | collective-permute-start | bytes 1585160 | tf_op jit(solution)/shard_map/ppermute | solution.py:51
  81.2 1.9 collective-permute-start.4
  83.1 8.5 %collective-permute-done.6.refs_5_ = bf16[1032,256]{1,0:T(8,128)(2,1)S(1)} collective-permute-done((bf16[1032,256]{1,0:T(8,128)(2,1)S(1)}, bf16[1032,256]{1,0:T(8,128)(2,1)S(1)}, u32[]{:S(2)}, u32[]{:S(2)}) %collective-permute-start.6) | collective-permute-done | bytes 528416 | tf_op jit(solution)/shard_map/ppermute | solution.py:51
  91.6 5.3 %collective-permute-start.7 = (bf16[1032,256]{1,0:T(8,128)(2,1)S(1)}, bf16[1032,256]{1,0:T(8,128)(2,1)S(1)}, u32[]{:S(2)}, u32[]{:S(2)}) collective-permute-start(bf16[1032,256]{1,0:T(8,128)(2,1)S(1)} %collective-permute-done.6.refs_5_), channel_id=1, source_target_pairs={{0,14},{2,0},{4,2},{6,4},{8,6},{10,8},{12,10},{14,12},{1,15},{3,1}... | collective-permute-start | bytes 1585160 | tf_op jit(solution)/shard_map/ppermute | solution.py:51
  97.0 1.9 collective-permute-start.8
  101.6 5.0 %collective-permute-done.7.refs_4_ = bf16[1032,256]{1,0:T(8,128)(2,1)S(1)} collective-permute-done((bf16[1032,256]{1,0:T(8,128)(2,1)S(1)}, bf16[1032,256]{1,0:T(8,128)(2,1)S(1)}, u32[]{:S(2)}, u32[]{:S(2)}) %collective-permute-start.7) | collective-permute-done | bytes 528416 | tf_op jit(solution)/shard_map/ppermute | solution.py:51
  106.6 1.7 shard_map.97.early
  108.6 1.9 collective-permute-start.9
  110.5 5.3 %collective-permute-start.11 = (bf16[344,256]{1,0:T(8,128)(2,1)S(1)}, bf16[344,256]{1,0:T(8,128)(2,1)S(1)}, u32[]{:S(2)}, u32[]{:S(2)}) collective-permute-start(bf16[344,256]{1,0:T(8,128)(2,1)S(1)} %slice.86), channel_id=1, source_target_pairs={{0,14},{2,0},{4,2},{6,4},{8,6},{10,8},{12,10},{14,12},{1,15},{3,1}... | collective-permute-start | bytes 528392 | tf_op jit(solution)/shard_map/ppermute | solution.py:51
  115.8 1.7 shard_map.95.early
  118.8 2.6 %collective-permute-start.10 = (bf16[256,344]{1,0:T(8,128)(2,1)S(1)}, bf16[256,344]{1,0:T(8,128)(2,1)S(1)}, u32[]{:S(2)}, u32[]{:S(2)}) collective-permute-start(bf16[256,344]{1,0:T(8,128)(2,1)S(1)} %fusion.1.own), channel_id=1, source_target_pairs={{0,1},{1,0},{2,3},{3,2},{4,5},{5,4},{6,7},{7,6},{8,9},{9,8},{10,11... | collective-permute-start | bytes 528392 | tf_op jit(solution)/shard_map/ppermute | solution.py:19
  121.5 3.8 %collective-permute-done.10.other = bf16[256,344]{1,0:T(8,128)(2,1)S(1)} collective-permute-done((bf16[256,344]{1,0:T(8,128)(2,1)S(1)}, bf16[256,344]{1,0:T(8,128)(2,1)S(1)}, u32[]{:S(2)}, u32[]{:S(2)}) %collective-permute-start.10) | collective-permute-done | bytes 176160 | tf_op jit(solution)/shard_map/ppermute | solution.py:19
  125.2 1.7 shard_map.100
  126.9 6.5 %collective-permute-start.12 = (bf16[4,8,64,256]{3,2,1,0:T(8,128)(2,1)}, bf16[4,8,64,256]{3,2,1,0:T(8,128)(2,1)}, u32[]{:S(2)}, u32[]{:S(2)}) collective-permute-start(bf16[4,8,64,256]{3,2,1,0:T(8,128)(2,1)} %shard_map.100), channel_id=1, source_target_pairs={{0,16},{16,0},{1,17},{17,1},{2,18},{18,2},{3,19},{19,3},{4,20},{20... | collective-permute-start | bytes 3145736 | tf_op jit(solution)/shard_map/ppermute | solution.py:19
  137.5 2.6 %add_convert_fusion = bf16[4,8,64,256]{3,2,1,0:T(8,128)(2,1)} fusion(f32[4,8,64,256]{3,2,1,0:T(8,128)S(1)} %shard_map.99, bf16[4,8,64,256]{3,2,1,0:T(8,128)(2,1)} %collective-permute-done.12), kind=kLoop, calls=%fused_computation.4 | loop fusion | flops 1572864 | bytes 4194304 | tf_op jit(solution)/shard_map/convert_element_type | solution.py:167
  142.6 3.5 %all-to-all-start.1 = ((bf16[4,8,64,256]{3,2,1,0:T(8,128)(2,1)}), bf16[4,8,64,256]{3,2,1,0:T(8,128)(2,1)S(1)}, u32[]{:S(2)}, u32[]{:S(2)}) async-start(bf16[4,8,64,256]{3,2,1,0:T(8,128)(2,1)} %add_convert_fusion), calls=%async_computation.1 | async-start | bytes 2097152 | tf_op jit(solution)/shard_map/all_to_all | solution.py:178
  146.7 2.3 %collective-permute-start.13 = (bf16[8,2048]{1,0:T(8,128)(2,1)S(1)}, bf16[8,2048]{1,0:T(8,128)(2,1)S(1)}, u32[]{:S(2)}, u32[]{:S(2)}) collective-permute-start(bf16[8,2048]{1,0:T(8,128)(2,1)S(1)} %convolution_convert_fusion), channel_id=1, source_target_pairs={{0,1},{1,0},{2,3},{3,2},{4,5},{5,4},{6,7},{7,6},{8,9},{9,8},{10,11... | collective-permute-start | bytes 98312 | tf_op jit(solution)/shard_map/ppermute | solution.py:19
  149.3 12.0 %all-to-all-done.1 = bf16[4,8,64,256]{3,2,1,0:T(8,128)(2,1)S(1)} async-done(((bf16[4,8,64,256]{3,2,1,0:T(8,128)(2,1)}), bf16[4,8,64,256]{3,2,1,0:T(8,128)(2,1)S(1)}, u32[]{:S(2)}, u32[]{:S(2)}) %all-to-all-start.1) | async-done | bytes 1048608 | tf_op jit(solution)/shard_map/all_to_all | solution.py:178
  162.3 3.5 %all-to-all-start.2 = ((bf16[8,8,8,256]{3,2,1,0:T(8,128)(2,1)}), bf16[8,8,8,256]{3,2,1,0:T(8,128)(2,1)S(1)}, u32[]{:S(2)}, u32[]{:S(2)}) async-start(bf16[8,8,8,256]{3,2,1,0:T(8,128)(2,1)} %bitcast.15), calls=%async_computation.2 | async-start | bytes 524288 | tf_op jit(solution)/shard_map/all_to_all | solution.py:182
  165.9 10.5 %all-to-all-done.2 = bf16[8,8,8,256]{3,2,1,0:T(8,128)(2,1)S(1)} async-done(((bf16[8,8,8,256]{3,2,1,0:T(8,128)(2,1)}), bf16[8,8,8,256]{3,2,1,0:T(8,128)(2,1)S(1)}, u32[]{:S(2)}, u32[]{:S(2)}) %all-to-all-start.2) | async-done | bytes 262176 | tf_op jit(solution)/shard_map/all_to_all | solution.py:182
  177.7 12.5 %all_to_all.30 = bf16[16,8,384]{2,1,0:T(8,128)(2,1)S(1)} all-to-all(bf16[16,8,384]{2,1,0:T(8,128)(2,1)S(1)} %pad_maximum_fusion.3), channel_id=1, replica_groups=mesh['yh'=4,'x'=4,'c'=2,'z'=8,'yl'=2] {'z','yl'}, dimensions={0} | all-to-all | bytes 196608 | tf_op jit(solution)/shard_map/all_to_all | solution.py:194
  190.9 16.5 %all_to_all.31 = bf16[32,2,384]{2,1,0:T(2,128)(2,1)S(1)} all-to-all(bf16[32,2,384]{2,1,0:T(2,128)(2,1)S(1)} %reshape.97), channel_id=1, replica_groups=mesh['yh'=4,'x'=4,'c'=2,'z'=8,'yl'=2] {'yh','x','c'}, dimensions={0} | all-to-all | bytes 98304 | tf_op jit(solution)/shard_map/all_to_all | solution.py:199
  208.1 3.5 %all-to-all-start.5 = ((f32[16,2,256]{2,1,0:T(2,128)}), f32[16,2,256]{2,1,0:T(2,128)S(1)}, u32[]{:S(2)}, u32[]{:S(2)}) async-start(f32[16,2,256]{2,1,0:T(2,128)} %broadcast_in_dim.16), calls=%async_computation.5 | async-start | bytes 65536 | tf_op jit(solution)/shard_map/all_to_all | solution.py:24
  211.7 7.4 %all-to-all-done.5 = f32[16,2,256]{2,1,0:T(2,128)S(1)} async-done(((f32[16,2,256]{2,1,0:T(2,128)}), f32[16,2,256]{2,1,0:T(2,128)S(1)}, u32[]{:S(2)}, u32[]{:S(2)}) %all-to-all-start.5) | async-done | bytes 32800 | tf_op jit(solution)/shard_map/all_to_all | solution.py:24
  (103 shorter events, 20.0 us)
Async XLA Ops:
  2.2 16.3 %copy-start.6 = (bf16[344,256]{1,0:T(8,128)(2,1)S(1)}, bf16[344,256]{1,0:T(8,128)(2,1)}, u32[]{:S(2)}) copy-start(bf16[344,256]{1,0:T(8,128)(2,1)} %param.12) | copy-start | bytes 528388
  2.2 16.3 %copy-start.7 = (bf16[256,344]{0,1:T(8,128)(2,1)S(1)}, bf16[256,344]{0,1:T(8,128)(2,1)}, u32[]{:S(2)}) copy-start(bf16[256,344]{0,1:T(8,128)(2,1)} %param.11) | copy-start | bytes 528388
  2.2 16.3 %copy-start.8 = (bf16[256,344]{0,1:T(8,128)(2,1)S(1)}, bf16[256,344]{0,1:T(8,128)(2,1)}, u32[]{:S(2)}) copy-start(bf16[256,344]{0,1:T(8,128)(2,1)} %param.10) | copy-start | bytes 528388
  2.3 5.5 %collective-permute-start = (bf16[8,2176]{1,0:T(8,128)(2,1)S(1)}, bf16[8,2176]{1,0:T(8,128)(2,1)S(1)}, u32[]{:S(2)}, u32[]{:S(2)}) collective-permute-start(bf16[8,2176]{1,0:T(8,128)(2,1)S(1)} %pad_maximum_fusion.6), channel_id=1, source_target_pairs={{0,1},{1,0},{2,3},{3,2},{4,5},{5,4},{6,7},{7,6},{8,9},{9,8},{10,11... | collective-permute-start | bytes 104456 | tf_op jit(solution)/shard_map/ppermute | solution.py:19
  7.7 10.7 %copy-start.10 = (bf16[8,2176]{1,0:T(8,128)(2,1)}, bf16[8,2176]{1,0:T(8,128)(2,1)S(1)}, u32[]{:S(2)}) copy-start(bf16[8,2176]{1,0:T(8,128)(2,1)S(1)} %collective-permute-done) | copy-start | bytes 104452
  8.9 38.8 %all-to-all-start = ((bf16[16,16,2304]{2,1,0:T(8,128)(2,1)}), bf16[16,16,2304]{2,1,0:T(8,128)(2,1)}, u32[]{:S(2)}, u32[]{:S(2)}) async-start(bf16[16,16,2304]{2,1,0:T(8,128)(2,1)} %broadcast_in_dim.14), calls=%async_computation | async-start | bytes 2359296 | tf_op jit(solution)/shard_map/all_to_all | solution.py:24
  18.5 46.0 %collective-permute-start.2 = (bf16[1032,256]{1,0:T(8,128)(2,1)S(1)}, bf16[1032,256]{1,0:T(8,128)(2,1)S(1)}, u32[]{:S(2)}, u32[]{:S(2)}) collective-permute-start(bf16[1032,256]{1,0:T(8,128)(2,1)S(1)} %pad_maximum_fusion.1.refs_0_), channel_id=1, source_target_pairs={{0,2},{2,4},{4,6},{6,8},{8,10},{10,12},{12,14},{14,0},{1,3},{3,5},... | collective-permute-start | bytes 1585160 | tf_op jit(solution)/shard_map/ppermute | solution.py:51
  47.7 51.3 %collective-permute-start.1 = (bf16[16,16,2304]{2,1,0:T(8,128)(2,1)}, bf16[16,16,2304]{2,1,0:T(8,128)(2,1)S(1)}, u32[]{:S(2)}, u32[]{:S(2)}) collective-permute-start(bf16[16,16,2304]{2,1,0:T(8,128)(2,1)} %all-to-all-done), channel_id=1, source_target_pairs={{0,16},{16,0},{1,17},{17,1},{2,18},{18,2},{3,19},{19,3},{4,20},{20... | collective-permute-start | bytes 3538952 | tf_op jit(solution)/shard_map/ppermute | solution.py:19
  53.8 22.0 %collective-permute-start.5 = (bf16[1032,256]{1,0:T(8,128)(2,1)S(1)}, bf16[1032,256]{1,0:T(8,128)(2,1)S(1)}, u32[]{:S(2)}, u32[]{:S(2)}) collective-permute-start(bf16[1032,256]{1,0:T(8,128)(2,1)S(1)} %pad_maximum_fusion.1.refs_0_), channel_id=1, source_target_pairs={{0,14},{2,0},{4,2},{6,4},{8,6},{10,8},{12,10},{14,12},{1,15},{3,1}... | collective-permute-start | bytes 1585160 | tf_op jit(solution)/shard_map/ppermute | solution.py:51
  64.5 16.6 %collective-permute-start.3 = (bf16[1032,256]{1,0:T(8,128)(2,1)S(1)}, bf16[1032,256]{1,0:T(8,128)(2,1)S(1)}, u32[]{:S(2)}, u32[]{:S(2)}) collective-permute-start(bf16[1032,256]{1,0:T(8,128)(2,1)S(1)} %collective-permute-done.2.refs_1_), channel_id=1, source_target_pairs={{0,2},{2,4},{4,6},{6,8},{8,10},{10,12},{12,14},{14,0},{1,3},{3,5},... | collective-permute-start | bytes 1585160 | tf_op jit(solution)/shard_map/ppermute | solution.py:51
  75.8 15.8 %collective-permute-start.6 = (bf16[1032,256]{1,0:T(8,128)(2,1)S(1)}, bf16[1032,256]{1,0:T(8,128)(2,1)S(1)}, u32[]{:S(2)}, u32[]{:S(2)}) collective-permute-start(bf16[1032,256]{1,0:T(8,128)(2,1)S(1)} %collective-permute-done.5.refs_6_), channel_id=1, source_target_pairs={{0,14},{2,0},{4,2},{6,4},{8,6},{10,8},{12,10},{14,12},{1,15},{3,1}... | collective-permute-start | bytes 1585160 | tf_op jit(solution)/shard_map/ppermute | solution.py:51
  81.2 15.8 %collective-permute-start.4 = (bf16[1032,256]{1,0:T(8,128)(2,1)S(1)}, bf16[1032,256]{1,0:T(8,128)(2,1)S(1)}, u32[]{:S(2)}, u32[]{:S(2)}) collective-permute-start(bf16[1032,256]{1,0:T(8,128)(2,1)S(1)} %collective-permute-done.3.refs_2_), channel_id=1, source_target_pairs={{0,2},{2,4},{4,6},{6,8},{8,10},{10,12},{12,14},{14,0},{1,3},{3,5},... | collective-permute-start | bytes 1585160 | tf_op jit(solution)/shard_map/ppermute | solution.py:51
  91.6 33.6 %copy-start = (bf16[1032,256]{1,0:T(8,128)(2,1)}, bf16[1032,256]{1,0:T(8,128)(2,1)S(1)}, u32[]{:S(2)}) copy-start(bf16[1032,256]{1,0:T(8,128)(2,1)S(1)} %collective-permute-done.6.refs_5_) | copy-start | bytes 1585156
  91.6 14.9 %collective-permute-start.7 = (bf16[1032,256]{1,0:T(8,128)(2,1)S(1)}, bf16[1032,256]{1,0:T(8,128)(2,1)S(1)}, u32[]{:S(2)}, u32[]{:S(2)}) collective-permute-start(bf16[1032,256]{1,0:T(8,128)(2,1)S(1)} %collective-permute-done.6.refs_5_), channel_id=1, source_target_pairs={{0,14},{2,0},{4,2},{6,4},{8,6},{10,8},{12,10},{14,12},{1,15},{3,1}... | collective-permute-start | bytes 1585160 | tf_op jit(solution)/shard_map/ppermute | solution.py:51
  97.0 11.2 %collective-permute-start.8 = (bf16[688,256]{1,0:T(8,128)(2,1)S(1)}, bf16[688,256]{1,0:T(8,128)(2,1)S(1)}, u32[]{:S(2)}, u32[]{:S(2)}) collective-permute-start(bf16[688,256]{1,0:T(8,128)(2,1)S(1)} %slice.82), channel_id=1, source_target_pairs={{0,2},{2,4},{4,6},{6,8},{8,10},{10,12},{12,14},{14,0},{1,3},{3,5},... | collective-permute-start | bytes 1056776 | tf_op jit(solution)/shard_map/ppermute | solution.py:51
  98.9 1.0 copy-start.4
  108.6 10.0 %collective-permute-start.9 = (bf16[256,688]{1,0:T(8,128)(2,1)S(1)}, bf16[256,688]{1,0:T(8,128)(2,1)S(1)}, u32[]{:S(2)}, u32[]{:S(2)}) collective-permute-start(bf16[256,688]{1,0:T(8,128)(2,1)S(1)} %shard_map.98), channel_id=1, source_target_pairs={{0,1},{1,0},{2,3},{3,2},{4,5},{5,4},{6,7},{7,6},{8,9},{9,8},{10,11... | collective-permute-start | bytes 1056776 | tf_op jit(solution)/shard_map/ppermute | solution.py:19
  110.5 11.0 %collective-permute-start.11 = (bf16[344,256]{1,0:T(8,128)(2,1)S(1)}, bf16[344,256]{1,0:T(8,128)(2,1)S(1)}, u32[]{:S(2)}, u32[]{:S(2)}) collective-permute-start(bf16[344,256]{1,0:T(8,128)(2,1)S(1)} %slice.86), channel_id=1, source_target_pairs={{0,14},{2,0},{4,2},{6,4},{8,6},{10,8},{12,10},{14,12},{1,15},{3,1}... | collective-permute-start | bytes 528392 | tf_op jit(solution)/shard_map/ppermute | solution.py:51
  118.8 14.6 %copy-start.13 = (s32[8]{0:T(128)S(1)}, s32[8]{0:T(128)}, u32[]{:S(2)}) copy-start(s32[8]{0:T(128)} %param.15) | copy-start | bytes 100
  118.8 6.4 %collective-permute-start.10 = (bf16[256,344]{1,0:T(8,128)(2,1)S(1)}, bf16[256,344]{1,0:T(8,128)(2,1)S(1)}, u32[]{:S(2)}, u32[]{:S(2)}) collective-permute-start(bf16[256,344]{1,0:T(8,128)(2,1)S(1)} %fusion.1.own), channel_id=1, source_target_pairs={{0,1},{1,0},{2,3},{3,2},{4,5},{5,4},{6,7},{7,6},{8,9},{9,8},{10,11... | collective-permute-start | bytes 528392 | tf_op jit(solution)/shard_map/ppermute | solution.py:19
  125.2 1.7 copy-start.2
  126.9 10.5 %collective-permute-start.12 = (bf16[4,8,64,256]{3,2,1,0:T(8,128)(2,1)}, bf16[4,8,64,256]{3,2,1,0:T(8,128)(2,1)}, u32[]{:S(2)}, u32[]{:S(2)}) collective-permute-start(bf16[4,8,64,256]{3,2,1,0:T(8,128)(2,1)} %shard_map.100), channel_id=1, source_target_pairs={{0,16},{16,0},{1,17},{17,1},{2,18},{18,2},{3,19},{19,3},{4,20},{20... | collective-permute-start | bytes 3145736 | tf_op jit(solution)/shard_map/ppermute | solution.py:19
  134.8 1.0 copy-start.1
  135.8 0.9 copy-start.3
  142.6 18.7 %all-to-all-start.1 = ((bf16[4,8,64,256]{3,2,1,0:T(8,128)(2,1)}), bf16[4,8,64,256]{3,2,1,0:T(8,128)(2,1)S(1)}, u32[]{:S(2)}, u32[]{:S(2)}) async-start(bf16[4,8,64,256]{3,2,1,0:T(8,128)(2,1)} %add_convert_fusion), calls=%async_computation.1 | async-start | bytes 2097152 | tf_op jit(solution)/shard_map/all_to_all | solution.py:178
  146.7 19.1 %collective-permute-start.13 = (bf16[8,2048]{1,0:T(8,128)(2,1)S(1)}, bf16[8,2048]{1,0:T(8,128)(2,1)S(1)}, u32[]{:S(2)}, u32[]{:S(2)}) collective-permute-start(bf16[8,2048]{1,0:T(8,128)(2,1)S(1)} %convolution_convert_fusion), channel_id=1, source_target_pairs={{0,1},{1,0},{2,3},{3,2},{4,5},{5,4},{6,7},{7,6},{8,9},{9,8},{10,11... | collective-permute-start | bytes 98312 | tf_op jit(solution)/shard_map/ppermute | solution.py:19
  161.5 15.2 %copy-start.5 = (bf16[8,4096]{1,0:T(8,128)(2,1)S(1)}, bf16[8,4096]{1,0:T(8,128)(2,1)}, u32[]{:S(2)}) copy-start(bf16[8,4096]{1,0:T(8,128)(2,1)} %param.8) | copy-start | bytes 196612
  161.5 15.4 %copy-start.11 = (f32[4096]{0:T(1024)S(1)}, f32[4096]{0:T(1024)}, u32[]{:S(2)}) copy-start(f32[4096]{0:T(1024)} %param.9) | copy-start | bytes 49156
  161.5 15.4 %copy-start.12 = (f32[8]{0:T(128)S(1)}, f32[8]{0:T(128)}, u32[]{:S(2)}) copy-start(f32[8]{0:T(128)} %compare_convert_fusion.1) | copy-start | bytes 100
  162.3 56.8 %copy-start.9 = (f32[2,4096]{1,0:T(2,128)S(1)}, f32[2,4096]{1,0:T(2,128)}, u32[]{:S(2)}) copy-start(f32[2,4096]{1,0:T(2,128)} %param.13) | copy-start | bytes 98308
  162.3 14.1 %all-to-all-start.2 = ((bf16[8,8,8,256]{3,2,1,0:T(8,128)(2,1)}), bf16[8,8,8,256]{3,2,1,0:T(8,128)(2,1)S(1)}, u32[]{:S(2)}, u32[]{:S(2)}) async-start(bf16[8,8,8,256]{3,2,1,0:T(8,128)(2,1)} %bitcast.15), calls=%async_computation.2 | async-start | bytes 524288 | tf_op jit(solution)/shard_map/all_to_all | solution.py:182
  208.1 11.0 %all-to-all-start.5 = ((f32[16,2,256]{2,1,0:T(2,128)}), f32[16,2,256]{2,1,0:T(2,128)S(1)}, u32[]{:S(2)}, u32[]{:S(2)}) async-start(f32[16,2,256]{2,1,0:T(2,128)} %broadcast_in_dim.16), calls=%async_computation.5 | async-start | bytes 65536 | tf_op jit(solution)/shard_map/all_to_all | solution.py:24

commit v4 on v3

--- a/solution.py
+++ b/solution.py
@@ -63,18 +63,18 @@
 EARLY = (0, 1, 2, 3, 5, 6, 7)
 
 
-def early_kernel(rows, *refs):
+def early_kernel(half, rows, *refs):
     *blocks, out = refs
-    for start in range(0, 256, 128):
-        total = 0.0
-        for j, block in zip(EARLY, blocks):
-            x = rows[start : start + 128, 256 * j : 256 * j + 256]
-            total += times(x, block[:688])
-        out[start : start + 128] = total
-
-
-def last_kernel(rows, early, block, out):
-    out[...] = (early[...] + times(rows[:, 1024:1280], block[...])).astype(out.dtype)
+    total = 0.0
+    for j, block in zip(EARLY, blocks):
+        total += times(rows[half, :, 256 * j : 256 * j + 256], block[:688])
+    out[...] = total
+
+
+def last_kernel(half, mine, theirs, early_mine, early_theirs, block, out):
+    for start, rows, early in ((0, mine, early_mine), (128, theirs, early_theirs)):
+        total = early[...] + times(rows[half, :, 1024:1280], block[...])
+        out[start : start + 128] = total.astype(out.dtype)
 
 
 def times(a, b):
@@ -84,23 +84,25 @@
 VMEM = pl.BlockSpec(memory_space=pltpu.VMEM)
 
 
-def product(kernel, dtype, depth, *operands):
+def product(kernel, count, dtype, depth, *operands):
     return pl.pallas_call(
         kernel,
-        out_shape=jax.ShapeDtypeStruct((256, 688), dtype),
+        out_shape=jax.ShapeDtypeStruct((count, 688), dtype),
         in_specs=[VMEM] * len(operands),
         out_specs=VMEM,
-        cost_estimate=pl.CostEstimate(flops=2 * 256 * depth * 688, bytes_accessed=2048 * depth, transcendentals=0),
+        cost_estimate=pl.CostEstimate(flops=2 * count * depth * 688, bytes_accessed=2048 * depth, transcendentals=0),
         compiler_params=pltpu.CompilerParams(vmem_limit_bytes=16 << 20),
     )(*operands)
 
 
-def early_product(rows, blocks):
-    return product(early_kernel, F32, 1792, rows, *blocks)
-
-
-def last_product(rows, early, block, dtype):
-    return product(last_kernel, dtype, 256, rows, early, block)
+def early_product(half, rows, blocks):
+    kernel = functools.partial(early_kernel, half)
+    return product(kernel, 128, F32, 1792, rows, *blocks)
+
+
+def last_product(half, dtype, *operands):
+    kernel = functools.partial(last_kernel, half)
+    return product(kernel, 256, dtype, 256, *operands)
 
 
 def rows_of(core, own, other):
@@ -148,16 +150,16 @@
     other_code = received[:, 2048]
     table, _ = by_class(centroids.astype(BF16), yl)
     sent = jnp.concatenate([x, table.reshape(16, 256)], axis=1)
-    mine = to_everyone(sent, ROWS)
+    copies = jnp.broadcast_to(sent.reshape(2, 1, 8, 2304), (2, 16, 8, 2304))
+    mine = lax.all_to_all(copies, ROWS, 1, 1, tiled=True).reshape(2, 128, 2304)
     theirs = swapped(mine, "c")
-    both = jnp.stack([mine, theirs])
-    rows = both[..., :2048].reshape(2, 16, 2, 8, 2048)
-    kept = rows[:, :, 0].reshape(256, 2048)
-    away = rows[:, :, 1].reshape(256, 2048)
-    away_early = early_product(away, weights)
-    away_part = last_product(away, away_early, last_first, BF16)
+
+    early_mine = early_product(1, mine, weights)
+    early_theirs = early_product(1, theirs, weights)
+    away_part = last_product(1, BF16, mine, theirs, early_mine, early_theirs, last_first)
     away_part = swapped(away_part, "yl")
-    kept_part = last_product(kept, early_product(kept, weights), last_first, F32)
+    early_mine, early_theirs = early_product(0, mine, weights), early_product(0, theirs, weights)
+    kept_part = last_product(0, F32, mine, theirs, early_mine, early_theirs, last_first)
     both = kept_part + away_part.astype(F32)
     hidden = (jax.nn.silu(both[:, :344]) * both[:, 344:]).astype(BF16)
     other_hidden = swapped(hidden, "yl")
@@ -168,9 +170,9 @@
 
     mine, theirs, terms = lax.optimization_barrier((mine, theirs, terms))
     core = lax.axis_index("c")
-    lists = jnp.stack([mine[..., 2048:], theirs[..., 2048:]]).reshape(2, 4, 4, 2, 2048)
+    lists = jnp.stack([mine[..., 2048:], theirs[..., 2048:]]).reshape(2, 2, 4, 4, 2048)
     lists = jnp.where(core == 0, lists, lists[::-1])
-    lists = lists.transpose(2, 1, 0, 3, 4).reshape(64, 2048)
+    lists = lists.transpose(3, 2, 0, 1, 4).reshape(64, 2048)
     picked = jnp.dot(one_hot(code), lists, preferred_element_type=F32).astype(BF16)
     other_picked = jnp.dot(one_hot(other_code), lists, preferred_element_type=F32).astype(BF16)
     coarse = interleaved(picked, swapped(other_picked, "yl"), yl)

time: 221 us -> 212 us (0.959)
  waiting for transfers between devices: 82.7 us -> 63 us
  Pallas kernels: 6.35 us -> 13.2 us
  starting transfers between devices: 80.2 us -> 84.2 us
  other arithmetic: 10.2 us -> 7.92 us
    all_to_all x2 -> x1, waiting for transfers between devices: 32.5 us -> 7.36 us  [to_everyone(): return lax.all_to_all(copies, axis, split_axis=0, concat_axis=0, tiled=True)]
    all_to_all x0 -> x1, starting transfers between devices: none -> 9.72 us  [program(): mine = lax.all_to_all(copies, ROWS, 1, 1, tiled=True).reshape(2, 128, 2304)]
    all_to_all x2 -> x1, starting transfers between devices: 13.1 us -> 3.5 us  [to_everyone(): return lax.all_to_all(copies, axis, split_axis=0, concat_axis=0, tiled=True)]
    all_to_all x0 -> x1, waiting for transfers between devices: none -> 6.16 us  [program(): mine = lax.all_to_all(copies, ROWS, 1, 1, tiled=True).reshape(2, 128, 2304)]
    pallas_call x4 -> x6, Pallas kernels: 3.94 us -> 8.63 us  [product(): pl.pallas_call(kernel, out_shape=jax.ShapeDtypeStruct((count, 688), dtype...]
    ppermute x8, starting transfers between devices: 36.4 us -> 39.6 us  [hop(): return lax.ppermute(value, 'z', pairs)]
    unnamed x29 -> x38, local copies, waits for them, and re-layouts: 3.04 us -> 5.96 us
    ppermute x8, waiting for transfers between devices: 22.9 us -> 25.6 us  [hop(): return lax.ppermute(value, 'z', pairs)]
  transfers between devices with their start and end apart: 18 -> 18, of which waited for: 10 -> 10; matrix products, arithmetic and copies ran while one was open for 3% -> 2% of each run, Pallas kernels for 2% -> 5%
where the time goes in v4:
time: 212 us; the launch traced here: 210 us
  starting transfers between devices  84.2 us (40%)
  waiting for transfers between devices  63 us (30%)
  blocking collectives  29.2 us (14%)
  Pallas kernels  13.2 us (6%)
  local copies, waits for them, and re-layouts  10.9 us (5%)
  other arithmetic  7.92 us (4%)
    ppermute x8, starting transfers between devices, hop(): return lax.ppermute(value, 'z', pairs)  39.6 us
    ppermute x8, waiting for transfers between devices, hop(): return lax.ppermute(value, 'z', pairs)  25.6 us
    ppermute x6, starting transfers between devices, swapped(): return lax.ppermute(value, axis, SWAP)  24.2 us
    all_to_all x1, blocking collectives, program(): sums = lax.all_to_all(sums.reshape(32, 2, 384), LIST, 0, 0, tiled=True)  16.5 us
    all_to_all x1, blocking collectives, program(): blocks = lax.all_to_all(blocks, SHARD, 0, 0, tiled=True).reshape(128, 384)  12.7 us
    all_to_all x1, waiting for transfers between devices, program(): terms = lax.all_to_all(terms, ('yh', 'yl'), 0, 0, tiled=True)  10.3 us
    all_to_all x1, waiting for transfers between devices, program(): terms = lax.all_to_all(terms, 'x', 0, 0, tiled=True)  10.2 us
    all_to_all x1, starting transfers between devices, program(): mine = lax.all_to_all(copies, ROWS, 1, 1, tiled=True).reshape(2, 128, 2304)  9.72 us
  transfers between devices with their start and end apart: 18, of which 10 were waited for; matrix products, arithmetic and copies ran while one was open for 2% of the time, Pallas kernels for 5%

profile of v4, /device:TPU:1, one launch (start us, length us, event | category | flops | bytes accessed | tf_op | source)
XLA Modules:
  0.0 210.3 jit_solution(582037314093740998)
XLA Ops:
  2.3 4.0 %collective-permute-start = (bf16[8,2176]{1,0:T(8,128)(2,1)S(1)}, bf16[8,2176]{1,0:T(8,128)(2,1)S(1)}, u32[]{:S(2)}, u32[]{:S(2)}) collective-permute-start(bf16[8,2176]{1,0:T(8,128)(2,1)S(1)} %pad_maximum_fusion.3), channel_id=1, source_target_pairs={{0,1},{1,0},{2,3},{3,2},{4,5},{5,4},{6,7},{7,6},{8,9},{9,8},{10,11... | collective-permute-start | bytes 104456 | tf_op jit(solution)/shard_map/ppermute | solution.py:19
  8.7 9.7 %all-to-all-start = ((bf16[2,16,8,2304]{3,2,0,1:T(8,128)(2,1)}), bf16[2,16,8,2304]{3,2,0,1:T(8,128)(2,1)}, u32[]{:S(2)}, u32[]{:S(2)}) async-start(bf16[2,16,8,2304]{3,2,0,1:T(8,128)(2,1)} %broadcast_in_dim.17), calls=%async_computation | async-start | bytes 2359296 | tf_op jit(solution)/shard_map/all_to_all | solution.py:154
  18.5 4.0 %collective-permute-start.2 = (bf16[1032,256]{1,0:T(8,128)(2,1)S(1)}, bf16[1032,256]{1,0:T(8,128)(2,1)S(1)}, u32[]{:S(2)}, u32[]{:S(2)}) collective-permute-start(bf16[1032,256]{1,0:T(8,128)(2,1)S(1)} %pad_maximum_fusion.refs_0_), channel_id=1, source_target_pairs={{0,2},{2,4},{4,6},{6,8},{8,10},{10,12},{12,14},{14,0},{1,3},{3,5},... | collective-permute-start | bytes 1585160 | tf_op jit(solution)/shard_map/ppermute | solution.py:51
  22.5 8.6 %collective-permute-start.5 = (bf16[1032,256]{1,0:T(8,128)(2,1)S(1)}, bf16[1032,256]{1,0:T(8,128)(2,1)S(1)}, u32[]{:S(2)}, u32[]{:S(2)}) collective-permute-start(bf16[1032,256]{1,0:T(8,128)(2,1)S(1)} %pad_maximum_fusion.refs_0_), channel_id=1, source_target_pairs={{0,14},{2,0},{4,2},{6,4},{8,6},{10,8},{12,10},{14,12},{1,15},{3,1}... | collective-permute-start | bytes 1585160 | tf_op jit(solution)/shard_map/ppermute | solution.py:51
  31.1 8.4 %collective-permute-done.2.refs_1_ = bf16[1032,256]{1,0:T(8,128)(2,1)S(1)} collective-permute-done((bf16[1032,256]{1,0:T(8,128)(2,1)S(1)}, bf16[1032,256]{1,0:T(8,128)(2,1)S(1)}, u32[]{:S(2)}, u32[]{:S(2)}) %collective-permute-start.2) | collective-permute-done | bytes 528416 | tf_op jit(solution)/shard_map/ppermute | solution.py:51
  39.6 1.9 collective-permute-start.3
  41.5 6.2 %all-to-all-done = bf16[2,16,8,2304]{3,2,0,1:T(8,128)(2,1)} async-done(((bf16[2,16,8,2304]{3,2,0,1:T(8,128)(2,1)}), bf16[2,16,8,2304]{3,2,0,1:T(8,128)(2,1)}, u32[]{:S(2)}, u32[]{:S(2)}) %all-to-all-start) | async-done | bytes 1179680 | tf_op jit(solution)/shard_map/all_to_all | solution.py:154
  49.0 6.2 %collective-permute-start.1 = (bf16[2,128,2304]{2,1,0:T(8,128)(2,1)S(1)}, bf16[2,128,2304]{2,1,0:T(8,128)(2,1)S(1)}, u32[]{:S(2)}, u32[]{:S(2)}) collective-permute-start(bf16[2,128,2304]{2,1,0:T(8,128)(2,1)S(1)} %bitcast.53), channel_id=1, source_target_pairs={{0,16},{16,0},{1,17},{17,1},{2,18},{18,2},{3,19},{19,3},{4,20},{20... | collective-permute-start | bytes 3538952 | tf_op jit(solution)/shard_map/ppermute | solution.py:19
  55.2 10.7 %collective-permute-start.6 = (bf16[1032,256]{1,0:T(8,128)(2,1)S(1)}, bf16[1032,256]{1,0:T(8,128)(2,1)S(1)}, u32[]{:S(2)}, u32[]{:S(2)}) collective-permute-start(bf16[1032,256]{1,0:T(8,128)(2,1)S(1)} %collective-permute-done.5.refs_6_), channel_id=1, source_target_pairs={{0,14},{2,0},{4,2},{6,4},{8,6},{10,8},{12,10},{14,12},{1,15},{3,1}... | collective-permute-start | bytes 1585160 | tf_op jit(solution)/shard_map/ppermute | solution.py:51
  66.7 1.9 collective-permute-start.4
  68.6 8.6 %collective-permute-done.6.refs_5_ = bf16[1032,256]{1,0:T(8,128)(2,1)S(1)} collective-permute-done((bf16[1032,256]{1,0:T(8,128)(2,1)S(1)}, bf16[1032,256]{1,0:T(8,128)(2,1)S(1)}, u32[]{:S(2)}, u32[]{:S(2)}) %collective-permute-start.6) | collective-permute-done | bytes 528416 | tf_op jit(solution)/shard_map/ppermute | solution.py:51
  77.2 5.3 %collective-permute-start.7 = (bf16[1032,256]{1,0:T(8,128)(2,1)S(1)}, bf16[1032,256]{1,0:T(8,128)(2,1)S(1)}, u32[]{:S(2)}, u32[]{:S(2)}) collective-permute-start(bf16[1032,256]{1,0:T(8,128)(2,1)S(1)} %collective-permute-done.6.refs_5_), channel_id=1, source_target_pairs={{0,14},{2,0},{4,2},{6,4},{8,6},{10,8},{12,10},{14,12},{1,15},{3,1}... | collective-permute-start | bytes 1585160 | tf_op jit(solution)/shard_map/ppermute | solution.py:51
  83.3 1.9 collective-permute-start.8
  85.2 7.8 %collective-permute-done.7.refs_4_ = bf16[1032,256]{1,0:T(8,128)(2,1)S(1)} collective-permute-done((bf16[1032,256]{1,0:T(8,128)(2,1)S(1)}, bf16[1032,256]{1,0:T(8,128)(2,1)S(1)}, u32[]{:S(2)}, u32[]{:S(2)}) %collective-permute-start.7) | collective-permute-done | bytes 528416 | tf_op jit(solution)/shard_map/ppermute | solution.py:51
  95.9 2.3 %shard_map.99.early_theirs = f32[128,688]{1,0:T(8,128)S(1)} custom-call(bf16[2,128,2304]{2,1,0:T(8,128)(2,1)S(1)} %collective-permute-done.1.rows.theirs, bf16[1032,256]{1,0:T(8,128)(2,1)S(1)} %pad_maximum_fusion.refs_0_, bf16[1032,256]{1,0:T(8,128)(2,1)S(1)} %collective-permute-done.2.refs_1_, bf16[1032,256]{1,0:T(8,128)(2,1)} %collective-permute-done.3.refs_2_, ...), custom_call_target="tpu_custom_call" | custom-call | flops 315621376 | bytes 3670016 | tf_op jit(solution)/shard_map/pallas_call | solution.py:88
  98.6 1.9 collective-permute-start.9
  100.5 5.3 %collective-permute-start.11 = (bf16[344,256]{1,0:T(8,128)(2,1)S(1)}, bf16[344,256]{1,0:T(8,128)(2,1)S(1)}, u32[]{:S(2)}, u32[]{:S(2)}) collective-permute-start(bf16[344,256]{1,0:T(8,128)(2,1)S(1)} %slice.72), channel_id=1, source_target_pairs={{0,14},{2,0},{4,2},{6,4},{8,6},{10,8},{12,10},{14,12},{1,15},{3,1}... | collective-permute-start | bytes 528392 | tf_op jit(solution)/shard_map/ppermute | solution.py:51
  107.8 1.9 shard_map.96.early_theirs
  110.3 3.4 %collective-permute-start.10 = (bf16[256,344]{1,0:T(8,128)(2,1)S(1)}, bf16[256,344]{1,0:T(8,128)(2,1)S(1)}, u32[]{:S(2)}, u32[]{:S(2)}) collective-permute-start(bf16[256,344]{1,0:T(8,128)(2,1)S(1)} %fusion.own), channel_id=1, source_target_pairs={{0,1},{1,0},{2,3},{3,2},{4,5},{5,4},{6,7},{7,6},{8,9},{9,8},{10,11... | collective-permute-start | bytes 528392 | tf_op jit(solution)/shard_map/ppermute | solution.py:19
  113.7 3.0 %collective-permute-done.10.other = bf16[256,344]{1,0:T(8,128)(2,1)S(1)} collective-permute-done((bf16[256,344]{1,0:T(8,128)(2,1)S(1)}, bf16[256,344]{1,0:T(8,128)(2,1)S(1)}, u32[]{:S(2)}, u32[]{:S(2)}) %collective-permute-start.10) | collective-permute-done | bytes 176160 | tf_op jit(solution)/shard_map/ppermute | solution.py:19
  116.7 2.8 %shard_map.102 = bf16[4,8,64,256]{3,2,1,0:T(8,128)(2,1)} custom-call(bf16[256,344]{1,0:T(8,128)(2,1)S(1)} %fusion.own, bf16[256,344]{1,0:T(8,128)(2,1)S(1)} %collective-permute-done.10.other, bf16[344,256]{1,0:T(8,128)(2,1)S(1)} %collective-permute-done.11.fourth, bf16[1032,256]{1,0:T(8,128)(2,1)S(1)} %pad_maximum_fusion.refs_0_, ...), custom_call_target="tpu_custom_call" | custom-call | flops 360710144 | bytes 3145728 | tf_op jit(solution)/shard_map/pallas_call | solution.py:126
  119.6 5.1 %collective-permute-start.12 = (bf16[4,8,64,256]{3,2,1,0:T(8,128)(2,1)}, bf16[4,8,64,256]{3,2,1,0:T(8,128)(2,1)}, u32[]{:S(2)}, u32[]{:S(2)}) collective-permute-start(bf16[4,8,64,256]{3,2,1,0:T(8,128)(2,1)} %shard_map.102), channel_id=1, source_target_pairs={{0,16},{16,0},{1,17},{17,1},{2,18},{18,2},{3,19},{19,3},{4,20},{20... | collective-permute-start | bytes 3145736 | tf_op jit(solution)/shard_map/ppermute | solution.py:19
  130.5 2.6 %add_convert_fusion = bf16[4,8,64,256]{3,2,1,0:T(8,128)(2,1)} fusion(f32[4,8,64,256]{3,2,1,0:T(8,128)S(1)} %shard_map.101, bf16[4,8,64,256]{3,2,1,0:T(8,128)(2,1)} %collective-permute-done.12), kind=kLoop, calls=%fused_computation.2 | loop fusion | flops 1572864 | bytes 4194304 | tf_op jit(solution)/shard_map/convert_element_type | solution.py:169
  133.1 3.6 %all-to-all-start.1 = ((bf16[4,8,64,256]{3,2,1,0:T(8,128)(2,1)}), bf16[4,8,64,256]{3,2,1,0:T(8,128)(2,1)S(1)}, u32[]{:S(2)}, u32[]{:S(2)}) async-start(bf16[4,8,64,256]{3,2,1,0:T(8,128)(2,1)} %add_convert_fusion), calls=%async_computation.1 | async-start | bytes 2097152 | tf_op jit(solution)/shard_map/all_to_all | solution.py:180
  137.9 3.6 %collective-permute-start.13 = (bf16[8,2048]{1,0:T(8,128)(2,1)S(1)}, bf16[8,2048]{1,0:T(8,128)(2,1)S(1)}, u32[]{:S(2)}, u32[]{:S(2)}) collective-permute-start(bf16[8,2048]{1,0:T(8,128)(2,1)S(1)} %convolution_convert_fusion), channel_id=1, source_target_pairs={{0,1},{1,0},{2,3},{3,2},{4,5},{5,4},{6,7},{7,6},{8,9},{9,8},{10,11... | collective-permute-start | bytes 98312 | tf_op jit(solution)/shard_map/ppermute | solution.py:19
  141.7 10.2 %all-to-all-done.1 = bf16[4,8,64,256]{3,2,1,0:T(8,128)(2,1)S(1)} async-done(((bf16[4,8,64,256]{3,2,1,0:T(8,128)(2,1)}), bf16[4,8,64,256]{3,2,1,0:T(8,128)(2,1)S(1)}, u32[]{:S(2)}, u32[]{:S(2)}) %all-to-all-start.1) | async-done | bytes 1048608 | tf_op jit(solution)/shard_map/all_to_all | solution.py:180
  152.9 3.6 %all-to-all-start.2 = ((bf16[8,8,8,256]{3,2,1,0:T(8,128)(2,1)}), bf16[8,8,8,256]{3,2,1,0:T(8,128)(2,1)S(1)}, u32[]{:S(2)}, u32[]{:S(2)}) async-start(bf16[8,8,8,256]{3,2,1,0:T(8,128)(2,1)} %bitcast.13), calls=%async_computation.2 | async-start | bytes 524288 | tf_op jit(solution)/shard_map/all_to_all | solution.py:184
  156.5 10.3 %all-to-all-done.2 = bf16[8,8,8,256]{3,2,1,0:T(8,128)(2,1)S(1)} async-done(((bf16[8,8,8,256]{3,2,1,0:T(8,128)(2,1)}), bf16[8,8,8,256]{3,2,1,0:T(8,128)(2,1)S(1)}, u32[]{:S(2)}, u32[]{:S(2)}) %all-to-all-start.2) | async-done | bytes 262176 | tf_op jit(solution)/shard_map/all_to_all | solution.py:184
  168.1 12.7 %all_to_all.30 = bf16[16,8,384]{2,1,0:T(8,128)(2,1)S(1)} all-to-all(bf16[16,8,384]{2,1,0:T(8,128)(2,1)S(1)} %pad_maximum_fusion.1), channel_id=1, replica_groups=mesh['yh'=4,'x'=4,'c'=2,'z'=8,'yl'=2] {'z','yl'}, dimensions={0} | all-to-all | bytes 196608 | tf_op jit(solution)/shard_map/all_to_all | solution.py:196
  181.5 16.5 %all_to_all.31 = bf16[32,2,384]{2,1,0:T(2,128)(2,1)S(1)} all-to-all(bf16[32,2,384]{2,1,0:T(2,128)(2,1)S(1)} %reshape.117), channel_id=1, replica_groups=mesh['yh'=4,'x'=4,'c'=2,'z'=8,'yl'=2] {'yh','x','c'}, dimensions={0} | all-to-all | bytes 98304 | tf_op jit(solution)/shard_map/all_to_all | solution.py:201
  198.6 3.5 %all-to-all-start.5 = ((f32[16,2,256]{2,1,0:T(2,128)}), f32[16,2,256]{2,1,0:T(2,128)S(1)}, u32[]{:S(2)}, u32[]{:S(2)}) async-start(f32[16,2,256]{2,1,0:T(2,128)} %broadcast_in_dim.19), calls=%async_computation.5 | async-start | bytes 65536 | tf_op jit(solution)/shard_map/all_to_all | solution.py:24
  202.3 7.4 %all-to-all-done.5 = f32[16,2,256]{2,1,0:T(2,128)S(1)} async-done(((f32[16,2,256]{2,1,0:T(2,128)}), f32[16,2,256]{2,1,0:T(2,128)S(1)}, u32[]{:S(2)}, u32[]{:S(2)}) %all-to-all-start.5) | async-done | bytes 32800 | tf_op jit(solution)/shard_map/all_to_all | solution.py:24
  (114 shorter events, 24.2 us)
Async XLA Ops:
  2.3 5.3 %collective-permute-start = (bf16[8,2176]{1,0:T(8,128)(2,1)S(1)}, bf16[8,2176]{1,0:T(8,128)(2,1)S(1)}, u32[]{:S(2)}, u32[]{:S(2)}) collective-permute-start(bf16[8,2176]{1,0:T(8,128)(2,1)S(1)} %pad_maximum_fusion.3), channel_id=1, source_target_pairs={{0,1},{1,0},{2,3},{3,2},{4,5},{5,4},{6,7},{7,6},{8,9},{9,8},{10,11... | collective-permute-start | bytes 104456 | tf_op jit(solution)/shard_map/ppermute | solution.py:19
  8.7 9.7 %copy-start.12 = (bf16[344,256]{1,0:T(8,128)(2,1)S(1)}, bf16[344,256]{1,0:T(8,128)(2,1)}, u32[]{:S(2)}) copy-start(bf16[344,256]{1,0:T(8,128)(2,1)} %param.12) | copy-start | bytes 528388
  8.7 9.7 %copy-start.13 = (bf16[256,344]{0,1:T(8,128)(2,1)S(1)}, bf16[256,344]{0,1:T(8,128)(2,1)}, u32[]{:S(2)}) copy-start(bf16[256,344]{0,1:T(8,128)(2,1)} %param.11) | copy-start | bytes 528388
  8.7 9.8 %copy-start.14 = (bf16[256,344]{0,1:T(8,128)(2,1)S(1)}, bf16[256,344]{0,1:T(8,128)(2,1)}, u32[]{:S(2)}) copy-start(bf16[256,344]{0,1:T(8,128)(2,1)} %param.10) | copy-start | bytes 528388
  8.7 38.9 %all-to-all-start = ((bf16[2,16,8,2304]{3,2,0,1:T(8,128)(2,1)}), bf16[2,16,8,2304]{3,2,0,1:T(8,128)(2,1)}, u32[]{:S(2)}, u32[]{:S(2)}) async-start(bf16[2,16,8,2304]{3,2,0,1:T(8,128)(2,1)} %broadcast_in_dim.17), calls=%async_computation | async-start | bytes 2359296 | tf_op jit(solution)/shard_map/all_to_all | solution.py:154
  18.5 21.0 %collective-permute-start.2 = (bf16[1032,256]{1,0:T(8,128)(2,1)S(1)}, bf16[1032,256]{1,0:T(8,128)(2,1)S(1)}, u32[]{:S(2)}, u32[]{:S(2)}) collective-permute-start(bf16[1032,256]{1,0:T(8,128)(2,1)S(1)} %pad_maximum_fusion.refs_0_), channel_id=1, source_target_pairs={{0,2},{2,4},{4,6},{6,8},{8,10},{10,12},{12,14},{14,0},{1,3},{3,5},... | collective-permute-start | bytes 1585160 | tf_op jit(solution)/shard_map/ppermute | solution.py:51
  22.5 32.7 %collective-permute-start.5 = (bf16[1032,256]{1,0:T(8,128)(2,1)S(1)}, bf16[1032,256]{1,0:T(8,128)(2,1)S(1)}, u32[]{:S(2)}, u32[]{:S(2)}) collective-permute-start(bf16[1032,256]{1,0:T(8,128)(2,1)S(1)} %pad_maximum_fusion.refs_0_), channel_id=1, source_target_pairs={{0,14},{2,0},{4,2},{6,4},{8,6},{10,8},{12,10},{14,12},{1,15},{3,1}... | collective-permute-start | bytes 1585160 | tf_op jit(solution)/shard_map/ppermute | solution.py:51
  39.6 27.1 %collective-permute-start.3 = (bf16[1032,256]{1,0:T(8,128)(2,1)S(1)}, bf16[1032,256]{1,0:T(8,128)(2,1)}, u32[]{:S(2)}, u32[]{:S(2)}) collective-permute-start(bf16[1032,256]{1,0:T(8,128)(2,1)S(1)} %collective-permute-done.2.refs_1_), channel_id=1, source_target_pairs={{0,2},{2,4},{4,6},{6,8},{8,10},{10,12},{12,14},{14,0},{1,3},{3,5},... | collective-permute-start | bytes 1585160 | tf_op jit(solution)/shard_map/ppermute | solution.py:51
  49.0 46.9 %collective-permute-start.1 = (bf16[2,128,2304]{2,1,0:T(8,128)(2,1)S(1)}, bf16[2,128,2304]{2,1,0:T(8,128)(2,1)S(1)}, u32[]{:S(2)}, u32[]{:S(2)}) collective-permute-start(bf16[2,128,2304]{2,1,0:T(8,128)(2,1)S(1)} %bitcast.53), channel_id=1, source_target_pairs={{0,16},{16,0},{1,17},{17,1},{2,18},{18,2},{3,19},{19,3},{4,20},{20... | collective-permute-start | bytes 3538952 | tf_op jit(solution)/shard_map/ppermute | solution.py:19
  55.2 22.0 %collective-permute-start.6 = (bf16[1032,256]{1,0:T(8,128)(2,1)S(1)}, bf16[1032,256]{1,0:T(8,128)(2,1)S(1)}, u32[]{:S(2)}, u32[]{:S(2)}) collective-permute-start(bf16[1032,256]{1,0:T(8,128)(2,1)S(1)} %collective-permute-done.5.refs_6_), channel_id=1, source_target_pairs={{0,14},{2,0},{4,2},{6,4},{8,6},{10,8},{12,10},{14,12},{1,15},{3,1}... | collective-permute-start | bytes 1585160 | tf_op jit(solution)/shard_map/ppermute | solution.py:51
  66.7 16.6 %collective-permute-start.4 = (bf16[1032,256]{1,0:T(8,128)(2,1)}, bf16[1032,256]{1,0:T(8,128)(2,1)S(1)}, u32[]{:S(2)}, u32[]{:S(2)}) collective-permute-start(bf16[1032,256]{1,0:T(8,128)(2,1)} %collective-permute-done.3.refs_2_), channel_id=1, source_target_pairs={{0,2},{2,4},{4,6},{6,8},{8,10},{10,12},{12,14},{14,0},{1,3},{3,5},... | collective-permute-start | bytes 1585160 | tf_op jit(solution)/shard_map/ppermute | solution.py:51
  77.2 39.5 %copy-start.5 = (bf16[1032,256]{1,0:T(8,128)(2,1)}, bf16[1032,256]{1,0:T(8,128)(2,1)S(1)}, u32[]{:S(2)}) copy-start(bf16[1032,256]{1,0:T(8,128)(2,1)S(1)} %collective-permute-done.6.refs_5_) | copy-start | bytes 1585156
  77.2 15.8 %collective-permute-start.7 = (bf16[1032,256]{1,0:T(8,128)(2,1)S(1)}, bf16[1032,256]{1,0:T(8,128)(2,1)S(1)}, u32[]{:S(2)}, u32[]{:S(2)}) collective-permute-start(bf16[1032,256]{1,0:T(8,128)(2,1)S(1)} %collective-permute-done.6.refs_5_), channel_id=1, source_target_pairs={{0,14},{2,0},{4,2},{6,4},{8,6},{10,8},{12,10},{14,12},{1,15},{3,1}... | collective-permute-start | bytes 1585160 | tf_op jit(solution)/shard_map/ppermute | solution.py:51
  83.3 14.9 %collective-permute-start.8 = (bf16[688,256]{1,0:T(8,128)(2,1)S(1)}, bf16[688,256]{1,0:T(8,128)(2,1)S(1)}, u32[]{:S(2)}, u32[]{:S(2)}) collective-permute-start(bf16[688,256]{1,0:T(8,128)(2,1)S(1)} %slice.69), channel_id=1, source_target_pairs={{0,2},{2,4},{4,6},{6,8},{8,10},{10,12},{12,14},{14,0},{1,3},{3,5},... | collective-permute-start | bytes 1056776 | tf_op jit(solution)/shard_map/ppermute | solution.py:51
  95.9 13.7 %copy-start = (bf16[2,128,2304]{2,1,0:T(8,128)(2,1)}, bf16[2,128,2304]{2,1,0:T(8,128)(2,1)S(1)}, u32[]{:S(2)}) copy-start(bf16[2,128,2304]{2,1,0:T(8,128)(2,1)S(1)} %collective-permute-done.1.rows.theirs) | copy-start | bytes 3538948
  98.6 11.4 %collective-permute-start.9 = (bf16[256,688]{1,0:T(8,128)(2,1)S(1)}, bf16[256,688]{1,0:T(8,128)(2,1)S(1)}, u32[]{:S(2)}, u32[]{:S(2)}) collective-permute-start(bf16[256,688]{1,0:T(8,128)(2,1)S(1)} %shard_map.100), channel_id=1, source_target_pairs={{0,1},{1,0},{2,3},{3,2},{4,5},{5,4},{6,7},{7,6},{8,9},{9,8},{10,11... | collective-permute-start | bytes 1056776 | tf_op jit(solution)/shard_map/ppermute | solution.py:19
  100.5 13.2 %collective-permute-start.11 = (bf16[344,256]{1,0:T(8,128)(2,1)S(1)}, bf16[344,256]{1,0:T(8,128)(2,1)S(1)}, u32[]{:S(2)}, u32[]{:S(2)}) collective-permute-start(bf16[344,256]{1,0:T(8,128)(2,1)S(1)} %slice.72), channel_id=1, source_target_pairs={{0,14},{2,0},{4,2},{6,4},{8,6},{10,8},{12,10},{14,12},{1,15},{3,1}... | collective-permute-start | bytes 528392 | tf_op jit(solution)/shard_map/ppermute | solution.py:51
  110.0 6.7 %copy-start.3 = (bf16[1032,256]{1,0:T(8,128)(2,1)S(1)}, bf16[1032,256]{1,0:T(8,128)(2,1)}, u32[]{:S(2)}) copy-start(bf16[1032,256]{1,0:T(8,128)(2,1)} %copy-done.1) | copy-start | bytes 1585156
  110.3 14.4 %copy-start.17 = (s32[8]{0:T(128)S(1)}, s32[8]{0:T(128)}, u32[]{:S(2)}) copy-start(s32[8]{0:T(128)} %param.15) | copy-start | bytes 100
  110.3 6.4 %collective-permute-start.10 = (bf16[256,344]{1,0:T(8,128)(2,1)S(1)}, bf16[256,344]{1,0:T(8,128)(2,1)S(1)}, u32[]{:S(2)}, u32[]{:S(2)}) collective-permute-start(bf16[256,344]{1,0:T(8,128)(2,1)S(1)} %fusion.own), channel_id=1, source_target_pairs={{0,1},{1,0},{2,3},{3,2},{4,5},{5,4},{6,7},{7,6},{8,9},{9,8},{10,11... | collective-permute-start | bytes 528392 | tf_op jit(solution)/shard_map/ppermute | solution.py:19
  113.7 5.9 %copy-start.9 = (bf16[344,256]{1,0:T(8,128)(2,1)}, bf16[344,256]{1,0:T(8,128)(2,1)S(1)}, u32[]{:S(2)}) copy-start(bf16[344,256]{1,0:T(8,128)(2,1)S(1)} %collective-permute-done.11.fourth) | copy-start | bytes 528388
  116.7 2.8 %copy-start.7 = (bf16[256,344]{1,0:T(8,128)(2,1)}, bf16[256,344]{1,0:T(8,128)(2,1)S(1)}, u32[]{:S(2)}) copy-start(bf16[256,344]{1,0:T(8,128)(2,1)S(1)} %collective-permute-done.10.other) | copy-start | bytes 528388
  119.6 10.9 %collective-permute-start.12 = (bf16[4,8,64,256]{3,2,1,0:T(8,128)(2,1)}, bf16[4,8,64,256]{3,2,1,0:T(8,128)(2,1)}, u32[]{:S(2)}, u32[]{:S(2)}) collective-permute-start(bf16[4,8,64,256]{3,2,1,0:T(8,128)(2,1)} %shard_map.102), channel_id=1, source_target_pairs={{0,16},{16,0},{1,17},{17,1},{2,18},{18,2},{3,19},{19,3},{4,20},{20... | collective-permute-start | bytes 3145736 | tf_op jit(solution)/shard_map/ppermute | solution.py:19
  124.8 1.0 copy-start.4
  133.1 3.9 %slice-start = ((bf16[2,128,2304]{2,1,0:T(8,128)(2,1)}), bf16[2,128,256]{2,1,0:T(8,128)(2,1)S(1)}, s32[]{:S(2)}) async-start(bf16[2,128,2304]{2,1,0:T(8,128)(2,1)} %copy-done), calls=%async_computation.6 | async-start | bytes 262144 | tf_op jit(solution)/shard_map/slice | solution.py:173
  133.1 18.8 %all-to-all-start.1 = ((bf16[4,8,64,256]{3,2,1,0:T(8,128)(2,1)}), bf16[4,8,64,256]{3,2,1,0:T(8,128)(2,1)S(1)}, u32[]{:S(2)}, u32[]{:S(2)}) async-start(bf16[4,8,64,256]{3,2,1,0:T(8,128)(2,1)} %add_convert_fusion), calls=%async_computation.1 | async-start | bytes 2097152 | tf_op jit(solution)/shard_map/all_to_all | solution.py:180
  137.9 18.6 %collective-permute-start.13 = (bf16[8,2048]{1,0:T(8,128)(2,1)S(1)}, bf16[8,2048]{1,0:T(8,128)(2,1)S(1)}, u32[]{:S(2)}, u32[]{:S(2)}) collective-permute-start(bf16[8,2048]{1,0:T(8,128)(2,1)S(1)} %convolution_convert_fusion), channel_id=1, source_target_pairs={{0,1},{1,0},{2,3},{3,2},{4,5},{5,4},{6,7},{7,6},{8,9},{9,8},{10,11... | collective-permute-start | bytes 98312 | tf_op jit(solution)/shard_map/ppermute | solution.py:19
  152.9 14.2 %copy-start.11 = (bf16[8,4096]{1,0:T(8,128)(2,1)S(1)}, bf16[8,4096]{1,0:T(8,128)(2,1)}, u32[]{:S(2)}) copy-start(bf16[8,4096]{1,0:T(8,128)(2,1)} %param.8) | copy-start | bytes 196612
  152.9 13.9 %all-to-all-start.2 = ((bf16[8,8,8,256]{3,2,1,0:T(8,128)(2,1)}), bf16[8,8,8,256]{3,2,1,0:T(8,128)(2,1)S(1)}, u32[]{:S(2)}, u32[]{:S(2)}) async-start(bf16[8,8,8,256]{3,2,1,0:T(8,128)(2,1)} %bitcast.13), calls=%async_computation.2 | async-start | bytes 524288 | tf_op jit(solution)/shard_map/all_to_all | solution.py:184
  156.5 10.9 %copy-start.16 = (f32[4096]{0:T(1024)S(1)}, f32[4096]{0:T(1024)}, u32[]{:S(2)}) copy-start(f32[4096]{0:T(1024)} %param.9) | copy-start | bytes 49156
  166.9 42.7 %copy-start.15 = (f32[2,4096]{1,0:T(2,128)S(1)}, f32[2,4096]{1,0:T(2,128)}, u32[]{:S(2)}) copy-start(f32[2,4096]{1,0:T(2,128)} %param.13) | copy-start | bytes 98308
  198.6 11.0 %all-to-all-start.5 = ((f32[16,2,256]{2,1,0:T(2,128)}), f32[16,2,256]{2,1,0:T(2,128)S(1)}, u32[]{:S(2)}, u32[]{:S(2)}) async-start(f32[16,2,256]{2,1,0:T(2,128)} %broadcast_in_dim.19), calls=%async_computation.5 | async-start | bytes 65536 | tf_op jit(solution)/shard_map/all_to_all | solution.py:24
  (5 other events, 4.7 us)

commit v5 on v4

--- a/solution.py
+++ b/solution.py
@@ -63,17 +63,21 @@
 EARLY = (0, 1, 2, 3, 5, 6, 7)
 
 
+def taken(rows, half, j):
+    return rows[:, half, :, 256 * j : 256 * j + 256].reshape(128, 256)
+
+
 def early_kernel(half, rows, *refs):
     *blocks, out = refs
     total = 0.0
     for j, block in zip(EARLY, blocks):
-        total += times(rows[half, :, 256 * j : 256 * j + 256], block[:688])
+        total += times(taken(rows, half, j), block[:688])
     out[...] = total
 
 
 def last_kernel(half, mine, theirs, early_mine, early_theirs, block, out):
     for start, rows, early in ((0, mine, early_mine), (128, theirs, early_theirs)):
-        total = early[...] + times(rows[half, :, 1024:1280], block[...])
+        total = early[...] + times(taken(rows, half, 4), block[...])
         out[start : start + 128] = total.astype(out.dtype)
 
 
@@ -150,8 +154,7 @@
     other_code = received[:, 2048]
     table, _ = by_class(centroids.astype(BF16), yl)
     sent = jnp.concatenate([x, table.reshape(16, 256)], axis=1)
-    copies = jnp.broadcast_to(sent.reshape(2, 1, 8, 2304), (2, 16, 8, 2304))
-    mine = lax.all_to_all(copies, ROWS, 1, 1, tiled=True).reshape(2, 128, 2304)
+    mine = to_everyone(sent.reshape(2, 8, 2304), ROWS)
     theirs = swapped(mine, "c")
 
     early_mine = early_product(1, mine, weights)
@@ -170,9 +173,9 @@
 
     mine, theirs, terms = lax.optimization_barrier((mine, theirs, terms))
     core = lax.axis_index("c")
-    lists = jnp.stack([mine[..., 2048:], theirs[..., 2048:]]).reshape(2, 2, 4, 4, 2048)
+    lists = jnp.stack([mine[..., 2048:], theirs[..., 2048:]]).reshape(2, 4, 4, 2, 2048)
     lists = jnp.where(core == 0, lists, lists[::-1])
-    lists = lists.transpose(3, 2, 0, 1, 4).reshape(64, 2048)
+    lists = lists.transpose(2, 1, 0, 3, 4).reshape(64, 2048)
     picked = jnp.dot(one_hot(code), lists, preferred_element_type=F32).astype(BF16)
     other_picked = jnp.dot(one_hot(other_code), lists, preferred_element_type=F32).astype(BF16)
     coarse = interleaved(picked, swapped(other_picked, "yl"), yl)

time: 212 us -> 210 us (level)
    all_to_all x1 -> x0, starting transfers between devices: 9.72 us -> none  [program(): mine = lax.all_to_all(copies, ROWS, 1, 1, tiled=True).reshape(2, 128, 2304)]
    all_to_all x1 -> x2, starting transfers between devices: 3.5 us -> 13.2 us  [to_everyone(): return lax.all_to_all(copies, axis, split_axis=0, concat_axis=0, tiled=True)]
    all_to_all x1 -> x2, waiting for transfers between devices: 7.36 us -> 13.6 us  [to_everyone(): return lax.all_to_all(copies, axis, split_axis=0, concat_axis=0, tiled=True)]
    all_to_all x1 -> x0, waiting for transfers between devices: 6.16 us -> none  [program(): mine = lax.all_to_all(copies, ROWS, 1, 1, tiled=True).reshape(2, 128, 2304)]
    unnamed x38 -> x36, local copies, waits for them, and re-layouts: 5.96 us -> 5.81 us
where the time goes in v5:
time: 210 us; the launch traced here: 209 us
  starting transfers between devices  84.1 us (40%)
  waiting for transfers between devices  62.7 us (30%)
  blocking collectives  29.2 us (14%)
  Pallas kernels  13.2 us (6%)
  local copies, waits for them, and re-layouts  9.49 us (5%)
  other arithmetic  8.26 us (4%)
    ppermute x8, starting transfers between devices, hop(): return lax.ppermute(value, 'z', pairs)  39.6 us
    ppermute x8, waiting for transfers between devices, hop(): return lax.ppermute(value, 'z', pairs)  25.5 us
    ppermute x6, starting transfers between devices, swapped(): return lax.ppermute(value, axis, SWAP)  24.1 us
    all_to_all x1, blocking collectives, program(): sums = lax.all_to_all(sums.reshape(32, 2, 384), LIST, 0, 0, tiled=True)  16.5 us
    all_to_all x2, waiting for transfers between devices, to_everyone(): return lax.all_to_all(copies, axis, split_axis=0, concat_axis=0, tiled=True)  13.6 us
    all_to_all x2, starting transfers between devices, to_everyone(): return lax.all_to_all(copies, axis, split_axis=0, concat_axis=0, tiled=True)  13.2 us
    all_to_all x1, blocking collectives, program(): blocks = lax.all_to_all(blocks, SHARD, 0, 0, tiled=True).reshape(128, 384)  12.7 us
    all_to_all x1, waiting for transfers between devices, program(): terms = lax.all_to_all(terms, ('yh', 'yl'), 0, 0, tiled=True)  10.3 us
  transfers between devices with their start and end apart: 18, of which 10 were waited for; matrix products, arithmetic and copies ran while one was open for 2% of the time, Pallas kernels for 5%

profile of v5, /device:TPU:1, one launch (start us, length us, event | category | flops | bytes accessed | tf_op | source)
XLA Modules:
  0.0 208.9 jit_solution(12450499831967458617)
XLA Ops:
  2.3 4.0 %collective-permute-start = (bf16[8,2176]{1,0:T(8,128)(2,1)S(1)}, bf16[8,2176]{1,0:T(8,128)(2,1)S(1)}, u32[]{:S(2)}, u32[]{:S(2)}) collective-permute-start(bf16[8,2176]{1,0:T(8,128)(2,1)S(1)} %pad_maximum_fusion.5), channel_id=1, source_target_pairs={{0,1},{1,0},{2,3},{3,2},{4,5},{5,4},{6,7},{7,6},{8,9},{9,8},{10,11... | collective-permute-start | bytes 104456 | tf_op jit(solution)/shard_map/ppermute | solution.py:19
  8.7 9.7 %all-to-all-start = ((bf16[16,2,8,2304]{3,2,1,0:T(8,128)(2,1)}), bf16[16,2,8,2304]{3,2,1,0:T(8,128)(2,1)S(1)}, u32[]{:S(2)}, u32[]{:S(2)}) async-start(bf16[16,2,8,2304]{3,2,1,0:T(8,128)(2,1)} %broadcast_in_dim.14), calls=%async_computation | async-start | bytes 2359296 | tf_op jit(solution)/shard_map/all_to_all | solution.py:24
  18.5 4.0 %collective-permute-start.2 = (bf16[1032,256]{1,0:T(8,128)(2,1)S(1)}, bf16[1032,256]{1,0:T(8,128)(2,1)S(1)}, u32[]{:S(2)}, u32[]{:S(2)}) collective-permute-start(bf16[1032,256]{1,0:T(8,128)(2,1)S(1)} %pad_maximum_fusion.refs_0_), channel_id=1, source_target_pairs={{0,2},{2,4},{4,6},{6,8},{8,10},{10,12},{12,14},{14,0},{1,3},{3,5},... | collective-permute-start | bytes 1585160 | tf_op jit(solution)/shard_map/ppermute | solution.py:51
  22.5 8.6 %collective-permute-start.5 = (bf16[1032,256]{1,0:T(8,128)(2,1)S(1)}, bf16[1032,256]{1,0:T(8,128)(2,1)S(1)}, u32[]{:S(2)}, u32[]{:S(2)}) collective-permute-start(bf16[1032,256]{1,0:T(8,128)(2,1)S(1)} %pad_maximum_fusion.refs_0_), channel_id=1, source_target_pairs={{0,14},{2,0},{4,2},{6,4},{8,6},{10,8},{12,10},{14,12},{1,15},{3,1}... | collective-permute-start | bytes 1585160 | tf_op jit(solution)/shard_map/ppermute | solution.py:51
  31.1 8.3 %collective-permute-done.2.refs_1_ = bf16[1032,256]{1,0:T(8,128)(2,1)S(1)} collective-permute-done((bf16[1032,256]{1,0:T(8,128)(2,1)S(1)}, bf16[1032,256]{1,0:T(8,128)(2,1)S(1)}, u32[]{:S(2)}, u32[]{:S(2)}) %collective-permute-start.2) | collective-permute-done | bytes 528416 | tf_op jit(solution)/shard_map/ppermute | solution.py:51
  39.4 1.9 collective-permute-start.3
  41.3 6.2 %all-to-all-done.rows.mine = bf16[16,2,8,2304]{3,2,1,0:T(8,128)(2,1)S(1)} async-done(((bf16[16,2,8,2304]{3,2,1,0:T(8,128)(2,1)}), bf16[16,2,8,2304]{3,2,1,0:T(8,128)(2,1)S(1)}, u32[]{:S(2)}, u32[]{:S(2)}) %all-to-all-start) | async-done | bytes 1179680 | tf_op jit(solution)/shard_map/all_to_all | solution.py:24
  47.6 6.2 %collective-permute-start.1 = (bf16[16,2,8,2304]{3,2,1,0:T(8,128)(2,1)S(1)}, bf16[16,2,8,2304]{3,2,1,0:T(8,128)(2,1)S(1)}, u32[]{:S(2)}, u32[]{:S(2)}) collective-permute-start(bf16[16,2,8,2304]{3,2,1,0:T(8,128)(2,1)S(1)} %all-to-all-done.rows.mine), channel_id=1, source_target_pairs={{0,16},{16,0},{1,17},{17,1},{2,18},{18,2},{3,19},{19,3},{4,20},{20... | collective-permute-start | bytes 3538952 | tf_op jit(solution)/shard_map/ppermute | solution.py:19
  53.7 10.7 %collective-permute-start.6 = (bf16[1032,256]{1,0:T(8,128)(2,1)S(1)}, bf16[1032,256]{1,0:T(8,128)(2,1)S(1)}, u32[]{:S(2)}, u32[]{:S(2)}) collective-permute-start(bf16[1032,256]{1,0:T(8,128)(2,1)S(1)} %collective-permute-done.5.refs_6_), channel_id=1, source_target_pairs={{0,14},{2,0},{4,2},{6,4},{8,6},{10,8},{12,10},{14,12},{1,15},{3,1}... | collective-permute-start | bytes 1585160 | tf_op jit(solution)/shard_map/ppermute | solution.py:51
  65.2 1.9 collective-permute-start.4
  67.1 8.6 %collective-permute-done.6.refs_5_ = bf16[1032,256]{1,0:T(8,128)(2,1)S(1)} collective-permute-done((bf16[1032,256]{1,0:T(8,128)(2,1)S(1)}, bf16[1032,256]{1,0:T(8,128)(2,1)S(1)}, u32[]{:S(2)}, u32[]{:S(2)}) %collective-permute-start.6) | collective-permute-done | bytes 528416 | tf_op jit(solution)/shard_map/ppermute | solution.py:51
  75.8 5.3 %collective-permute-start.7 = (bf16[1032,256]{1,0:T(8,128)(2,1)S(1)}, bf16[1032,256]{1,0:T(8,128)(2,1)S(1)}, u32[]{:S(2)}, u32[]{:S(2)}) collective-permute-start(bf16[1032,256]{1,0:T(8,128)(2,1)S(1)} %collective-permute-done.6.refs_5_), channel_id=1, source_target_pairs={{0,14},{2,0},{4,2},{6,4},{8,6},{10,8},{12,10},{14,12},{1,15},{3,1}... | collective-permute-start | bytes 1585160 | tf_op jit(solution)/shard_map/ppermute | solution.py:51
  81.8 1.9 collective-permute-start.8
  83.7 7.8 %collective-permute-done.7.refs_4_ = bf16[1032,256]{1,0:T(8,128)(2,1)S(1)} collective-permute-done((bf16[1032,256]{1,0:T(8,128)(2,1)S(1)}, bf16[1032,256]{1,0:T(8,128)(2,1)S(1)}, u32[]{:S(2)}, u32[]{:S(2)}) %collective-permute-start.7) | collective-permute-done | bytes 528416 | tf_op jit(solution)/shard_map/ppermute | solution.py:51
  94.5 2.3 %shard_map.99.early_theirs = f32[128,688]{1,0:T(8,128)S(1)} custom-call(bf16[16,2,8,2304]{3,2,1,0:T(8,128)(2,1)S(1)} %collective-permute-done.1.rows.theirs, bf16[1032,256]{1,0:T(8,128)(2,1)S(1)} %pad_maximum_fusion.refs_0_, bf16[1032,256]{1,0:T(8,128)(2,1)S(1)} %collective-permute-done.2.refs_1_, bf16[1032,256]{1,0:T(8,128)(2,1)} %collective-permute-done.3.refs_2_, ...), custom_call_target="tpu_custom_call" | custom-call | flops 315621376 | bytes 3670016 | tf_op jit(solution)/shard_map/pallas_call | solution.py:92
  97.1 1.9 collective-permute-start.9
  99.1 5.3 %collective-permute-start.11 = (bf16[344,256]{1,0:T(8,128)(2,1)S(1)}, bf16[344,256]{1,0:T(8,128)(2,1)S(1)}, u32[]{:S(2)}, u32[]{:S(2)}) collective-permute-start(bf16[344,256]{1,0:T(8,128)(2,1)S(1)} %slice.72), channel_id=1, source_target_pairs={{0,14},{2,0},{4,2},{6,4},{8,6},{10,8},{12,10},{14,12},{1,15},{3,1}... | collective-permute-start | bytes 528392 | tf_op jit(solution)/shard_map/ppermute | solution.py:51
  104.4 1.9 shard_map.95.early_mine
  108.9 3.4 %collective-permute-start.10 = (bf16[256,344]{1,0:T(8,128)(2,1)S(1)}, bf16[256,344]{1,0:T(8,128)(2,1)S(1)}, u32[]{:S(2)}, u32[]{:S(2)}) collective-permute-start(bf16[256,344]{1,0:T(8,128)(2,1)S(1)} %fusion.own), channel_id=1, source_target_pairs={{0,1},{1,0},{2,3},{3,2},{4,5},{5,4},{6,7},{7,6},{8,9},{9,8},{10,11... | collective-permute-start | bytes 528392 | tf_op jit(solution)/shard_map/ppermute | solution.py:19
  112.3 3.0 %collective-permute-done.10.other = bf16[256,344]{1,0:T(8,128)(2,1)S(1)} collective-permute-done((bf16[256,344]{1,0:T(8,128)(2,1)S(1)}, bf16[256,344]{1,0:T(8,128)(2,1)S(1)}, u32[]{:S(2)}, u32[]{:S(2)}) %collective-permute-start.10) | collective-permute-done | bytes 176160 | tf_op jit(solution)/shard_map/ppermute | solution.py:19
  115.3 2.8 %shard_map.102 = bf16[4,8,64,256]{3,2,1,0:T(8,128)(2,1)} custom-call(bf16[256,344]{1,0:T(8,128)(2,1)S(1)} %fusion.own, bf16[256,344]{1,0:T(8,128)(2,1)S(1)} %collective-permute-done.10.other, bf16[344,256]{1,0:T(8,128)(2,1)S(1)} %collective-permute-done.11.fourth, bf16[1032,256]{1,0:T(8,128)(2,1)S(1)} %pad_maximum_fusion.refs_0_, ...), custom_call_target="tpu_custom_call" | custom-call | flops 360710144 | bytes 3145728 | tf_op jit(solution)/shard_map/pallas_call | solution.py:130
  118.1 5.0 %collective-permute-start.12 = (bf16[4,8,64,256]{3,2,1,0:T(8,128)(2,1)}, bf16[4,8,64,256]{3,2,1,0:T(8,128)(2,1)}, u32[]{:S(2)}, u32[]{:S(2)}) collective-permute-start(bf16[4,8,64,256]{3,2,1,0:T(8,128)(2,1)} %shard_map.102), channel_id=1, source_target_pairs={{0,16},{16,0},{1,17},{17,1},{2,18},{18,2},{3,19},{19,3},{4,20},{20... | collective-permute-start | bytes 3145736 | tf_op jit(solution)/shard_map/ppermute | solution.py:19
  129.1 2.6 %add_convert_fusion = bf16[4,8,64,256]{3,2,1,0:T(8,128)(2,1)} fusion(f32[4,8,64,256]{3,2,1,0:T(8,128)S(1)} %shard_map.101, bf16[4,8,64,256]{3,2,1,0:T(8,128)(2,1)} %collective-permute-done.12), kind=kLoop, calls=%fused_computation.2 | loop fusion | flops 1572864 | bytes 4194304 | tf_op jit(solution)/shard_map/convert_element_type | solution.py:172
  131.7 3.6 %all-to-all-start.1 = ((bf16[4,8,64,256]{3,2,1,0:T(8,128)(2,1)}), bf16[4,8,64,256]{3,2,1,0:T(8,128)(2,1)S(1)}, u32[]{:S(2)}, u32[]{:S(2)}) async-start(bf16[4,8,64,256]{3,2,1,0:T(8,128)(2,1)} %add_convert_fusion), calls=%async_computation.1 | async-start | bytes 2097152 | tf_op jit(solution)/shard_map/all_to_all | solution.py:183
  136.6 3.6 %collective-permute-start.13 = (bf16[8,2048]{1,0:T(8,128)(2,1)S(1)}, bf16[8,2048]{1,0:T(8,128)(2,1)S(1)}, u32[]{:S(2)}, u32[]{:S(2)}) collective-permute-start(bf16[8,2048]{1,0:T(8,128)(2,1)S(1)} %convolution_convert_fusion), channel_id=1, source_target_pairs={{0,1},{1,0},{2,3},{3,2},{4,5},{5,4},{6,7},{7,6},{8,9},{9,8},{10,11... | collective-permute-start | bytes 98312 | tf_op jit(solution)/shard_map/ppermute | solution.py:19
  140.5 10.0 %all-to-all-done.1 = bf16[4,8,64,256]{3,2,1,0:T(8,128)(2,1)S(1)} async-done(((bf16[4,8,64,256]{3,2,1,0:T(8,128)(2,1)}), bf16[4,8,64,256]{3,2,1,0:T(8,128)(2,1)S(1)}, u32[]{:S(2)}, u32[]{:S(2)}) %all-to-all-start.1) | async-done | bytes 1048608 | tf_op jit(solution)/shard_map/all_to_all | solution.py:183
  151.4 3.6 %all-to-all-start.2 = ((bf16[8,8,8,256]{3,2,1,0:T(8,128)(2,1)}), bf16[8,8,8,256]{3,2,1,0:T(8,128)(2,1)S(1)}, u32[]{:S(2)}, u32[]{:S(2)}) async-start(bf16[8,8,8,256]{3,2,1,0:T(8,128)(2,1)} %bitcast.12), calls=%async_computation.2 | async-start | bytes 524288 | tf_op jit(solution)/shard_map/all_to_all | solution.py:187
  155.1 10.3 %all-to-all-done.2 = bf16[8,8,8,256]{3,2,1,0:T(8,128)(2,1)S(1)} async-done(((bf16[8,8,8,256]{3,2,1,0:T(8,128)(2,1)}), bf16[8,8,8,256]{3,2,1,0:T(8,128)(2,1)S(1)}, u32[]{:S(2)}, u32[]{:S(2)}) %all-to-all-start.2) | async-done | bytes 262176 | tf_op jit(solution)/shard_map/all_to_all | solution.py:187
  166.7 12.7 %all_to_all.30 = bf16[16,8,384]{2,1,0:T(8,128)(2,1)S(1)} all-to-all(bf16[16,8,384]{2,1,0:T(8,128)(2,1)S(1)} %pad_maximum_fusion.2), channel_id=1, replica_groups=mesh['yh'=4,'x'=4,'c'=2,'z'=8,'yl'=2] {'z','yl'}, dimensions={0} | all-to-all | bytes 196608 | tf_op jit(solution)/shard_map/all_to_all | solution.py:199
  180.0 16.5 %all_to_all.31 = bf16[32,2,384]{2,1,0:T(2,128)(2,1)S(1)} all-to-all(bf16[32,2,384]{2,1,0:T(2,128)(2,1)S(1)} %reshape.98), channel_id=1, replica_groups=mesh['yh'=4,'x'=4,'c'=2,'z'=8,'yl'=2] {'yh','x','c'}, dimensions={0} | all-to-all | bytes 98304 | tf_op jit(solution)/shard_map/all_to_all | solution.py:204
  197.2 3.5 %all-to-all-start.5 = ((f32[16,2,256]{2,1,0:T(2,128)}), f32[16,2,256]{2,1,0:T(2,128)S(1)}, u32[]{:S(2)}, u32[]{:S(2)}) async-start(f32[16,2,256]{2,1,0:T(2,128)} %broadcast_in_dim.16), calls=%async_computation.5 | async-start | bytes 65536 | tf_op jit(solution)/shard_map/all_to_all | solution.py:24
  200.8 7.4 %all-to-all-done.5 = f32[16,2,256]{2,1,0:T(2,128)S(1)} async-done(((f32[16,2,256]{2,1,0:T(2,128)}), f32[16,2,256]{2,1,0:T(2,128)S(1)}, u32[]{:S(2)}, u32[]{:S(2)}) %all-to-all-start.5) | async-done | bytes 32800 | tf_op jit(solution)/shard_map/all_to_all | solution.py:24
  (113 shorter events, 23.1 us)
Async XLA Ops:
  2.3 5.3 %collective-permute-start = (bf16[8,2176]{1,0:T(8,128)(2,1)S(1)}, bf16[8,2176]{1,0:T(8,128)(2,1)S(1)}, u32[]{:S(2)}, u32[]{:S(2)}) collective-permute-start(bf16[8,2176]{1,0:T(8,128)(2,1)S(1)} %pad_maximum_fusion.5), channel_id=1, source_target_pairs={{0,1},{1,0},{2,3},{3,2},{4,5},{5,4},{6,7},{7,6},{8,9},{9,8},{10,11... | collective-permute-start | bytes 104456 | tf_op jit(solution)/shard_map/ppermute | solution.py:19
  8.7 9.7 %copy-start.12 = (bf16[344,256]{1,0:T(8,128)(2,1)S(1)}, bf16[344,256]{1,0:T(8,128)(2,1)}, u32[]{:S(2)}) copy-start(bf16[344,256]{1,0:T(8,128)(2,1)} %param.12) | copy-start | bytes 528388
  8.7 9.7 %copy-start.13 = (bf16[256,344]{0,1:T(8,128)(2,1)S(1)}, bf16[256,344]{0,1:T(8,128)(2,1)}, u32[]{:S(2)}) copy-start(bf16[256,344]{0,1:T(8,128)(2,1)} %param.11) | copy-start | bytes 528388
  8.7 9.7 %copy-start.14 = (bf16[256,344]{0,1:T(8,128)(2,1)S(1)}, bf16[256,344]{0,1:T(8,128)(2,1)}, u32[]{:S(2)}) copy-start(bf16[256,344]{0,1:T(8,128)(2,1)} %param.10) | copy-start | bytes 528388
  8.7 38.8 %all-to-all-start = ((bf16[16,2,8,2304]{3,2,1,0:T(8,128)(2,1)}), bf16[16,2,8,2304]{3,2,1,0:T(8,128)(2,1)S(1)}, u32[]{:S(2)}, u32[]{:S(2)}) async-start(bf16[16,2,8,2304]{3,2,1,0:T(8,128)(2,1)} %broadcast_in_dim.14), calls=%async_computation | async-start | bytes 2359296 | tf_op jit(solution)/shard_map/all_to_all | solution.py:24
  18.5 20.9 %collective-permute-start.2 = (bf16[1032,256]{1,0:T(8,128)(2,1)S(1)}, bf16[1032,256]{1,0:T(8,128)(2,1)S(1)}, u32[]{:S(2)}, u32[]{:S(2)}) collective-permute-start(bf16[1032,256]{1,0:T(8,128)(2,1)S(1)} %pad_maximum_fusion.refs_0_), channel_id=1, source_target_pairs={{0,2},{2,4},{4,6},{6,8},{8,10},{10,12},{12,14},{14,0},{1,3},{3,5},... | collective-permute-start | bytes 1585160 | tf_op jit(solution)/shard_map/ppermute | solution.py:51
  22.5 31.2 %collective-permute-start.5 = (bf16[1032,256]{1,0:T(8,128)(2,1)S(1)}, bf16[1032,256]{1,0:T(8,128)(2,1)S(1)}, u32[]{:S(2)}, u32[]{:S(2)}) collective-permute-start(bf16[1032,256]{1,0:T(8,128)(2,1)S(1)} %pad_maximum_fusion.refs_0_), channel_id=1, source_target_pairs={{0,14},{2,0},{4,2},{6,4},{8,6},{10,8},{12,10},{14,12},{1,15},{3,1}... | collective-permute-start | bytes 1585160 | tf_op jit(solution)/shard_map/ppermute | solution.py:51
  39.4 25.8 %collective-permute-start.3 = (bf16[1032,256]{1,0:T(8,128)(2,1)S(1)}, bf16[1032,256]{1,0:T(8,128)(2,1)}, u32[]{:S(2)}, u32[]{:S(2)}) collective-permute-start(bf16[1032,256]{1,0:T(8,128)(2,1)S(1)} %collective-permute-done.2.refs_1_), channel_id=1, source_target_pairs={{0,2},{2,4},{4,6},{6,8},{8,10},{10,12},{12,14},{14,0},{1,3},{3,5},... | collective-permute-start | bytes 1585160 | tf_op jit(solution)/shard_map/ppermute | solution.py:51
  47.6 46.9 %collective-permute-start.1 = (bf16[16,2,8,2304]{3,2,1,0:T(8,128)(2,1)S(1)}, bf16[16,2,8,2304]{3,2,1,0:T(8,128)(2,1)S(1)}, u32[]{:S(2)}, u32[]{:S(2)}) collective-permute-start(bf16[16,2,8,2304]{3,2,1,0:T(8,128)(2,1)S(1)} %all-to-all-done.rows.mine), channel_id=1, source_target_pairs={{0,16},{16,0},{1,17},{17,1},{2,18},{18,2},{3,19},{19,3},{4,20},{20... | collective-permute-start | bytes 3538952 | tf_op jit(solution)/shard_map/ppermute | solution.py:19
  53.7 22.0 %collective-permute-start.6 = (bf16[1032,256]{1,0:T(8,128)(2,1)S(1)}, bf16[1032,256]{1,0:T(8,128)(2,1)S(1)}, u32[]{:S(2)}, u32[]{:S(2)}) collective-permute-start(bf16[1032,256]{1,0:T(8,128)(2,1)S(1)} %collective-permute-done.5.refs_6_), channel_id=1, source_target_pairs={{0,14},{2,0},{4,2},{6,4},{8,6},{10,8},{12,10},{14,12},{1,15},{3,1}... | collective-permute-start | bytes 1585160 | tf_op jit(solution)/shard_map/ppermute | solution.py:51
  65.2 16.6 %collective-permute-start.4 = (bf16[1032,256]{1,0:T(8,128)(2,1)}, bf16[1032,256]{1,0:T(8,128)(2,1)S(1)}, u32[]{:S(2)}, u32[]{:S(2)}) collective-permute-start(bf16[1032,256]{1,0:T(8,128)(2,1)} %collective-permute-done.3.refs_2_), channel_id=1, source_target_pairs={{0,2},{2,4},{4,6},{6,8},{8,10},{10,12},{12,14},{14,0},{1,3},{3,5},... | collective-permute-start | bytes 1585160 | tf_op jit(solution)/shard_map/ppermute | solution.py:51
  75.7 39.5 %copy-start.5 = (bf16[1032,256]{1,0:T(8,128)(2,1)}, bf16[1032,256]{1,0:T(8,128)(2,1)S(1)}, u32[]{:S(2)}) copy-start(bf16[1032,256]{1,0:T(8,128)(2,1)S(1)} %collective-permute-done.6.refs_5_) | copy-start | bytes 1585156
  75.8 15.8 %collective-permute-start.7 = (bf16[1032,256]{1,0:T(8,128)(2,1)S(1)}, bf16[1032,256]{1,0:T(8,128)(2,1)S(1)}, u32[]{:S(2)}, u32[]{:S(2)}) collective-permute-start(bf16[1032,256]{1,0:T(8,128)(2,1)S(1)} %collective-permute-done.6.refs_5_), channel_id=1, source_target_pairs={{0,14},{2,0},{4,2},{6,4},{8,6},{10,8},{12,10},{14,12},{1,15},{3,1}... | collective-permute-start | bytes 1585160 | tf_op jit(solution)/shard_map/ppermute | solution.py:51
  81.8 15.0 %collective-permute-start.8 = (bf16[688,256]{1,0:T(8,128)(2,1)S(1)}, bf16[688,256]{1,0:T(8,128)(2,1)S(1)}, u32[]{:S(2)}, u32[]{:S(2)}) collective-permute-start(bf16[688,256]{1,0:T(8,128)(2,1)S(1)} %slice.69), channel_id=1, source_target_pairs={{0,2},{2,4},{4,6},{6,8},{8,10},{10,12},{12,14},{14,0},{1,3},{3,5},... | collective-permute-start | bytes 1056776 | tf_op jit(solution)/shard_map/ppermute | solution.py:51
  94.5 13.7 %copy-start = (bf16[16,2,8,2304]{3,2,1,0:T(8,128)(2,1)}, bf16[16,2,8,2304]{3,2,1,0:T(8,128)(2,1)S(1)}, u32[]{:S(2)}) copy-start(bf16[16,2,8,2304]{3,2,1,0:T(8,128)(2,1)S(1)} %collective-permute-done.1.rows.theirs) | copy-start | bytes 3538948
  97.1 11.5 %collective-permute-start.9 = (bf16[256,688]{1,0:T(8,128)(2,1)S(1)}, bf16[256,688]{1,0:T(8,128)(2,1)S(1)}, u32[]{:S(2)}, u32[]{:S(2)}) collective-permute-start(bf16[256,688]{1,0:T(8,128)(2,1)S(1)} %shard_map.100), channel_id=1, source_target_pairs={{0,1},{1,0},{2,3},{3,2},{4,5},{5,4},{6,7},{7,6},{8,9},{9,8},{10,11... | collective-permute-start | bytes 1056776 | tf_op jit(solution)/shard_map/ppermute | solution.py:19
  99.1 13.2 %collective-permute-start.11 = (bf16[344,256]{1,0:T(8,128)(2,1)S(1)}, bf16[344,256]{1,0:T(8,128)(2,1)S(1)}, u32[]{:S(2)}, u32[]{:S(2)}) collective-permute-start(bf16[344,256]{1,0:T(8,128)(2,1)S(1)} %slice.72), channel_id=1, source_target_pairs={{0,14},{2,0},{4,2},{6,4},{8,6},{10,8},{12,10},{14,12},{1,15},{3,1}... | collective-permute-start | bytes 528392 | tf_op jit(solution)/shard_map/ppermute | solution.py:51
  108.6 6.7 %copy-start.3 = (bf16[1032,256]{1,0:T(8,128)(2,1)S(1)}, bf16[1032,256]{1,0:T(8,128)(2,1)}, u32[]{:S(2)}) copy-start(bf16[1032,256]{1,0:T(8,128)(2,1)} %copy-done.1) | copy-start | bytes 1585156
  108.9 14.3 %copy-start.17 = (s32[8]{0:T(128)S(1)}, s32[8]{0:T(128)}, u32[]{:S(2)}) copy-start(s32[8]{0:T(128)} %param.15) | copy-start | bytes 100
  108.9 6.4 %collective-permute-start.10 = (bf16[256,344]{1,0:T(8,128)(2,1)S(1)}, bf16[256,344]{1,0:T(8,128)(2,1)S(1)}, u32[]{:S(2)}, u32[]{:S(2)}) collective-permute-start(bf16[256,344]{1,0:T(8,128)(2,1)S(1)} %fusion.own), channel_id=1, source_target_pairs={{0,1},{1,0},{2,3},{3,2},{4,5},{5,4},{6,7},{7,6},{8,9},{9,8},{10,11... | collective-permute-start | bytes 528392 | tf_op jit(solution)/shard_map/ppermute | solution.py:19
  112.3 5.9 %copy-start.9 = (bf16[344,256]{1,0:T(8,128)(2,1)}, bf16[344,256]{1,0:T(8,128)(2,1)S(1)}, u32[]{:S(2)}) copy-start(bf16[344,256]{1,0:T(8,128)(2,1)S(1)} %collective-permute-done.11.fourth) | copy-start | bytes 528388
  115.3 2.8 %copy-start.7 = (bf16[256,344]{1,0:T(8,128)(2,1)}, bf16[256,344]{1,0:T(8,128)(2,1)S(1)}, u32[]{:S(2)}) copy-start(bf16[256,344]{1,0:T(8,128)(2,1)S(1)} %collective-permute-done.10.other) | copy-start | bytes 528388
  118.1 10.9 %collective-permute-start.12 = (bf16[4,8,64,256]{3,2,1,0:T(8,128)(2,1)}, bf16[4,8,64,256]{3,2,1,0:T(8,128)(2,1)}, u32[]{:S(2)}, u32[]{:S(2)}) collective-permute-start(bf16[4,8,64,256]{3,2,1,0:T(8,128)(2,1)} %shard_map.102), channel_id=1, source_target_pairs={{0,16},{16,0},{1,17},{17,1},{2,18},{18,2},{3,19},{19,3},{4,20},{20... | collective-permute-start | bytes 3145736 | tf_op jit(solution)/shard_map/ppermute | solution.py:19
  123.3 1.0 copy-start.4
  131.7 3.7 %slice-start = ((bf16[16,2,8,2304]{3,2,1,0:T(8,128)(2,1)}), bf16[16,2,8,256]{3,2,1,0:T(8,128)(2,1)S(1)}, s32[]{:S(2)}) async-start(bf16[16,2,8,2304]{3,2,1,0:T(8,128)(2,1)} %copy-done), calls=%async_computation.6 | async-start | bytes 262144 | tf_op jit(solution)/shard_map/slice | solution.py:176
  131.7 18.8 %all-to-all-start.1 = ((bf16[4,8,64,256]{3,2,1,0:T(8,128)(2,1)}), bf16[4,8,64,256]{3,2,1,0:T(8,128)(2,1)S(1)}, u32[]{:S(2)}, u32[]{:S(2)}) async-start(bf16[4,8,64,256]{3,2,1,0:T(8,128)(2,1)} %add_convert_fusion), calls=%async_computation.1 | async-start | bytes 2097152 | tf_op jit(solution)/shard_map/all_to_all | solution.py:183
  136.6 18.4 %collective-permute-start.13 = (bf16[8,2048]{1,0:T(8,128)(2,1)S(1)}, bf16[8,2048]{1,0:T(8,128)(2,1)S(1)}, u32[]{:S(2)}, u32[]{:S(2)}) collective-permute-start(bf16[8,2048]{1,0:T(8,128)(2,1)S(1)} %convolution_convert_fusion), channel_id=1, source_target_pairs={{0,1},{1,0},{2,3},{3,2},{4,5},{5,4},{6,7},{7,6},{8,9},{9,8},{10,11... | collective-permute-start | bytes 98312 | tf_op jit(solution)/shard_map/ppermute | solution.py:19
  151.4 14.2 %copy-start.11 = (bf16[8,4096]{1,0:T(8,128)(2,1)S(1)}, bf16[8,4096]{1,0:T(8,128)(2,1)}, u32[]{:S(2)}) copy-start(bf16[8,4096]{1,0:T(8,128)(2,1)} %param.8) | copy-start | bytes 196612
  151.4 13.9 %all-to-all-start.2 = ((bf16[8,8,8,256]{3,2,1,0:T(8,128)(2,1)}), bf16[8,8,8,256]{3,2,1,0:T(8,128)(2,1)S(1)}, u32[]{:S(2)}, u32[]{:S(2)}) async-start(bf16[8,8,8,256]{3,2,1,0:T(8,128)(2,1)} %bitcast.12), calls=%async_computation.2 | async-start | bytes 524288 | tf_op jit(solution)/shard_map/all_to_all | solution.py:187
  155.0 10.8 %copy-start.16 = (f32[4096]{0:T(1024)S(1)}, f32[4096]{0:T(1024)}, u32[]{:S(2)}) copy-start(f32[4096]{0:T(1024)} %param.9) | copy-start | bytes 49156
  165.4 42.7 %copy-start.15 = (f32[2,4096]{1,0:T(2,128)S(1)}, f32[2,4096]{1,0:T(2,128)}, u32[]{:S(2)}) copy-start(f32[2,4096]{1,0:T(2,128)} %param.13) | copy-start | bytes 98308
  197.2 11.0 %all-to-all-start.5 = ((f32[16,2,256]{2,1,0:T(2,128)}), f32[16,2,256]{2,1,0:T(2,128)S(1)}, u32[]{:S(2)}, u32[]{:S(2)}) async-start(f32[16,2,256]{2,1,0:T(2,128)} %broadcast_in_dim.16), calls=%async_computation.5 | async-start | bytes 65536 | tf_op jit(solution)/shard_map/all_to_all | solution.py:24
  (5 other events, 4.7 us)

commit v6 on v5

--- a/solution.py
+++ b/solution.py
@@ -194,17 +194,18 @@
     alive = (live > 0).astype(F32)[:, None]
     residuals = (alive * (embedding.astype(F32) - coarse.astype(F32))).astype(BF16)
 
-    blocks = embedding.reshape(8, 16, 256).transpose(1, 0, 2)
-    blocks = jnp.concatenate([blocks, jnp.broadcast_to(code_block, (16, 8, 128))], axis=2)
-    blocks = lax.all_to_all(blocks, SHARD, 0, 0, tiled=True).reshape(128, 384)
-    member = one_hot(blocks[:, 256])
-    sums = jnp.dot(member.T, blocks[:, :256], preferred_element_type=F32).astype(BF16)
+    blocks = embedding.reshape(8, 8, 512).transpose(1, 0, 2)
+    blocks = jnp.concatenate([blocks, jnp.broadcast_to(code_block, (8, 8, 128))], axis=2)
+    blocks = lax.all_to_all(blocks, "z", 0, 0, tiled=True).reshape(64, 640)
+    member = one_hot(blocks[:, 512])
+    sums = jnp.dot(member.T, blocks[:, :512], preferred_element_type=F32).astype(BF16)
     counts = jnp.sum(member.astype(F32), axis=0).astype(BF16)
     sums = jnp.concatenate([sums, jnp.broadcast_to(counts[:, None], (64, 128))], axis=1)
-    sums = lax.all_to_all(sums.reshape(32, 2, 384), LIST, 0, 0, tiled=True)
+    sums = lax.all_to_all(sums.reshape(32, 2, 640), LIST, 0, 0, tiled=True)
     sums = jnp.sum(sums.astype(F32), axis=0)
-    total = to_everyone(sums[:, :256], SHARD).transpose(1, 0, 2).reshape(2, 4096)
-    refreshed = (centroids + total) / (1.0 + sums[:, 256:257])
+    sums = to_everyone(sums, SHARD).reshape(8, 2, 2, 640).sum(axis=1)
+    total = sums[:, :, :512].transpose(1, 0, 2).reshape(2, 4096)
+    refreshed = (centroids + total) / (1.0 + sums[0, :, 512:513])
     return residuals, refreshed
 
 

time: 210 us -> 209 us (level)
  blocking collectives: 29.2 us -> 38.9 us
  waiting for transfers between devices: 62.7 us -> 55.3 us
  starting transfers between devices: 84.1 us -> 80.7 us
    all_to_all x2 -> x3, blocking collectives: 29.2 us -> 38.9 us  [the longest x1 16.5 us: program(): sums = lax.all_to_all(sums.reshape(32, 2, 640), LIST, 0, 0, tiled=True)]
    all_to_all x2 -> x1, waiting for transfers between devices: 13.6 us -> 6.21 us  [to_everyone(): return lax.all_to_all(copies, axis, split_axis=0, concat_axis=0, tiled=True)]
    all_to_all x2 -> x1, starting transfers between devices: 13.2 us -> 9.67 us  [to_everyone(): return lax.all_to_all(copies, axis, split_axis=0, concat_axis=0, tiled=True)]
    unnamed x36 -> x38, local copies, waits for them, and re-layouts: 5.81 us -> 5.85 us
  transfers between devices with their start and end apart: 18 -> 17, of which waited for: 10 -> 9; matrix products, arithmetic and copies ran while one was open for 2% -> 2% of each run, Pallas kernels for 5% -> 5%
where the time goes in v6:
time: 209 us; the launch traced here: 207 us
  starting transfers between devices  80.7 us (39%)
  waiting for transfers between devices  55.3 us (26%)
  blocking collectives  38.9 us (19%)
  Pallas kernels  13.2 us (6%)
  local copies, waits for them, and re-layouts  8.94 us (4%)
  other arithmetic  8.22 us (4%)
    ppermute x8, starting transfers between devices, hop(): return lax.ppermute(value, 'z', pairs)  39.6 us
    ppermute x8, waiting for transfers between devices, hop(): return lax.ppermute(value, 'z', pairs)  25.5 us
    ppermute x6, starting transfers between devices, swapped(): return lax.ppermute(value, axis, SWAP)  24.1 us
    all_to_all x1, blocking collectives, program(): sums = lax.all_to_all(sums.reshape(32, 2, 640), LIST, 0, 0, tiled=True)  16.5 us
    all_to_all x1, blocking collectives, program(): blocks = lax.all_to_all(blocks, 'z', 0, 0, tiled=True).reshape(64, 640)  12.1 us
    all_to_all x1, blocking collectives, to_everyone(): return lax.all_to_all(copies, axis, split_axis=0, concat_axis=0, tiled=True)  10.3 us
    all_to_all x1, waiting for transfers between devices, program(): terms = lax.all_to_all(terms, ('yh', 'yl'), 0, 0, tiled=True)  10.3 us
    all_to_all x1, waiting for transfers between devices, program(): terms = lax.all_to_all(terms, 'x', 0, 0, tiled=True)  9.97 us
  transfers between devices with their start and end apart: 17, of which 9 were waited for; matrix products, arithmetic and copies ran while one was open for 2% of the time, Pallas kernels for 5%

profile of v6, /device:TPU:1, one launch (start us, length us, event | category | flops | bytes accessed | tf_op | source)
XLA Modules:
  0.0 207.2 jit_solution(13547649528852642079)
XLA Ops:
  2.3 4.0 %collective-permute-start = (bf16[8,2176]{1,0:T(8,128)(2,1)S(1)}, bf16[8,2176]{1,0:T(8,128)(2,1)S(1)}, u32[]{:S(2)}, u32[]{:S(2)}) collective-permute-start(bf16[8,2176]{1,0:T(8,128)(2,1)S(1)} %pad_maximum_fusion.5), channel_id=1, source_target_pairs={{0,1},{1,0},{2,3},{3,2},{4,5},{5,4},{6,7},{7,6},{8,9},{9,8},{10,11... | collective-permute-start | bytes 104456 | tf_op jit(solution)/shard_map/ppermute | solution.py:19
  8.7 9.7 %all-to-all-start = ((bf16[16,2,8,2304]{3,2,1,0:T(8,128)(2,1)}), bf16[16,2,8,2304]{3,2,1,0:T(8,128)(2,1)S(1)}, u32[]{:S(2)}, u32[]{:S(2)}) async-start(bf16[16,2,8,2304]{3,2,1,0:T(8,128)(2,1)} %broadcast_in_dim.14), calls=%async_computation | async-start | bytes 2359296 | tf_op jit(solution)/shard_map/all_to_all | solution.py:24
  18.5 4.0 %collective-permute-start.2 = (bf16[1032,256]{1,0:T(8,128)(2,1)S(1)}, bf16[1032,256]{1,0:T(8,128)(2,1)S(1)}, u32[]{:S(2)}, u32[]{:S(2)}) collective-permute-start(bf16[1032,256]{1,0:T(8,128)(2,1)S(1)} %pad_maximum_fusion.refs_0_), channel_id=1, source_target_pairs={{0,2},{2,4},{4,6},{6,8},{8,10},{10,12},{12,14},{14,0},{1,3},{3,5},... | collective-permute-start | bytes 1585160 | tf_op jit(solution)/shard_map/ppermute | solution.py:51
  22.5 8.6 %collective-permute-start.5 = (bf16[1032,256]{1,0:T(8,128)(2,1)S(1)}, bf16[1032,256]{1,0:T(8,128)(2,1)S(1)}, u32[]{:S(2)}, u32[]{:S(2)}) collective-permute-start(bf16[1032,256]{1,0:T(8,128)(2,1)S(1)} %pad_maximum_fusion.refs_0_), channel_id=1, source_target_pairs={{0,14},{2,0},{4,2},{6,4},{8,6},{10,8},{12,10},{14,12},{1,15},{3,1}... | collective-permute-start | bytes 1585160 | tf_op jit(solution)/shard_map/ppermute | solution.py:51
  31.1 8.3 %collective-permute-done.2.refs_1_ = bf16[1032,256]{1,0:T(8,128)(2,1)S(1)} collective-permute-done((bf16[1032,256]{1,0:T(8,128)(2,1)S(1)}, bf16[1032,256]{1,0:T(8,128)(2,1)S(1)}, u32[]{:S(2)}, u32[]{:S(2)}) %collective-permute-start.2) | collective-permute-done | bytes 528416 | tf_op jit(solution)/shard_map/ppermute | solution.py:51
  39.4 1.9 collective-permute-start.3
  41.4 6.2 %all-to-all-done.rows.mine = bf16[16,2,8,2304]{3,2,1,0:T(8,128)(2,1)S(1)} async-done(((bf16[16,2,8,2304]{3,2,1,0:T(8,128)(2,1)}), bf16[16,2,8,2304]{3,2,1,0:T(8,128)(2,1)S(1)}, u32[]{:S(2)}, u32[]{:S(2)}) %all-to-all-start) | async-done | bytes 1179680 | tf_op jit(solution)/shard_map/all_to_all | solution.py:24
  47.6 6.2 %collective-permute-start.1 = (bf16[16,2,8,2304]{3,2,1,0:T(8,128)(2,1)S(1)}, bf16[16,2,8,2304]{3,2,1,0:T(8,128)(2,1)S(1)}, u32[]{:S(2)}, u32[]{:S(2)}) collective-permute-start(bf16[16,2,8,2304]{3,2,1,0:T(8,128)(2,1)S(1)} %all-to-all-done.rows.mine), channel_id=1, source_target_pairs={{0,16},{16,0},{1,17},{17,1},{2,18},{18,2},{3,19},{19,3},{4,20},{20... | collective-permute-start | bytes 3538952 | tf_op jit(solution)/shard_map/ppermute | solution.py:19
  53.7 10.7 %collective-permute-start.6 = (bf16[1032,256]{1,0:T(8,128)(2,1)S(1)}, bf16[1032,256]{1,0:T(8,128)(2,1)S(1)}, u32[]{:S(2)}, u32[]{:S(2)}) collective-permute-start(bf16[1032,256]{1,0:T(8,128)(2,1)S(1)} %collective-permute-done.5.refs_6_), channel_id=1, source_target_pairs={{0,14},{2,0},{4,2},{6,4},{8,6},{10,8},{12,10},{14,12},{1,15},{3,1}... | collective-permute-start | bytes 1585160 | tf_op jit(solution)/shard_map/ppermute | solution.py:51
  65.2 1.9 collective-permute-start.4
  67.1 8.6 %collective-permute-done.6.refs_5_ = bf16[1032,256]{1,0:T(8,128)(2,1)S(1)} collective-permute-done((bf16[1032,256]{1,0:T(8,128)(2,1)S(1)}, bf16[1032,256]{1,0:T(8,128)(2,1)S(1)}, u32[]{:S(2)}, u32[]{:S(2)}) %collective-permute-start.6) | collective-permute-done | bytes 528416 | tf_op jit(solution)/shard_map/ppermute | solution.py:51
  75.8 5.3 %collective-permute-start.7 = (bf16[1032,256]{1,0:T(8,128)(2,1)S(1)}, bf16[1032,256]{1,0:T(8,128)(2,1)S(1)}, u32[]{:S(2)}, u32[]{:S(2)}) collective-permute-start(bf16[1032,256]{1,0:T(8,128)(2,1)S(1)} %collective-permute-done.6.refs_5_), channel_id=1, source_target_pairs={{0,14},{2,0},{4,2},{6,4},{8,6},{10,8},{12,10},{14,12},{1,15},{3,1}... | collective-permute-start | bytes 1585160 | tf_op jit(solution)/shard_map/ppermute | solution.py:51
  81.8 1.9 collective-permute-start.8
  83.8 7.8 %collective-permute-done.7.refs_4_ = bf16[1032,256]{1,0:T(8,128)(2,1)S(1)} collective-permute-done((bf16[1032,256]{1,0:T(8,128)(2,1)S(1)}, bf16[1032,256]{1,0:T(8,128)(2,1)S(1)}, u32[]{:S(2)}, u32[]{:S(2)}) %collective-permute-start.7) | collective-permute-done | bytes 528416 | tf_op jit(solution)/shard_map/ppermute | solution.py:51
  92.6 1.9 shard_map.98.early_mine
  94.5 2.3 %shard_map.99.early_theirs = f32[128,688]{1,0:T(8,128)S(1)} custom-call(bf16[16,2,8,2304]{3,2,1,0:T(8,128)(2,1)S(1)} %collective-permute-done.1.rows.theirs, bf16[1032,256]{1,0:T(8,128)(2,1)S(1)} %pad_maximum_fusion.refs_0_, bf16[1032,256]{1,0:T(8,128)(2,1)S(1)} %collective-permute-done.2.refs_1_, bf16[1032,256]{1,0:T(8,128)(2,1)} %collective-permute-done.3.refs_2_, ...), custom_call_target="tpu_custom_call" | custom-call | flops 315621376 | bytes 3670016 | tf_op jit(solution)/shard_map/pallas_call | solution.py:92
  97.2 1.9 collective-permute-start.9
  99.1 5.3 %collective-permute-start.11 = (bf16[344,256]{1,0:T(8,128)(2,1)S(1)}, bf16[344,256]{1,0:T(8,128)(2,1)S(1)}, u32[]{:S(2)}, u32[]{:S(2)}) collective-permute-start(bf16[344,256]{1,0:T(8,128)(2,1)S(1)} %slice.72), channel_id=1, source_target_pairs={{0,14},{2,0},{4,2},{6,4},{8,6},{10,8},{12,10},{14,12},{1,15},{3,1}... | collective-permute-start | bytes 528392 | tf_op jit(solution)/shard_map/ppermute | solution.py:51
  106.3 1.9 shard_map.96.early_theirs
  108.9 3.4 %collective-permute-start.10 = (bf16[256,344]{1,0:T(8,128)(2,1)S(1)}, bf16[256,344]{1,0:T(8,128)(2,1)S(1)}, u32[]{:S(2)}, u32[]{:S(2)}) collective-permute-start(bf16[256,344]{1,0:T(8,128)(2,1)S(1)} %fusion.own), channel_id=1, source_target_pairs={{0,1},{1,0},{2,3},{3,2},{4,5},{5,4},{6,7},{7,6},{8,9},{9,8},{10,11... | collective-permute-start | bytes 528392 | tf_op jit(solution)/shard_map/ppermute | solution.py:19
  112.3 3.0 %collective-permute-done.10.other = bf16[256,344]{1,0:T(8,128)(2,1)S(1)} collective-permute-done((bf16[256,344]{1,0:T(8,128)(2,1)S(1)}, bf16[256,344]{1,0:T(8,128)(2,1)S(1)}, u32[]{:S(2)}, u32[]{:S(2)}) %collective-permute-start.10) | collective-permute-done | bytes 176160 | tf_op jit(solution)/shard_map/ppermute | solution.py:19
  115.3 2.8 %shard_map.102 = bf16[4,8,64,256]{3,2,1,0:T(8,128)(2,1)} custom-call(bf16[256,344]{1,0:T(8,128)(2,1)S(1)} %fusion.own, bf16[256,344]{1,0:T(8,128)(2,1)S(1)} %collective-permute-done.10.other, bf16[344,256]{1,0:T(8,128)(2,1)S(1)} %collective-permute-done.11.fourth, bf16[1032,256]{1,0:T(8,128)(2,1)S(1)} %pad_maximum_fusion.refs_0_, ...), custom_call_target="tpu_custom_call" | custom-call | flops 360710144 | bytes 3145728 | tf_op jit(solution)/shard_map/pallas_call | solution.py:130
  118.2 5.0 %collective-permute-start.12 = (bf16[4,8,64,256]{3,2,1,0:T(8,128)(2,1)}, bf16[4,8,64,256]{3,2,1,0:T(8,128)(2,1)}, u32[]{:S(2)}, u32[]{:S(2)}) collective-permute-start(bf16[4,8,64,256]{3,2,1,0:T(8,128)(2,1)} %shard_map.102), channel_id=1, source_target_pairs={{0,16},{16,0},{1,17},{17,1},{2,18},{18,2},{3,19},{19,3},{4,20},{20... | collective-permute-start | bytes 3145736 | tf_op jit(solution)/shard_map/ppermute | solution.py:19
  129.1 2.6 %add_convert_fusion = bf16[4,8,64,256]{3,2,1,0:T(8,128)(2,1)} fusion(f32[4,8,64,256]{3,2,1,0:T(8,128)S(1)} %shard_map.101, bf16[4,8,64,256]{3,2,1,0:T(8,128)(2,1)} %collective-permute-done.12), kind=kLoop, calls=%fused_computation.2 | loop fusion | flops 1572864 | bytes 4194304 | tf_op jit(solution)/shard_map/convert_element_type | solution.py:172
  131.7 3.6 %all-to-all-start.1 = ((bf16[4,8,64,256]{3,2,1,0:T(8,128)(2,1)}), bf16[4,8,64,256]{3,2,1,0:T(8,128)(2,1)S(1)}, u32[]{:S(2)}, u32[]{:S(2)}) async-start(bf16[4,8,64,256]{3,2,1,0:T(8,128)(2,1)} %add_convert_fusion), calls=%async_computation.1 | async-start | bytes 2097152 | tf_op jit(solution)/shard_map/all_to_all | solution.py:183
  136.7 3.6 %collective-permute-start.13 = (bf16[8,2048]{1,0:T(8,128)(2,1)S(1)}, bf16[8,2048]{1,0:T(8,128)(2,1)S(1)}, u32[]{:S(2)}, u32[]{:S(2)}) collective-permute-start(bf16[8,2048]{1,0:T(8,128)(2,1)S(1)} %convolution_convert_fusion), channel_id=1, source_target_pairs={{0,1},{1,0},{2,3},{3,2},{4,5},{5,4},{6,7},{7,6},{8,9},{9,8},{10,11... | collective-permute-start | bytes 98312 | tf_op jit(solution)/shard_map/ppermute | solution.py:19
  140.5 10.0 %all-to-all-done.1 = bf16[4,8,64,256]{3,2,1,0:T(8,128)(2,1)S(1)} async-done(((bf16[4,8,64,256]{3,2,1,0:T(8,128)(2,1)}), bf16[4,8,64,256]{3,2,1,0:T(8,128)(2,1)S(1)}, u32[]{:S(2)}, u32[]{:S(2)}) %all-to-all-start.1) | async-done | bytes 1048608 | tf_op jit(solution)/shard_map/all_to_all | solution.py:183
  151.5 3.6 %all-to-all-start.2 = ((bf16[8,8,8,256]{3,2,1,0:T(8,128)(2,1)}), bf16[8,8,8,256]{3,2,1,0:T(8,128)(2,1)S(1)}, u32[]{:S(2)}, u32[]{:S(2)}) async-start(bf16[8,8,8,256]{3,2,1,0:T(8,128)(2,1)} %bitcast.12), calls=%async_computation.2 | async-start | bytes 524288 | tf_op jit(solution)/shard_map/all_to_all | solution.py:187
  155.1 10.3 %all-to-all-done.2 = bf16[8,8,8,256]{3,2,1,0:T(8,128)(2,1)S(1)} async-done(((bf16[8,8,8,256]{3,2,1,0:T(8,128)(2,1)}), bf16[8,8,8,256]{3,2,1,0:T(8,128)(2,1)S(1)}, u32[]{:S(2)}, u32[]{:S(2)}) %all-to-all-start.2) | async-done | bytes 262176 | tf_op jit(solution)/shard_map/all_to_all | solution.py:187
  166.7 12.1 %all_to_all.30 = bf16[8,8,640]{2,1,0:T(8,128)(2,1)S(1)} all-to-all(bf16[8,8,640]{2,1,0:T(8,128)(2,1)S(1)} %pad_maximum_fusion.2), channel_id=1, replica_groups=mesh['yh'=4,'x'=4,'c'=2,'z'=8,'yl'=2] {'z'}, dimensions={0} | all-to-all | bytes 163840 | tf_op jit(solution)/shard_map/all_to_all | solution.py:199
  179.4 16.5 %all_to_all.31 = bf16[32,2,640]{2,1,0:T(2,128)(2,1)S(1)} all-to-all(bf16[32,2,640]{2,1,0:T(2,128)(2,1)S(1)} %reshape.110), channel_id=1, replica_groups=mesh['yh'=4,'x'=4,'c'=2,'z'=8,'yl'=2] {'yh','x','c'}, dimensions={0} | all-to-all | bytes 163840 | tf_op jit(solution)/shard_map/all_to_all | solution.py:204
  196.0 10.3 %all_to_all.32 = f32[16,2,640]{2,1,0:T(2,128)S(1)} all-to-all(f32[16,2,640]{2,1,0:T(2,128)S(1)} %broadcast_in_dim.16), channel_id=1, replica_groups=mesh['yh'=4,'x'=4,'c'=2,'z'=8,'yl'=2] {'z','yl'}, dimensions={0} | all-to-all | bytes 163840 | tf_op jit(solution)/shard_map/all_to_all | solution.py:24
  (116 shorter events, 20.7 us)
Async XLA Ops:
  2.3 5.3 %collective-permute-start = (bf16[8,2176]{1,0:T(8,128)(2,1)S(1)}, bf16[8,2176]{1,0:T(8,128)(2,1)S(1)}, u32[]{:S(2)}, u32[]{:S(2)}) collective-permute-start(bf16[8,2176]{1,0:T(8,128)(2,1)S(1)} %pad_maximum_fusion.5), channel_id=1, source_target_pairs={{0,1},{1,0},{2,3},{3,2},{4,5},{5,4},{6,7},{7,6},{8,9},{9,8},{10,11... | collective-permute-start | bytes 104456 | tf_op jit(solution)/shard_map/ppermute | solution.py:19
  8.7 9.7 %copy-start.12 = (bf16[344,256]{1,0:T(8,128)(2,1)S(1)}, bf16[344,256]{1,0:T(8,128)(2,1)}, u32[]{:S(2)}) copy-start(bf16[344,256]{1,0:T(8,128)(2,1)} %param.12) | copy-start | bytes 528388
  8.7 9.7 %copy-start.13 = (bf16[256,344]{0,1:T(8,128)(2,1)S(1)}, bf16[256,344]{0,1:T(8,128)(2,1)}, u32[]{:S(2)}) copy-start(bf16[256,344]{0,1:T(8,128)(2,1)} %param.11) | copy-start | bytes 528388
  8.7 9.7 %copy-start.14 = (bf16[256,344]{0,1:T(8,128)(2,1)S(1)}, bf16[256,344]{0,1:T(8,128)(2,1)}, u32[]{:S(2)}) copy-start(bf16[256,344]{0,1:T(8,128)(2,1)} %param.10) | copy-start | bytes 528388
  8.7 38.8 %all-to-all-start = ((bf16[16,2,8,2304]{3,2,1,0:T(8,128)(2,1)}), bf16[16,2,8,2304]{3,2,1,0:T(8,128)(2,1)S(1)}, u32[]{:S(2)}, u32[]{:S(2)}) async-start(bf16[16,2,8,2304]{3,2,1,0:T(8,128)(2,1)} %broadcast_in_dim.14), calls=%async_computation | async-start | bytes 2359296 | tf_op jit(solution)/shard_map/all_to_all | solution.py:24
  18.5 20.9 %collective-permute-start.2 = (bf16[1032,256]{1,0:T(8,128)(2,1)S(1)}, bf16[1032,256]{1,0:T(8,128)(2,1)S(1)}, u32[]{:S(2)}, u32[]{:S(2)}) collective-permute-start(bf16[1032,256]{1,0:T(8,128)(2,1)S(1)} %pad_maximum_fusion.refs_0_), channel_id=1, source_target_pairs={{0,2},{2,4},{4,6},{6,8},{8,10},{10,12},{12,14},{14,0},{1,3},{3,5},... | collective-permute-start | bytes 1585160 | tf_op jit(solution)/shard_map/ppermute | solution.py:51
  22.5 31.2 %collective-permute-start.5 = (bf16[1032,256]{1,0:T(8,128)(2,1)S(1)}, bf16[1032,256]{1,0:T(8,128)(2,1)S(1)}, u32[]{:S(2)}, u32[]{:S(2)}) collective-permute-start(bf16[1032,256]{1,0:T(8,128)(2,1)S(1)} %pad_maximum_fusion.refs_0_), channel_id=1, source_target_pairs={{0,14},{2,0},{4,2},{6,4},{8,6},{10,8},{12,10},{14,12},{1,15},{3,1}... | collective-permute-start | bytes 1585160 | tf_op jit(solution)/shard_map/ppermute | solution.py:51
  39.4 25.8 %collective-permute-start.3 = (bf16[1032,256]{1,0:T(8,128)(2,1)S(1)}, bf16[1032,256]{1,0:T(8,128)(2,1)}, u32[]{:S(2)}, u32[]{:S(2)}) collective-permute-start(bf16[1032,256]{1,0:T(8,128)(2,1)S(1)} %collective-permute-done.2.refs_1_), channel_id=1, source_target_pairs={{0,2},{2,4},{4,6},{6,8},{8,10},{10,12},{12,14},{14,0},{1,3},{3,5},... | collective-permute-start | bytes 1585160 | tf_op jit(solution)/shard_map/ppermute | solution.py:51
  47.6 46.9 %collective-permute-start.1 = (bf16[16,2,8,2304]{3,2,1,0:T(8,128)(2,1)S(1)}, bf16[16,2,8,2304]{3,2,1,0:T(8,128)(2,1)S(1)}, u32[]{:S(2)}, u32[]{:S(2)}) collective-permute-start(bf16[16,2,8,2304]{3,2,1,0:T(8,128)(2,1)S(1)} %all-to-all-done.rows.mine), channel_id=1, source_target_pairs={{0,16},{16,0},{1,17},{17,1},{2,18},{18,2},{3,19},{19,3},{4,20},{20... | collective-permute-start | bytes 3538952 | tf_op jit(solution)/shard_map/ppermute | solution.py:19
  53.7 22.0 %collective-permute-start.6 = (bf16[1032,256]{1,0:T(8,128)(2,1)S(1)}, bf16[1032,256]{1,0:T(8,128)(2,1)S(1)}, u32[]{:S(2)}, u32[]{:S(2)}) collective-permute-start(bf16[1032,256]{1,0:T(8,128)(2,1)S(1)} %collective-permute-done.5.refs_6_), channel_id=1, source_target_pairs={{0,14},{2,0},{4,2},{6,4},{8,6},{10,8},{12,10},{14,12},{1,15},{3,1}... | collective-permute-start | bytes 1585160 | tf_op jit(solution)/shard_map/ppermute | solution.py:51
  65.2 16.6 %collective-permute-start.4 = (bf16[1032,256]{1,0:T(8,128)(2,1)}, bf16[1032,256]{1,0:T(8,128)(2,1)S(1)}, u32[]{:S(2)}, u32[]{:S(2)}) collective-permute-start(bf16[1032,256]{1,0:T(8,128)(2,1)} %collective-permute-done.3.refs_2_), channel_id=1, source_target_pairs={{0,2},{2,4},{4,6},{6,8},{8,10},{10,12},{12,14},{14,0},{1,3},{3,5},... | collective-permute-start | bytes 1585160 | tf_op jit(solution)/shard_map/ppermute | solution.py:51
  75.8 39.6 %copy-start.5 = (bf16[1032,256]{1,0:T(8,128)(2,1)}, bf16[1032,256]{1,0:T(8,128)(2,1)S(1)}, u32[]{:S(2)}) copy-start(bf16[1032,256]{1,0:T(8,128)(2,1)S(1)} %collective-permute-done.6.refs_5_) | copy-start | bytes 1585156
  75.8 15.8 %collective-permute-start.7 = (bf16[1032,256]{1,0:T(8,128)(2,1)S(1)}, bf16[1032,256]{1,0:T(8,128)(2,1)S(1)}, u32[]{:S(2)}, u32[]{:S(2)}) collective-permute-start(bf16[1032,256]{1,0:T(8,128)(2,1)S(1)} %collective-permute-done.6.refs_5_), channel_id=1, source_target_pairs={{0,14},{2,0},{4,2},{6,4},{8,6},{10,8},{12,10},{14,12},{1,15},{3,1}... | collective-permute-start | bytes 1585160 | tf_op jit(solution)/shard_map/ppermute | solution.py:51
  81.8 15.0 %collective-permute-start.8 = (bf16[688,256]{1,0:T(8,128)(2,1)S(1)}, bf16[688,256]{1,0:T(8,128)(2,1)S(1)}, u32[]{:S(2)}, u32[]{:S(2)}) collective-permute-start(bf16[688,256]{1,0:T(8,128)(2,1)S(1)} %slice.69), channel_id=1, source_target_pairs={{0,2},{2,4},{4,6},{6,8},{8,10},{10,12},{12,14},{14,0},{1,3},{3,5},... | collective-permute-start | bytes 1056776 | tf_op jit(solution)/shard_map/ppermute | solution.py:51
  91.5 1.0 copy-start.2
  94.5 13.7 %copy-start = (bf16[16,2,8,2304]{3,2,1,0:T(8,128)(2,1)}, bf16[16,2,8,2304]{3,2,1,0:T(8,128)(2,1)S(1)}, u32[]{:S(2)}) copy-start(bf16[16,2,8,2304]{3,2,1,0:T(8,128)(2,1)S(1)} %collective-permute-done.1.rows.theirs) | copy-start | bytes 3538948
  97.2 11.5 %collective-permute-start.9 = (bf16[256,688]{1,0:T(8,128)(2,1)S(1)}, bf16[256,688]{1,0:T(8,128)(2,1)S(1)}, u32[]{:S(2)}, u32[]{:S(2)}) collective-permute-start(bf16[256,688]{1,0:T(8,128)(2,1)S(1)} %shard_map.100), channel_id=1, source_target_pairs={{0,1},{1,0},{2,3},{3,2},{4,5},{5,4},{6,7},{7,6},{8,9},{9,8},{10,11... | collective-permute-start | bytes 1056776 | tf_op jit(solution)/shard_map/ppermute | solution.py:19
  99.1 13.2 %collective-permute-start.11 = (bf16[344,256]{1,0:T(8,128)(2,1)S(1)}, bf16[344,256]{1,0:T(8,128)(2,1)S(1)}, u32[]{:S(2)}, u32[]{:S(2)}) collective-permute-start(bf16[344,256]{1,0:T(8,128)(2,1)S(1)} %slice.72), channel_id=1, source_target_pairs={{0,14},{2,0},{4,2},{6,4},{8,6},{10,8},{12,10},{14,12},{1,15},{3,1}... | collective-permute-start | bytes 528392 | tf_op jit(solution)/shard_map/ppermute | solution.py:51
  108.6 6.7 %copy-start.3 = (bf16[1032,256]{1,0:T(8,128)(2,1)S(1)}, bf16[1032,256]{1,0:T(8,128)(2,1)}, u32[]{:S(2)}) copy-start(bf16[1032,256]{1,0:T(8,128)(2,1)} %copy-done.1) | copy-start | bytes 1585156
  108.9 14.3 %copy-start.17 = (s32[8]{0:T(128)S(1)}, s32[8]{0:T(128)}, u32[]{:S(2)}) copy-start(s32[8]{0:T(128)} %param.15) | copy-start | bytes 100
  108.9 6.4 %collective-permute-start.10 = (bf16[256,344]{1,0:T(8,128)(2,1)S(1)}, bf16[256,344]{1,0:T(8,128)(2,1)S(1)}, u32[]{:S(2)}, u32[]{:S(2)}) collective-permute-start(bf16[256,344]{1,0:T(8,128)(2,1)S(1)} %fusion.own), channel_id=1, source_target_pairs={{0,1},{1,0},{2,3},{3,2},{4,5},{5,4},{6,7},{7,6},{8,9},{9,8},{10,11... | collective-permute-start | bytes 528392 | tf_op jit(solution)/shard_map/ppermute | solution.py:19
  112.3 5.9 %copy-start.9 = (bf16[344,256]{1,0:T(8,128)(2,1)}, bf16[344,256]{1,0:T(8,128)(2,1)S(1)}, u32[]{:S(2)}) copy-start(bf16[344,256]{1,0:T(8,128)(2,1)S(1)} %collective-permute-done.11.fourth) | copy-start | bytes 528388
  115.3 2.8 %copy-start.7 = (bf16[256,344]{1,0:T(8,128)(2,1)}, bf16[256,344]{1,0:T(8,128)(2,1)S(1)}, u32[]{:S(2)}) copy-start(bf16[256,344]{1,0:T(8,128)(2,1)S(1)} %collective-permute-done.10.other) | copy-start | bytes 528388
  118.2 10.9 %collective-permute-start.12 = (bf16[4,8,64,256]{3,2,1,0:T(8,128)(2,1)}, bf16[4,8,64,256]{3,2,1,0:T(8,128)(2,1)}, u32[]{:S(2)}, u32[]{:S(2)}) collective-permute-start(bf16[4,8,64,256]{3,2,1,0:T(8,128)(2,1)} %shard_map.102), channel_id=1, source_target_pairs={{0,16},{16,0},{1,17},{17,1},{2,18},{18,2},{3,19},{19,3},{4,20},{20... | collective-permute-start | bytes 3145736 | tf_op jit(solution)/shard_map/ppermute | solution.py:19
  123.4 1.0 copy-start.4
  131.7 3.7 %slice-start = ((bf16[16,2,8,2304]{3,2,1,0:T(8,128)(2,1)}), bf16[16,2,8,256]{3,2,1,0:T(8,128)(2,1)S(1)}, s32[]{:S(2)}) async-start(bf16[16,2,8,2304]{3,2,1,0:T(8,128)(2,1)} %copy-done), calls=%async_computation.6 | async-start | bytes 262144 | tf_op jit(solution)/shard_map/slice | solution.py:176
  131.7 18.8 %all-to-all-start.1 = ((bf16[4,8,64,256]{3,2,1,0:T(8,128)(2,1)}), bf16[4,8,64,256]{3,2,1,0:T(8,128)(2,1)S(1)}, u32[]{:S(2)}, u32[]{:S(2)}) async-start(bf16[4,8,64,256]{3,2,1,0:T(8,128)(2,1)} %add_convert_fusion), calls=%async_computation.1 | async-start | bytes 2097152 | tf_op jit(solution)/shard_map/all_to_all | solution.py:183
  136.7 18.4 %collective-permute-start.13 = (bf16[8,2048]{1,0:T(8,128)(2,1)S(1)}, bf16[8,2048]{1,0:T(8,128)(2,1)S(1)}, u32[]{:S(2)}, u32[]{:S(2)}) collective-permute-start(bf16[8,2048]{1,0:T(8,128)(2,1)S(1)} %convolution_convert_fusion), channel_id=1, source_target_pairs={{0,1},{1,0},{2,3},{3,2},{4,5},{5,4},{6,7},{7,6},{8,9},{9,8},{10,11... | collective-permute-start | bytes 98312 | tf_op jit(solution)/shard_map/ppermute | solution.py:19
  151.5 14.2 %copy-start.11 = (bf16[8,4096]{1,0:T(8,128)(2,1)S(1)}, bf16[8,4096]{1,0:T(8,128)(2,1)}, u32[]{:S(2)}) copy-start(bf16[8,4096]{1,0:T(8,128)(2,1)} %param.8) | copy-start | bytes 196612
  151.5 13.9 %all-to-all-start.2 = ((bf16[8,8,8,256]{3,2,1,0:T(8,128)(2,1)}), bf16[8,8,8,256]{3,2,1,0:T(8,128)(2,1)S(1)}, u32[]{:S(2)}, u32[]{:S(2)}) async-start(bf16[8,8,8,256]{3,2,1,0:T(8,128)(2,1)} %bitcast.12), calls=%async_computation.2 | async-start | bytes 524288 | tf_op jit(solution)/shard_map/all_to_all | solution.py:187
  155.0 10.8 %copy-start.16 = (f32[4096]{0:T(1024)S(1)}, f32[4096]{0:T(1024)}, u32[]{:S(2)}) copy-start(f32[4096]{0:T(1024)} %param.9) | copy-start | bytes 49156
  165.7 40.8 %copy-start.15 = (f32[2,4096]{1,0:T(2,128)S(1)}, f32[2,4096]{1,0:T(2,128)}, u32[]{:S(2)}) copy-start(f32[2,4096]{1,0:T(2,128)} %param.13) | copy-start | bytes 98308
  (4 other events, 3.7 us)
